TPU v7x, 128 devices: a whole 4x4x4 slice. The times are simulated.
128 devices in a mesh: row: 16 (over x_lo, z, core), col: 8 (over y, x_hi).
Axes of the slice: x: 4 (x_hi: 2, x_lo: 2; x = x_hi * 2 + x_lo), y: 4, z: 4, core: 2. Of those that a mesh axis runs over, the one named last changes fastest.
Arguments:
- die_current: float32 [16, 2048, 2048], P(None, 'row', 'col')
- die_shunt: float32 [2048, 2048], P('row', 'col'), may hold values from 0.01 to 0.1
- pkg_current: float32 [16, 4096], P(None, ('row', 'col')), may hold values from -6 to 6
- pkg_matrix: float32 [4096, 4096], P('row', 'col'), as said below
- pkg_block_inv: float32 [128, 32, 32], P(('row', 'col')), as said below
- bump_node: int32 [4096], replicated, may hold values from 0 to 4194303, as said below
- bump_conductance: float32 [4096], replicated, may hold values from 0.5 to 4
Outputs:
- die_drop: float32 [16, 2048, 2048], P(None, 'row', 'col')
- package_drop: float32 [16, 4096], P(None, ('row', 'col'))
Inputs may be any that keep to these rules, and one draw needn't show every extreme that they name: `bump_node`: bump b lies in lattice cell (b // 64, b % 64) of the die, the cells being 32 rows by 32 columns; the entry is row * 2048 + column, so no two bumps share a node. `pkg_matrix`: symmetric positive definite. `pkg_block_inv`: each block is symmetric positive definite.
All inputs are finite; a program needn't handle non-finite values.
Results may differ from a plain program's by a relative error of at most 0.0003.
Values sent between devices are 32-bit elements; how exact they have to be, the bound alone decides.
No kernel may reach another device: no remote copies, remote signals or barrier semaphores. Data moves between devices by JAX's collectives and lax.ppermute only.
A program may use at most 128 MiB of HBM per device.

v0:
```python
import jax
import jax.numpy as jnp
from jax import lax
from jax.sharding import Mesh
from jax.sharding import PartitionSpec as P

BUMP_C = 64
PB = 32
ITERS = 3
ROW = ("row_0", "row_1", "row_2")
COL = ("col_0", "col_1")
ROW_COL = ("row_0", "row_1", "row_2", "col_0", "col_1")


def with_halo(block, sides, width):
    for axis, dim in sides:
        count = lax.axis_size(axis)
        forward = [(i, i + 1) for i in range(count - 1)]
        backward = [(target, source) for source, target in forward]
        low = lax.ppermute(
            lax.slice_in_dim(block, block.shape[dim] - width, None, axis=dim), axis, forward
        )
        high = lax.ppermute(lax.slice_in_dim(block, 0, width, axis=dim), axis, backward)
        block = jnp.concatenate([low, block, high], axis=dim)
    return block


def joined_along(tiles, dim):
    lengths = list(tiles.shape[1:])
    lengths[dim] *= tiles.shape[0]
    return jnp.moveaxis(tiles, 0, dim).reshape(lengths)


def sent_to_all(shard, axis):
    copies = jnp.broadcast_to(shard, (lax.axis_size(axis), *shard.shape))
    return lax.all_to_all(copies, axis, split_axis=0, concat_axis=0, tiled=True)


def gathered_copies(shard, axis, dim):
    return joined_along(sent_to_all(shard, axis), dim)


def split_up(shard, dim, devices):
    before, after = (shard.shape[:dim], shard.shape[dim + 1 :])
    return jnp.moveaxis(shard.reshape(*before, devices, -1, *after), dim, 0)


def summed_on_arrival(shard, axis, dim):
    devices = lax.axis_size(axis)
    tiles = lax.all_to_all(split_up(shard, dim, devices), axis, 0, 0, tiled=True)
    return jnp.sum(tiles, axis=0)


def over_axes(shard, axes):
    for axis in axes:
        shard = lax.psum(shard, axis)
    return shard


def inner(ad, ap, bd, bp):
    return jnp.sum(ad * bd, axis=(1, 2)) + jnp.sum(ap * bp, axis=1)


def body(
    die_current, die_shunt, pkg_current, pkg_matrix, pkg_block_inv, bump_node, bump_conductance
):
    nrows = lax.axis_size(ROW)
    ncols = lax.axis_size(COL)
    irow = lax.axis_index(ROW)
    icol = lax.axis_index(COL)
    batch, tile_r, tile_c = die_current.shape
    total_c = tile_c * ncols
    bumps = bump_node.shape[0]
    local_n = pkg_current.shape[1]
    start = (irow * ncols + icol) * local_n
    lat_rows = bumps // BUMP_C // nrows
    lat_cols = BUMP_C // ncols
    seg_len = bumps // nrows
    cond_here = lax.dynamic_slice_in_dim(bump_conductance, start, local_n)
    step_r = jnp.arange(lat_rows, dtype=jnp.int32)
    step_c = jnp.arange(lat_cols, dtype=jnp.int32)
    chosen = (
        (irow * lat_rows + step_r[:, None]) * BUMP_C + icol * lat_cols + step_c[None, :]
    ).reshape(-1)
    mine = start + jnp.arange(local_n, dtype=jnp.int32)
    lat_r = mine // BUMP_C
    lat_c = mine % BUMP_C
    tile_bumps = lat_rows * lat_cols
    source = lat_c // lat_cols * tile_bumps + lat_r % lat_rows * lat_cols + lat_c % lat_cols
    nodes = bump_node[chosen]
    loc_r = nodes // total_c - irow * tile_r
    loc_c = nodes % total_c - icol * tile_c
    inside = (loc_r >= 0) & (loc_r < tile_r) & (loc_c >= 0) & (loc_c < tile_c)
    weight = inside.astype(jnp.float32)
    loc_r = jnp.clip(loc_r, 0, tile_r - 1)
    loc_c = jnp.clip(loc_c, 0, tile_c - 1)
    cond_sel = bump_conductance[chosen] * weight
    seg_index = jnp.clip(chosen - irow * seg_len, 0, seg_len - 1)
    diag_die = (4.0 + die_shunt).at[loc_r, loc_c].add(cond_sel)

    def apply_op(vd, vp):
        padded = with_halo(vd, ((ROW, 1), (COL, 2)), 1)
        beside_all = padded[:, 2:, 1:-1] + padded[:, :-2, 1:-1]
        beside_all = beside_all + padded[:, 1:-1, 2:] + padded[:, 1:-1, :-2]
        die = (4.0 + die_shunt) * vd - beside_all
        segment = gathered_copies(vp, COL, 1)
        partial_value = jnp.dot(segment, pkg_matrix, precision=lax.Precision.HIGHEST)
        pieces = partial_value.reshape(batch, nrows // ncols, ncols, local_n).transpose(0, 2, 1, 3)
        moved = lax.all_to_all(pieces, COL, split_axis=1, concat_axis=1, tiled=True)
        pkg_term = summed_on_arrival(moved.reshape(batch, nrows * local_n), ROW, 1)
        pkg_at = jnp.take(segment, seg_index, axis=1)
        at_bumps = vd[:, loc_r, loc_c] * weight
        gathered = gathered_copies(at_bumps, COL, 1)
        die_at = jnp.take(gathered, source, axis=1)
        die = die.at[:, loc_r, loc_c].add(cond_sel * (at_bumps - pkg_at))
        return (die, pkg_term + cond_here * (vp - die_at))

    def precond(rd, rp):
        blocks = rp.reshape(batch, -1, PB)
        zp = jnp.einsum("bac,kbc->kba", pkg_block_inv, blocks, precision=lax.Precision.HIGHEST)
        return (rd / diag_die, zp.reshape(batch, local_n))

    xd = jnp.zeros_like(die_current)
    xp = jnp.zeros_like(pkg_current)
    rd, rp = (die_current, pkg_current)

    def both_sums(rd, rp, zd, zp, wd, wp):
        return (
            over_axes(inner(rd, rp, zd, zp), ROW_COL),
            over_axes(inner(wd, wp, zd, zp), ROW_COL),
        )

    zd, zp = precond(rd, rp)
    wd, wp = apply_op(zd, zp)
    gamma, delta = both_sums(rd, rp, zd, zp, wd, wp)
    alpha = gamma / delta
    pd, pp, sd, sp = (zd, zp, wd, wp)
    for step in range(ITERS):
        xd = xd + alpha[:, None, None] * pd
        xp = xp + alpha[:, None] * pp
        rd = rd - alpha[:, None, None] * sd
        rp = rp - alpha[:, None] * sp
        if step + 1 < ITERS:
            zd, zp = precond(rd, rp)
            wd, wp = apply_op(zd, zp)
            fresh, delta = both_sums(rd, rp, zd, zp, wd, wp)
            ratio = fresh / gamma
            alpha = fresh / (delta - ratio * fresh / alpha)
            pd = zd + ratio[:, None, None] * pd
            pp = zp + ratio[:, None] * pp
            sd = wd + ratio[:, None, None] * sd
            sp = wp + ratio[:, None] * sp
            gamma = fresh
    return (xd, xp)


def solution(mesh):
    torus = Mesh(mesh.devices.reshape(2, 4, 2, 4, 2), ("row_0", "row_1", "row_2", "col_0", "col_1"))
    placed = (
        P(None, ROW, COL),
        P(ROW, COL),
        P(None, ROW_COL),
        P(ROW, COL),
        P(ROW_COL, None, None),
        P(),
        P(),
    )
    return jax.shard_map(
        body,
        mesh=torus,
        in_specs=placed,
        out_specs=(P(None, ROW, COL), P(None, ROW_COL)),
        check_vma=False,
    )
```

profile of v0, /device:TPU:1, one launch (start us, length us, event | category | flops | bytes accessed | tf_op | source)
XLA Modules:
  0.0 442.8 jit_solution(6681626139399830000)
XLA Ops:
  17.1 6.7 %all-to-all-start = ((f32[8,1,512]{2,1,0:T(1,128)}), f32[8,1,512]{2,1,0:T(1,128)S(1)}, u32[]{:S(2)}, u32[]{:S(2)}) async-start(f32[8,1,512]{2,1,0:T(1,128)} %reshape.390), calls=%async_computation | async-start | bytes 32768 | tf_op jit(solution)/shard_map/all_to_all | solution.py:36
  24.4 10.1 %copy.290 = f32[16,128,256]{0,2,1:T(8,128)} copy(f32[16,128,256]{2,1,0:T(8,128)} %copy-done.2) | data formatting | bytes 4194304 | tf_op jit(solution)/shard_map/div | solution.py:121
  40.7 6.7 %all-to-all-start.1 = ((f32[8,1,1024]{2,1,0:T(1,128)}), f32[8,1,1024]{2,1,0:T(1,128)S(1)}, u32[]{:S(2)}, u32[]{:S(2)}) async-start(f32[8,1,1024]{2,1,0:T(1,128)} %reshape.392), calls=%async_computation.1 | async-start | bytes 65536 | tf_op jit(solution)/shard_map/all_to_all | solution.py:109
  56.6 5.5 %collective-permute-start.3 = (f32[16,130,1]{1,0,2:T(8,128)S(1)}, f32[16,130,1]{1,0,2:T(8,128)S(1)}, u32[]{:S(2)}, u32[]{:S(2)}) collective-permute-start(f32[16,130,1]{1,0,2:T(8,128)S(1)} %copy.288), channel_id=1, source_target_pairs={{0,1},{1,2},{2,3},{3,4},{4,5},{5,6},{6,7},{8,9},{9,10},{10,11},{11... | collective-permute-start | bytes 24968 | tf_op jit(solution)/shard_map/ppermute | solution.py:20
  65.9 7.5 %all-to-all-start.3 = ((f32[8,1,512]{2,1,0:T(1,128)}), f32[8,1,512]{2,1,0:T(1,128)S(1)}, u32[]{:S(2)}, u32[]{:S(2)}) async-start(f32[8,1,512]{2,1,0:T(1,128)} %reshape.396), calls=%async_computation.3 | async-start | bytes 32768 | tf_op jit(solution)/shard_map/all_to_all | solution.py:36
  73.4 8.7 %fusion.9 = f32[16,128,256]{2,1,0:T(8,128)} fusion(f32[16,130,1]{2,1,0:T(8,128)} %copy.289, f32[16,1,256]{2,1,0:T(1,128)S(1)} %collective-permute-done, f32[16,128,256]{2,1,0:T(8,128)} %copy-done.2, f32[16,1,256]{2,1,0:T(1,128)S(1)} %collective-permute-done.1, f32[16,130,1]{2,1,0:T(8,128)} %copy.287, f32[128,256]{1,0:T(8,128)S(1)} %broadcast_add_fusion), kind=kLoop, calls=%fused_computation.44 | loop fusion | flops 6815744 | bytes 4374784 | tf_op jit(solution)/shard_map/sub | solution.py:105
  82.1 10.0 %copy.292 = f32[16,128,256]{0,2,1:T(8,128)} copy(f32[16,128,256]{2,1,0:T(8,128)} %fusion.9) | data formatting | bytes 4194304 | tf_op jit(solution)/shard_map/sub | solution.py:105
  92.1 3.8 scatter_fusion.1
  95.9 11.0 %copy.293 = f32[16,128,256]{2,1,0:T(8,128)} copy(f32[16,128,256]{0,2,1:T(8,128)} %scatter_fusion.1) | data formatting | bytes 4194304 | tf_op jit(solution)/shard_map/scatter-add | solution.py:115
  108.4 7.1 %all-to-all-start.2 = ((f32[16,1,512]{2,1,0:T(1,128)}), f32[16,1,512]{2,1,0:T(1,128)S(1)}, u32[]{:S(2)}, u32[]{:S(2)}) async-start(f32[16,1,512]{2,1,0:T(1,128)} %reshape.394), calls=%async_computation.2 | async-start | bytes 65536 | tf_op jit(solution)/shard_map/all_to_all | solution.py:50
  122.3 3.8 all-reduce.14
  126.0 6.9 %all-reduce.5 = (f32[16]{0:T(128)S(1)}, f32[16]{0:T(128)S(1)}) all-reduce(f32[16]{0:T(128)S(1)} %get-tuple-element.53, f32[16]{0:T(128)S(1)} %get-tuple-element.54), channel_id=1, replica_groups=mesh['row_0'=2,'row_1'=4,'row_2'=2,'col_0'=4,'col_1'=2] {'row_1'}, use_global_device_ids=true, to_apply=%region_4.5 | all-reduce | flops 32 | bytes 256 | tf_op jit(solution)/shard_map/psum | solution.py:56
  133.0 5.7 %all-reduce.11 = (f32[16]{0:T(128)S(1)}, f32[16]{0:T(128)S(1)}) all-reduce(f32[16]{0:T(128)S(1)} %get-tuple-element.35, f32[16]{0:T(128)S(1)} %get-tuple-element.36), channel_id=1, replica_groups=mesh['row_0'=2,'row_1'=4,'row_2'=2,'col_0'=4,'col_1'=2] {'row_2'}, use_global_device_ids=true, to_apply=%region_5.6 | all-reduce | flops 32 | bytes 256 | tf_op jit(solution)/shard_map/psum | solution.py:56
  138.6 8.6 %all-reduce.2 = (f32[16]{0:T(128)S(1)}, f32[16]{0:T(128)S(1)}) all-reduce(f32[16]{0:T(128)S(1)} %get-tuple-element.47, f32[16]{0:T(128)S(1)} %get-tuple-element.48), channel_id=1, replica_groups=mesh['row_0'=2,'row_1'=4,'row_2'=2,'col_0'=4,'col_1'=2] {'col_0'}, use_global_device_ids=true, to_apply=%region_6.7 | all-reduce | flops 32 | bytes 256 | tf_op jit(solution)/shard_map/psum | solution.py:56
  147.3 5.3 %all-reduce.8 = (f32[16]{0:T(128)S(1)}, f32[16]{0:T(128)S(1)}) all-reduce(f32[16]{0:T(128)S(1)} %get-tuple-element.29, f32[16]{0:T(128)S(1)} %get-tuple-element.30), channel_id=1, replica_groups=mesh['row_0'=2,'row_1'=4,'row_2'=2,'col_0'=4,'col_1'=2] {'col_1'}, use_global_device_ids=true, to_apply=%region_7.8 | all-reduce | flops 32 | bytes 256 | tf_op jit(solution)/shard_map/psum | solution.py:56
  156.1 4.3 all-to-all-start.4
  160.5 8.6 %copy.304 = f32[16,128,256]{0,2,1:T(8,128)} copy(f32[16,128,256]{2,1,0:T(8,128)S(1)} %broadcast_divide_fusion.1) | data formatting | bytes 4194304 | tf_op jit(solution)/shard_map/div | solution.py:121
  170.4 5.7 %collective-permute-start.4 = (f32[16,1,256]{2,1,0:T(1,128)S(1)}, f32[16,1,256]{2,1,0:T(1,128)S(1)}, u32[]{:S(2)}, u32[]{:S(2)}) collective-permute-start(f32[16,1,256]{2,1,0:T(1,128)S(1)} %get-tuple-element.80), channel_id=1, source_target_pairs={{8,0},{16,8},{24,16},{32,24},{40,32},{48,40},{56,48},{64,56},{72,6... | collective-permute-start | bytes 49160 | tf_op jit(solution)/shard_map/ppermute | solution.py:23
  182.5 6.9 %all-to-all-start.5 = ((f32[8,1,1024]{2,1,0:T(1,128)}), f32[8,1,1024]{2,1,0:T(1,128)S(1)}, u32[]{:S(2)}, u32[]{:S(2)}) async-start(f32[8,1,1024]{2,1,0:T(1,128)} %reshape.400), calls=%async_computation.5 | async-start | bytes 65536 | tf_op jit(solution)/shard_map/all_to_all | solution.py:109
  196.4 5.5 %collective-permute-start.7 = (f32[16,130,1]{1,0,2:T(8,128)S(1)}, f32[16,130,1]{1,0,2:T(8,128)S(1)}, u32[]{:S(2)}, u32[]{:S(2)}) collective-permute-start(f32[16,130,1]{1,0,2:T(8,128)S(1)} %copy.302), channel_id=1, source_target_pairs={{0,1},{1,2},{2,3},{3,4},{4,5},{5,6},{6,7},{8,9},{9,10},{10,11},{11... | collective-permute-start | bytes 24968 | tf_op jit(solution)/shard_map/ppermute | solution.py:20
  205.7 7.5 %all-to-all-start.7 = ((f32[8,1,512]{2,1,0:T(1,128)}), f32[8,1,512]{2,1,0:T(1,128)S(1)}, u32[]{:S(2)}, u32[]{:S(2)}) async-start(f32[8,1,512]{2,1,0:T(1,128)} %reshape.404), calls=%async_computation.7 | async-start | bytes 32768 | tf_op jit(solution)/shard_map/all_to_all | solution.py:36
  213.2 4.7 %fusion.5 = f32[16,128,256]{2,1,0:T(8,128)} fusion(f32[16,130,1]{2,1,0:T(8,128)} %copy.303, f32[16,1,256]{2,1,0:T(1,128)S(1)} %collective-permute-done.4, f32[16,128,256]{2,1,0:T(8,128)S(1)} %broadcast_divide_fusion.1, f32[16,1,256]{2,1,0:T(1,128)S(1)} %collective-permute-done.5, f32[16,130,1]{2,1,0:T(8,128)} %copy.301, f32[128,256]{1,0:T(8,128)S(1)} %broadcast_add_fusion), kind=kLoop, calls=%fused_computation.32 | loop fusion | flops 6815744 | bytes 4374784 | tf_op jit(solution)/shard_map/sub | solution.py:105
  218.0 10.0 %copy.306 = f32[16,128,256]{0,2,1:T(8,128)} copy(f32[16,128,256]{2,1,0:T(8,128)} %fusion.5) | data formatting | bytes 4194304 | tf_op jit(solution)/shard_map/sub | solution.py:105
  231.7 11.0 %copy.307 = f32[16,128,256]{2,1,0:T(8,128)} copy(f32[16,128,256]{0,2,1:T(8,128)} %scatter_fusion.2) | data formatting | bytes 4194304 | tf_op jit(solution)/shard_map/scatter-add | solution.py:115
  244.3 4.8 %all-to-all-start.6 = ((f32[16,1,512]{2,1,0:T(1,128)}), f32[16,1,512]{2,1,0:T(1,128)S(1)}, u32[]{:S(2)}, u32[]{:S(2)}) async-start(f32[16,1,512]{2,1,0:T(1,128)} %reshape.402), calls=%async_computation.6 | async-start | bytes 65536 | tf_op jit(solution)/shard_map/all_to_all | solution.py:50
  255.9 3.8 all-reduce.13
  259.7 7.8 %all-reduce.4 = (f32[16]{0:T(128)S(1)}, f32[16]{0:T(128)S(1)}) all-reduce(f32[16]{0:T(128)S(1)} %get-tuple-element.51, f32[16]{0:T(128)S(1)} %get-tuple-element.52), channel_id=1, replica_groups=mesh['row_0'=2,'row_1'=4,'row_2'=2,'col_0'=4,'col_1'=2] {'row_1'}, use_global_device_ids=true, to_apply=%region_20.22 | all-reduce | flops 32 | bytes 256 | tf_op jit(solution)/shard_map/psum | solution.py:56
  267.5 5.7 %all-reduce.10 = (f32[16]{0:T(128)S(1)}, f32[16]{0:T(128)S(1)}) all-reduce(f32[16]{0:T(128)S(1)} %get-tuple-element.33, f32[16]{0:T(128)S(1)} %get-tuple-element.34), channel_id=1, replica_groups=mesh['row_0'=2,'row_1'=4,'row_2'=2,'col_0'=4,'col_1'=2] {'row_2'}, use_global_device_ids=true, to_apply=%region_21.23 | all-reduce | flops 32 | bytes 256 | tf_op jit(solution)/shard_map/psum | solution.py:56
  273.2 8.9 %all-reduce.1 = (f32[16]{0:T(128)S(1)}, f32[16]{0:T(128)S(1)}) all-reduce(f32[16]{0:T(128)S(1)} %get-tuple-element.45, f32[16]{0:T(128)S(1)} %get-tuple-element.46), channel_id=1, replica_groups=mesh['row_0'=2,'row_1'=4,'row_2'=2,'col_0'=4,'col_1'=2] {'col_0'}, use_global_device_ids=true, to_apply=%region_22.24 | all-reduce | flops 32 | bytes 256 | tf_op jit(solution)/shard_map/psum | solution.py:56
  282.1 5.3 %all-reduce.7 = (f32[16]{0:T(128)S(1)}, f32[16]{0:T(128)S(1)}) all-reduce(f32[16]{0:T(128)S(1)} %get-tuple-element.27, f32[16]{0:T(128)S(1)} %get-tuple-element.28), channel_id=1, replica_groups=mesh['row_0'=2,'row_1'=4,'row_2'=2,'col_0'=4,'col_1'=2] {'col_1'}, use_global_device_ids=true, to_apply=%region_23.25 | all-reduce | flops 32 | bytes 256 | tf_op jit(solution)/shard_map/psum | solution.py:56
  288.0 5.9 %broadcast_divide_fusion = (f32[16,128,256]{2,1,0:T(8,128)}, f32[16,128,256]{2,1,0:T(8,128)}) fusion(f32[128,256]{1,0:T(8,128)S(1)} %scatter_fusion, f32[16,128,256]{2,1,0:T(8,128)} %copy.307, f32[16,128,256]{2,1,0:T(8,128)} %copy.293, f32[16]{0:T(128)S(1)} %get-tuple-element.63, f32[16]{0:T(128)S(1)} %get-tuple-element.61, f32[16,128,256]{2,1,0:T(8,128)} %param.9, ...), kind=kLoop, calls=%fused_computation.66 | loop fusion | flops 3670016 | bytes 10617024 | tf_op jit(solution)/shard_map/div | solution.py:121
  294.8 4.3 all-to-all-start.8
  300.1 10.0 %copy.318 = f32[16,128,256]{0,2,1:T(8,128)} copy(f32[16,128,256]{2,1,0:T(8,128)} %get-tuple-element.59) | data formatting | bytes 4194304 | tf_op jit(solution)/shard_map/div | solution.py:121
  312.0 5.7 %collective-permute-start.8 = (f32[16,1,256]{2,1,0:T(1,128)S(1)}, f32[16,1,256]{2,1,0:T(1,128)S(1)}, u32[]{:S(2)}, u32[]{:S(2)}) collective-permute-start(f32[16,1,256]{2,1,0:T(1,128)S(1)} %get-tuple-element.78), channel_id=1, source_target_pairs={{8,0},{16,8},{24,16},{32,24},{40,32},{48,40},{56,48},{64,56},{72,6... | collective-permute-start | bytes 49160 | tf_op jit(solution)/shard_map/ppermute | solution.py:23
  324.5 6.9 %all-to-all-start.9 = ((f32[8,1,1024]{2,1,0:T(1,128)}), f32[8,1,1024]{2,1,0:T(1,128)S(1)}, u32[]{:S(2)}, u32[]{:S(2)}) async-start(f32[8,1,1024]{2,1,0:T(1,128)} %reshape.408), calls=%async_computation.9 | async-start | bytes 65536 | tf_op jit(solution)/shard_map/all_to_all | solution.py:109
  340.7 6.1 %collective-permute-start.11 = (f32[16,130,1]{1,0,2:T(8,128)}, f32[16,130,1]{1,0,2:T(8,128)}, u32[]{:S(2)}, u32[]{:S(2)}) collective-permute-start(f32[16,130,1]{1,0,2:T(8,128)} %copy.316), channel_id=1, source_target_pairs={{0,1},{1,2},{2,3},{3,4},{4,5},{5,6},{6,7},{8,9},{9,10},{10,11},{11... | collective-permute-start | bytes 24968 | tf_op jit(solution)/shard_map/ppermute | solution.py:20
  352.3 7.0 %all-to-all-start.11 = ((f32[8,1,512]{2,1,0:T(1,128)}), f32[8,1,512]{2,1,0:T(1,128)}, u32[]{:S(2)}, u32[]{:S(2)}) async-start(f32[8,1,512]{2,1,0:T(1,128)} %reshape.412), calls=%async_computation.11 | async-start | bytes 32768 | tf_op jit(solution)/shard_map/all_to_all | solution.py:36
  359.3 8.4 %fusion.1 = f32[16,128,256]{2,1,0:T(8,128)} fusion(f32[16,130,1]{2,1,0:T(8,128)} %copy.317, f32[16,1,256]{2,1,0:T(1,128)} %copy-done.7, f32[16,128,256]{2,1,0:T(8,128)} %get-tuple-element.59, f32[16,1,256]{2,1,0:T(1,128)} %copy-done.8, f32[16,130,1]{2,1,0:T(8,128)S(1)} %copy.315, f32[128,256]{1,0:T(8,128)S(1)} %broadcast_add_fusion), kind=kLoop, calls=%fused_computation.20 | loop fusion | flops 6815744 | bytes 4374784 | tf_op jit(solution)/shard_map/sub | solution.py:105
  367.7 10.0 %copy.320 = f32[16,128,256]{0,2,1:T(8,128)} copy(f32[16,128,256]{2,1,0:T(8,128)} %fusion.1) | data formatting | bytes 4194304 | tf_op jit(solution)/shard_map/sub | solution.py:105
  377.7 3.8 scatter_fusion.3
  381.5 11.0 %copy.321 = f32[16,128,256]{2,1,0:T(8,128)} copy(f32[16,128,256]{0,2,1:T(8,128)} %scatter_fusion.3) | data formatting | bytes 4194304 | tf_op jit(solution)/shard_map/scatter-add | solution.py:115
  394.0 5.2 %all-to-all-start.10 = ((f32[16,1,512]{2,1,0:T(1,128)}), f32[16,1,512]{2,1,0:T(1,128)S(1)}, u32[]{:S(2)}, u32[]{:S(2)}) async-start(f32[16,1,512]{2,1,0:T(1,128)} %reshape.410), calls=%async_computation.10 | async-start | bytes 65536 | tf_op jit(solution)/shard_map/all_to_all | solution.py:50
  406.0 3.8 all-reduce.12
  409.8 7.8 %all-reduce.3 = (f32[16]{0:T(128)S(1)}, f32[16]{0:T(128)S(1)}) all-reduce(f32[16]{0:T(128)S(1)} %get-tuple-element.49, f32[16]{0:T(128)S(1)} %get-tuple-element.50), channel_id=1, replica_groups=mesh['row_0'=2,'row_1'=4,'row_2'=2,'col_0'=4,'col_1'=2] {'row_1'}, use_global_device_ids=true, to_apply=%region_36.38 | all-reduce | flops 32 | bytes 256 | tf_op jit(solution)/shard_map/psum | solution.py:56
  417.6 5.7 %all-reduce.9 = (f32[16]{0:T(128)S(1)}, f32[16]{0:T(128)S(1)}) all-reduce(f32[16]{0:T(128)S(1)} %get-tuple-element.31, f32[16]{0:T(128)S(1)} %get-tuple-element.32), channel_id=1, replica_groups=mesh['row_0'=2,'row_1'=4,'row_2'=2,'col_0'=4,'col_1'=2] {'row_2'}, use_global_device_ids=true, to_apply=%region_37.39 | all-reduce | flops 32 | bytes 256 | tf_op jit(solution)/shard_map/psum | solution.py:56
  423.3 8.9 %all-reduce = (f32[16]{0:T(128)S(1)}, f32[16]{0:T(128)S(1)}) all-reduce(f32[16]{0:T(128)S(1)} %get-tuple-element.43, f32[16]{0:T(128)S(1)} %get-tuple-element.44), channel_id=1, replica_groups=mesh['row_0'=2,'row_1'=4,'row_2'=2,'col_0'=4,'col_1'=2] {'col_0'}, use_global_device_ids=true, to_apply=%region_38.40 | all-reduce | flops 32 | bytes 256 | tf_op jit(solution)/shard_map/psum | solution.py:56
  432.2 5.3 %all-reduce.6 = (f32[16]{0:T(128)S(1)}, f32[16]{0:T(128)S(1)}) all-reduce(f32[16]{0:T(128)S(1)} %get-tuple-element.25, f32[16]{0:T(128)S(1)} %get-tuple-element.26), channel_id=1, replica_groups=mesh['row_0'=2,'row_1'=4,'row_2'=2,'col_0'=4,'col_1'=2] {'col_1'}, use_global_device_ids=true, to_apply=%region_39.41 | all-reduce | flops 32 | bytes 256 | tf_op jit(solution)/shard_map/psum | solution.py:56
  438.2 4.6 %multiply_add_fusion = f32[16,128,256]{2,1,0:T(8,128)} fusion(f32[16,128,256]{2,1,0:T(8,128)S(1)} %broadcast_divide_fusion.1, f32[16]{0:T(128)S(1)} %get-tuple-element.56, f32[16]{0:T(128)S(1)} %get-tuple-element.55, f32[16]{0:T(128)S(1)} %copy-done.13, f32[16]{0:T(128)S(1)} %copy-done.11, f32[16]{0:T(128)S(1)} %div.99, f32[16,128,256]{2,1,0:T(8,128)} %param.9, ...), kind=kLoop, calls=%fused_computation.54 | loop fusion | flops 5767168 | bytes 8520000 | tf_op jit(solution)/shard_map/add | solution.py:139
  (226 shorter events, 113.3 us)
Async XLA Ops:
  0.6 15.6 %copy-start = (f32[1,32,32]{2,1,0:T(8,128)S(1)}, f32[1,32,32]{2,1,0:T(8,128)}, u32[]{:S(2)}) copy-start(f32[1,32,32]{2,1,0:T(8,128)} %param.13) | copy-start | bytes 12292
  0.6 6.5 %copy-start.1 = (f32[16,128,256]{2,1,0:T(8,128)S(1)}, f32[16,128,256]{2,1,0:T(8,128)}, u32[]{:S(2)}) copy-start(f32[16,128,256]{2,1,0:T(8,128)} %param.9) | copy-start | bytes 6291460
  2.6 59.5 %copy-start.19 = (f32[32]{0:T(128)}, f32[32]{0:T(128)S(1)}, u32[]{:S(2)}) copy-start(f32[32]{0:T(128)S(1)} %get-tuple-element.69) | copy-start | bytes 388
  2.6 59.5 %copy-start.21 = (pred[32]{0:T(512)(128)(4,1)}, pred[32]{0:T(512)(128)(4,1)S(1)}, u32[]{:S(2)}) copy-start(pred[32]{0:T(512)(128)(4,1)S(1)} %get-tuple-element.87) | copy-start | bytes 100
  5.0 196.9 %copy-start.18 = (f32[32]{0:T(128)}, f32[32]{0:T(128)S(1)}, u32[]{:S(2)}) copy-start(f32[32]{0:T(128)S(1)} %broadcast_select_fusion) | copy-start | bytes 388
  7.2 9.0 %copy-start.4 = (f32[16,32]{1,0:T(8,128)S(1)}, f32[16,32]{1,0:T(8,128)}, u32[]{:S(2)}) copy-start(f32[16,32]{1,0:T(8,128)} %param.11) | copy-start | bytes 6148
  9.3 38.7 %collective-permute-start = (f32[16,1,256]{2,1,0:T(1,128)}, f32[16,1,256]{2,1,0:T(1,128)S(1)}, u32[]{:S(2)}, u32[]{:S(2)}) collective-permute-start(f32[16,1,256]{2,1,0:T(1,128)} %get-tuple-element.82), channel_id=1, source_target_pairs={{8,0},{16,8},{24,16},{32,24},{40,32},{48,40},{56,48},{64,56},{72,6... | collective-permute-start | bytes 49160 | tf_op jit(solution)/shard_map/ppermute | solution.py:23
  12.6 35.4 %collective-permute-start.1 = (f32[16,1,256]{2,1,0:T(1,128)S(1)}, f32[16,1,256]{2,1,0:T(1,128)S(1)}, u32[]{:S(2)}, u32[]{:S(2)}) collective-permute-start(f32[16,1,256]{2,1,0:T(1,128)S(1)} %get-tuple-element.81), channel_id=1, source_target_pairs={{0,8},{8,16},{16,24},{24,32},{32,40},{40,48},{48,56},{56,64},{64,7... | collective-permute-start | bytes 49160 | tf_op jit(solution)/shard_map/ppermute | solution.py:20
  17.1 19.7 %all-to-all-start = ((f32[8,1,512]{2,1,0:T(1,128)}), f32[8,1,512]{2,1,0:T(1,128)S(1)}, u32[]{:S(2)}, u32[]{:S(2)}) async-start(f32[8,1,512]{2,1,0:T(1,128)} %reshape.390), calls=%async_computation | async-start | bytes 32768 | tf_op jit(solution)/shard_map/all_to_all | solution.py:36
  24.4 94.1 %copy-start.23 = (s32[1024]{0:T(1024)}, s32[1024]{0:T(1024)S(1)}, u32[]{:S(2)}) copy-start(s32[1024]{0:T(1024)S(1)} %pad_clamp_fusion) | copy-start | bytes 12292
  24.4 263.5 %copy-start.14 = (pred[32]{0:T(512)(128)(4,1)}, pred[32]{0:T(512)(128)(4,1)S(1)}, u32[]{:S(2)}) copy-start(pred[32]{0:T(512)(128)(4,1)S(1)} %compare_and_fusion) | copy-start | bytes 100
  24.4 10.8 %copy-start.3 = (f32[256,512]{1,0:T(8,128)S(1)}, f32[256,512]{1,0:T(8,128)}, u32[]{:S(2)}) copy-start(f32[256,512]{1,0:T(8,128)} %param.12) | copy-start | bytes 1572868
  35.2 252.7 %copy-start.16 = (f32[32]{0:T(128)}, f32[32]{0:T(128)S(1)}, u32[]{:S(2)}) copy-start(f32[32]{0:T(128)S(1)} %dynamic_slice.3) | copy-start | bytes 388
  40.7 25.2 %all-to-all-start.1 = ((f32[8,1,1024]{2,1,0:T(1,128)}), f32[8,1,1024]{2,1,0:T(1,128)S(1)}, u32[]{:S(2)}, u32[]{:S(2)}) async-start(f32[8,1,1024]{2,1,0:T(1,128)} %reshape.392), calls=%async_computation.1 | async-start | bytes 65536 | tf_op jit(solution)/shard_map/all_to_all | solution.py:109
  53.4 9.5 %collective-permute-start.2 = (f32[16,130,1]{1,0,2:T(8,128)S(1)}, f32[16,130,1]{1,0,2:T(8,128)S(1)}, u32[]{:S(2)}, u32[]{:S(2)}) collective-permute-start(f32[16,130,1]{1,0,2:T(8,128)S(1)} %copy.286), channel_id=1, source_target_pairs={{1,0},{2,1},{3,2},{4,3},{5,4},{6,5},{7,6},{9,8},{10,9},{11,10},{12... | collective-permute-start | bytes 24968 | tf_op jit(solution)/shard_map/ppermute | solution.py:23
  56.6 7.9 %collective-permute-start.3 = (f32[16,130,1]{1,0,2:T(8,128)S(1)}, f32[16,130,1]{1,0,2:T(8,128)S(1)}, u32[]{:S(2)}, u32[]{:S(2)}) collective-permute-start(f32[16,130,1]{1,0,2:T(8,128)S(1)} %copy.288), channel_id=1, source_target_pairs={{0,1},{1,2},{2,3},{3,4},{4,5},{5,6},{6,7},{8,9},{9,10},{10,11},{11... | collective-permute-start | bytes 24968 | tf_op jit(solution)/shard_map/ppermute | solution.py:20
  65.9 42.5 %all-to-all-start.3 = ((f32[8,1,512]{2,1,0:T(1,128)}), f32[8,1,512]{2,1,0:T(1,128)S(1)}, u32[]{:S(2)}, u32[]{:S(2)}) async-start(f32[8,1,512]{2,1,0:T(1,128)} %reshape.396), calls=%async_computation.3 | async-start | bytes 32768 | tf_op jit(solution)/shard_map/all_to_all | solution.py:36
  108.4 12.9 %all-to-all-start.2 = ((f32[16,1,512]{2,1,0:T(1,128)}), f32[16,1,512]{2,1,0:T(1,128)S(1)}, u32[]{:S(2)}, u32[]{:S(2)}) async-start(f32[16,1,512]{2,1,0:T(1,128)} %reshape.394), calls=%async_computation.2 | async-start | bytes 65536 | tf_op jit(solution)/shard_map/all_to_all | solution.py:50
  156.1 22.3 %all-to-all-start.4 = ((f32[8,1,512]{2,1,0:T(1,128)}), f32[8,1,512]{2,1,0:T(1,128)S(1)}, u32[]{:S(2)}, u32[]{:S(2)}) async-start(f32[8,1,512]{2,1,0:T(1,128)} %reshape.398), calls=%async_computation.4 | async-start | bytes 32768 | tf_op jit(solution)/shard_map/all_to_all | solution.py:36
  170.4 19.0 %collective-permute-start.4 = (f32[16,1,256]{2,1,0:T(1,128)S(1)}, f32[16,1,256]{2,1,0:T(1,128)S(1)}, u32[]{:S(2)}, u32[]{:S(2)}) collective-permute-start(f32[16,1,256]{2,1,0:T(1,128)S(1)} %get-tuple-element.80), channel_id=1, source_target_pairs={{8,0},{16,8},{24,16},{32,24},{40,32},{48,40},{56,48},{64,56},{72,6... | collective-permute-start | bytes 49160 | tf_op jit(solution)/shard_map/ppermute | solution.py:23
  176.1 13.3 %collective-permute-start.5 = (f32[16,1,256]{2,1,0:T(1,128)S(1)}, f32[16,1,256]{2,1,0:T(1,128)S(1)}, u32[]{:S(2)}, u32[]{:S(2)}) collective-permute-start(f32[16,1,256]{2,1,0:T(1,128)S(1)} %get-tuple-element.79), channel_id=1, source_target_pairs={{0,8},{8,16},{16,24},{24,32},{32,40},{40,48},{48,56},{56,64},{64,7... | collective-permute-start | bytes 49160 | tf_op jit(solution)/shard_map/ppermute | solution.py:20
  182.5 23.2 %all-to-all-start.5 = ((f32[8,1,1024]{2,1,0:T(1,128)}), f32[8,1,1024]{2,1,0:T(1,128)S(1)}, u32[]{:S(2)}, u32[]{:S(2)}) async-start(f32[8,1,1024]{2,1,0:T(1,128)} %reshape.400), calls=%async_computation.5 | async-start | bytes 65536 | tf_op jit(solution)/shard_map/all_to_all | solution.py:109
  191.4 10.5 %copy-start.20 = (f32[32]{0:T(128)S(1)}, f32[32]{0:T(128)}, u32[]{:S(2)}) copy-start(f32[32]{0:T(128)} %copy-done.19) | copy-start | bytes 388
  191.4 10.5 %copy-start.22 = (pred[32]{0:T(512)(128)(4,1)S(1)}, pred[32]{0:T(512)(128)(4,1)}, u32[]{:S(2)}) copy-start(pred[32]{0:T(512)(128)(4,1)} %copy-done.21) | copy-start | bytes 100
  193.2 9.6 %collective-permute-start.6 = (f32[16,130,1]{1,0,2:T(8,128)S(1)}, f32[16,130,1]{1,0,2:T(8,128)S(1)}, u32[]{:S(2)}, u32[]{:S(2)}) collective-permute-start(f32[16,130,1]{1,0,2:T(8,128)S(1)} %copy.300), channel_id=1, source_target_pairs={{1,0},{2,1},{3,2},{4,3},{5,4},{6,5},{7,6},{9,8},{10,9},{11,10},{12... | collective-permute-start | bytes 24968 | tf_op jit(solution)/shard_map/ppermute | solution.py:23
  196.4 7.9 %collective-permute-start.7 = (f32[16,130,1]{1,0,2:T(8,128)S(1)}, f32[16,130,1]{1,0,2:T(8,128)S(1)}, u32[]{:S(2)}, u32[]{:S(2)}) collective-permute-start(f32[16,130,1]{1,0,2:T(8,128)S(1)} %copy.302), channel_id=1, source_target_pairs={{0,1},{1,2},{2,3},{3,4},{4,5},{5,6},{6,7},{8,9},{9,10},{10,11},{11... | collective-permute-start | bytes 24968 | tf_op jit(solution)/shard_map/ppermute | solution.py:20
  205.7 38.6 %all-to-all-start.7 = ((f32[8,1,512]{2,1,0:T(1,128)}), f32[8,1,512]{2,1,0:T(1,128)S(1)}, u32[]{:S(2)}, u32[]{:S(2)}) async-start(f32[8,1,512]{2,1,0:T(1,128)} %reshape.404), calls=%async_computation.7 | async-start | bytes 32768 | tf_op jit(solution)/shard_map/all_to_all | solution.py:36
  244.3 10.6 %all-to-all-start.6 = ((f32[16,1,512]{2,1,0:T(1,128)}), f32[16,1,512]{2,1,0:T(1,128)S(1)}, u32[]{:S(2)}, u32[]{:S(2)}) async-start(f32[16,1,512]{2,1,0:T(1,128)} %reshape.402), calls=%async_computation.6 | async-start | bytes 65536 | tf_op jit(solution)/shard_map/all_to_all | solution.py:50
  287.4 6.6 %copy-start.24 = (f32[16]{0:T(128)}, f32[16]{0:T(128)S(1)}, u32[]{:S(2)}) copy-start(f32[16]{0:T(128)S(1)} %get-tuple-element.39) | copy-start | bytes 196
  287.9 6.0 %copy-start.10 = (f32[16]{0:T(128)}, f32[16]{0:T(128)S(1)}, u32[]{:S(2)}) copy-start(f32[16]{0:T(128)S(1)} %get-tuple-element.61) | copy-start | bytes 196
  287.9 6.0 %copy-start.12 = (f32[16]{0:T(128)}, f32[16]{0:T(128)S(1)}, u32[]{:S(2)}) copy-start(f32[16]{0:T(128)S(1)} %get-tuple-element.63) | copy-start | bytes 196
  288.0 5.9 %copy-start.5 = (f32[16,32]{1,0:T(8,128)}, f32[16,32]{1,0:T(8,128)S(1)}, u32[]{:S(2)}) copy-start(f32[16,32]{1,0:T(8,128)S(1)} %multiply_subtract_fusion.2) | copy-start | bytes 6148
  294.8 25.1 %all-to-all-start.8 = ((f32[8,1,512]{2,1,0:T(1,128)}), f32[8,1,512]{2,1,0:T(1,128)S(1)}, u32[]{:S(2)}, u32[]{:S(2)}) async-start(f32[8,1,512]{2,1,0:T(1,128)} %reshape.406), calls=%async_computation.8 | async-start | bytes 32768 | tf_op jit(solution)/shard_map/all_to_all | solution.py:36
  312.0 19.5 %collective-permute-start.8 = (f32[16,1,256]{2,1,0:T(1,128)S(1)}, f32[16,1,256]{2,1,0:T(1,128)S(1)}, u32[]{:S(2)}, u32[]{:S(2)}) collective-permute-start(f32[16,1,256]{2,1,0:T(1,128)S(1)} %get-tuple-element.78), channel_id=1, source_target_pairs={{8,0},{16,8},{24,16},{32,24},{40,32},{48,40},{56,48},{64,56},{72,6... | collective-permute-start | bytes 49160 | tf_op jit(solution)/shard_map/ppermute | solution.py:23
  317.7 13.8 %collective-permute-start.9 = (f32[16,1,256]{2,1,0:T(1,128)S(1)}, f32[16,1,256]{2,1,0:T(1,128)S(1)}, u32[]{:S(2)}, u32[]{:S(2)}) collective-permute-start(f32[16,1,256]{2,1,0:T(1,128)S(1)} %get-tuple-element.77), channel_id=1, source_target_pairs={{0,8},{8,16},{16,24},{24,32},{32,40},{40,48},{48,56},{56,64},{64,7... | collective-permute-start | bytes 49160 | tf_op jit(solution)/shard_map/ppermute | solution.py:20
  324.5 27.8 %all-to-all-start.9 = ((f32[8,1,1024]{2,1,0:T(1,128)}), f32[8,1,1024]{2,1,0:T(1,128)S(1)}, u32[]{:S(2)}, u32[]{:S(2)}) async-start(f32[8,1,1024]{2,1,0:T(1,128)} %reshape.408), calls=%async_computation.9 | async-start | bytes 65536 | tf_op jit(solution)/shard_map/all_to_all | solution.py:109
  338.3 10.8 %collective-permute-start.10 = (f32[16,130,1]{1,0,2:T(8,128)}, f32[16,130,1]{1,0,2:T(8,128)}, u32[]{:S(2)}, u32[]{:S(2)}) collective-permute-start(f32[16,130,1]{1,0,2:T(8,128)} %copy.314), channel_id=1, source_target_pairs={{1,0},{2,1},{3,2},{4,3},{5,4},{6,5},{7,6},{9,8},{10,9},{11,10},{12... | collective-permute-start | bytes 24968 | tf_op jit(solution)/shard_map/ppermute | solution.py:23
  340.7 9.4 %collective-permute-start.11 = (f32[16,130,1]{1,0,2:T(8,128)}, f32[16,130,1]{1,0,2:T(8,128)}, u32[]{:S(2)}, u32[]{:S(2)}) collective-permute-start(f32[16,130,1]{1,0,2:T(8,128)} %copy.316), channel_id=1, source_target_pairs={{0,1},{1,2},{2,3},{3,4},{4,5},{5,6},{6,7},{8,9},{9,10},{10,11},{11... | collective-permute-start | bytes 24968 | tf_op jit(solution)/shard_map/ppermute | solution.py:20
  352.3 41.7 %all-to-all-start.11 = ((f32[8,1,512]{2,1,0:T(1,128)}), f32[8,1,512]{2,1,0:T(1,128)}, u32[]{:S(2)}, u32[]{:S(2)}) async-start(f32[8,1,512]{2,1,0:T(1,128)} %reshape.412), calls=%async_computation.11 | async-start | bytes 32768 | tf_op jit(solution)/shard_map/all_to_all | solution.py:36
  367.7 10.0 %copy-start.9 = (f32[32,16]{1,0:T(8,128)S(1)}, f32[32,16]{1,0:T(8,128)}, u32[]{:S(2)}) copy-start(f32[32,16]{1,0:T(8,128)} %get-tuple-element.57) | copy-start | bytes 6148
  394.0 11.0 %all-to-all-start.10 = ((f32[16,1,512]{2,1,0:T(1,128)}), f32[16,1,512]{2,1,0:T(1,128)S(1)}, u32[]{:S(2)}, u32[]{:S(2)}) async-start(f32[16,1,512]{2,1,0:T(1,128)} %reshape.410), calls=%async_computation.10 | async-start | bytes 65536 | tf_op jit(solution)/shard_map/all_to_all | solution.py:50
  399.2 6.6 %copy-start.6 = (f32[16,32]{1,0:T(8,128)S(1)}, f32[16,32]{1,0:T(8,128)}, u32[]{:S(2)}) copy-start(f32[16,32]{1,0:T(8,128)} %copy-done.5) | copy-start | bytes 6148
  399.2 6.6 %copy-start.15 = (pred[32]{0:T(512)(128)(4,1)S(1)}, pred[32]{0:T(512)(128)(4,1)}, u32[]{:S(2)}) copy-start(pred[32]{0:T(512)(128)(4,1)} %copy-done.14) | copy-start | bytes 100
  399.2 6.6 %copy-start.17 = (f32[32]{0:T(128)S(1)}, f32[32]{0:T(128)}, u32[]{:S(2)}) copy-start(f32[32]{0:T(128)} %copy-done.16) | copy-start | bytes 388
  399.2 38.3 %copy-start.25 = (f32[16]{0:T(128)S(1)}, f32[16]{0:T(128)}, u32[]{:S(2)}) copy-start(f32[16]{0:T(128)} %copy-done.24) | copy-start | bytes 196
  399.2 38.3 %copy-start.26 = (f32[16]{0:T(128)S(1)}, f32[16]{0:T(128)}, u32[]{:S(2)}) copy-start(f32[16]{0:T(128)} %get-tuple-element.62) | copy-start | bytes 196
  399.3 38.3 %copy-start.11 = (f32[16]{0:T(128)S(1)}, f32[16]{0:T(128)}, u32[]{:S(2)}) copy-start(f32[16]{0:T(128)} %copy-done.10) | copy-start | bytes 196
  399.3 38.3 %copy-start.13 = (f32[16]{0:T(128)S(1)}, f32[16]{0:T(128)}, u32[]{:S(2)}) copy-start(f32[16]{0:T(128)} %copy-done.12) | copy-start | bytes 196
  (3 other events, 2.5 us)
where the time goes:
time: 449 us; the launch traced here: 443 us
  local copies, waits for them, and re-layouts  145 us (32%)
  starting transfers between devices  119 us (27%)
  blocking collectives  93.2 us (21%)
  other arithmetic  74.7 us (17%)
  matrix products  5.78 us (1%)
    psum x15, blocking collectives, over_axes(): shard = lax.psum(shard, axis)  93.2 us
    all_to_all x6, starting transfers between devices, sent_to_all(): return lax.all_to_all(copies, axis, split_axis=0, concat_axis=0, tiled=True)  37.3 us
    scatter-add x3, local copies, waits for them, and re-layouts, apply_op(): die = die.at[:, loc_r, loc_c].add(cond_sel * (at_bumps - pkg_at))  33 us
    sub x3, local copies, waits for them, and re-layouts, apply_op(): die = (4.0 + die_shunt) * vd - beside_all  30 us
    div x3, local copies, waits for them, and re-layouts, precond(): return (rd / diag_die, zp.reshape(batch, local_n))  28.7 us
    ppermute x6, starting transfers between devices, with_halo(): lax.ppermute(lax.slice_in_dim(block, block.shape[dim] - width, None, axis...  25.1 us
    sub x3, other arithmetic, apply_op(): die = (4.0 + die_shunt) * vd - beside_all  21.8 us
    all_to_all x3, starting transfers between devices, apply_op(): moved = lax.all_to_all(pieces, COL, split_axis=1, concat_axis=1, tiled=True)  20.5 us
  transfers between devices with their start and end apart: 24, of which 3 were waited for; matrix products, arithmetic and copies ran while one was open for 44% of the time, Pallas kernels for 0%

commit v1 on v0

v1 whole, which is shorter than its diff:
```python
import functools

import jax
import jax.numpy as jnp
from jax import lax
from jax.experimental import pallas as pl
from jax.experimental.pallas import tpu as pltpu
from jax.sharding import Mesh
from jax.sharding import PartitionSpec as P

ROW = ("row_0", "row_1", "row_2")
COL = ("col_0", "col_1")
ROW_COL = ("row_0", "row_1", "row_2", "col_0", "col_1")

K = 16
TR, TC = 128, 256
ER, EC = 136, 384
CELL = 32
PLANES = K + 1
PAIRS = 9
HROWS = 56
OWN = 32
NB = 4096
HI = lax.Precision.HIGHEST


def iota(shape, dim):
    return lax.broadcasted_iota(jnp.int32, shape, dim)


def where_am_i():
    i = (lax.axis_index("row_0") * 4 + lax.axis_index("row_1")) * 2 + lax.axis_index("row_2")
    j = lax.axis_index("col_0") * 2 + lax.axis_index("col_1")
    return i, j


def dot_nt(a, b):
    return lax.dot_general(
        a, b, (((1,), (1,)), ((), ())), precision=HI, preferred_element_type=jnp.float32
    )


def dot_nn(a, b):
    return jnp.dot(a, b, precision=HI, preferred_element_type=jnp.float32)


def spread(j):
    group = iota((128, EC), 1) // CELL
    cell = jnp.where(group <= 8, 8 * j + group, jnp.where(group == 11, 8 * j - 1, -5))
    return (iota((128, EC), 0) % 64 == cell).astype(jnp.float32)


def lattice_chunk(l):
    return jnp.clip(l // 2, 0, NB // 128 - 1)


def extended_rows(parts):
    body = [jnp.broadcast_to(p, (CELL, EC)) for p in parts[1:5]]
    edge = jnp.where(iota((8, EC), 0) < 4, parts[5], parts[0])
    return jnp.concatenate(body + [edge], axis=0)


def padded(scr, x):
    scr[...] = jnp.zeros_like(scr)
    scr[:, 0 : x.shape[1]] = x
    return scr[...]


def pack(vp, vd):
    lane = iota((8, 128), 1)
    hi = pltpu.roll(vp[8:16], 32, 1)
    out = jnp.where(lane < 32, vp[0:8], hi)
    out = jnp.where(lane < 64, out, pltpu.roll(vd[0:8], 64, 1))
    return jnp.where(lane < 96, out, pltpu.roll(vd[8:16], 96, 1))


def gather_bumps(s_ref):
    at = iota((4 * TC, 128), 0)
    pick = (at // TC * 8 + at % TC // CELL == iota((4 * TC, 128), 1)).astype(jnp.float32)
    return dot_nn(s_ref[...], pick)


def down_cells(s_ref, k, z):
    for lr in range(4):
        rows = z[CELL * lr : CELL * (lr + 1)]
        s_ref[pl.ds(k, 1), TC * lr : TC * (lr + 1)] = jnp.sum(rows, axis=0, keepdims=True)


def fill(msg_ref, pay):
    def one(d, c):
        msg_ref[d] = pay
        return c

    lax.fori_loop(0, msg_ref.shape[0], one, 0, unroll=8)


def first_kernel(
    b_ref, sh_ref, bp_ref, p_ref, m_ref, node_ref, cond_ref,
    msg1_ref, msg0_ref, cm_ref, edge_ref, v0p_ref,
    a_ref, s_ref, pad_ref, z_ref,
):
    i, j = where_am_i()
    for t in range(4):
        for d in range(8):
            msg1_ref[d, 32 * t : 32 * (t + 1), :] = p_ref[32 * d : 32 * (d + 1), 128 * t : 128 * (t + 1)]
    lane = iota((TR, 128), 1)
    z = jnp.zeros((TR, 128), jnp.float32)
    for k in range(PLANES):
        lo = b_ref[k, :, 0:128] if k < K else sh_ref[:, 0:128]
        up = b_ref[k, :, 128:256] if k < K else sh_ref[:, 128:256]
        lo = pltpu.roll(lo, 3 * k, 1) if k else lo
        up = pltpu.roll(up, (64 + 3 * k - 125) % 128, 1)
        z = jnp.where((lane >= 3 * k) & (lane < 3 * k + 3), lo, z)
        z = jnp.where((lane >= 64 + 3 * k) & (lane < 67 + 3 * k), up, z)
    z_ref[...] = z.T

    @pl.when(j > 0)
    def _():
        msg1_ref[jnp.maximum(j - 1, 0), 128 : 128 + HROWS, :] = z_ref[0:HROWS, :]

    @pl.when(j < 7)
    def _():
        msg1_ref[jnp.minimum(j + 1, 7), 128 : 128 + HROWS, :] = z_ref[64 : 64 + HROWS, :]

    for k in range(PLANES):
        src = b_ref.at[k] if k < K else sh_ref
        edge_ref[k, 0:8, :] = src[0:8, :]
        edge_ref[k, 8:16, :] = src[TR - 8 : TR, :]
    a_ref[...] = jnp.zeros_like(a_ref)
    ln = iota((1, 128), 1)
    for lr in range(6):
        l = 4 * i + lr - 1
        chunk = lattice_chunk(l)
        ok = (ln // 64 == l % 2) & (l >= 0) & (l < 64)
        nd = node_ref[pl.ds(chunk, 1), :]
        a_ref[lr : lr + 1, :] = jnp.where(ok, nd // 2048 - CELL * l, 0).astype(jnp.float32)
        a_ref[8 + lr : 9 + lr, :] = jnp.where(ok, nd % 2048 - CELL * (ln % 64), 0).astype(jnp.float32)
        a_ref[16 + lr : 17 + lr, :] = jnp.where(ok, cond_ref[pl.ds(chunk, 1), :], 0.0)
    wide = dot_nn(a_ref[...], spread(j))
    maps = [extended_rows([wide[8 * n + lr : 8 * n + lr + 1] for lr in range(6)]) for n in range(3)]
    row = iota((ER, EC), 0)
    here = jnp.where(row < TR, row % CELL, jnp.where(row < TR + 4, row - TR, row - TR + 24))
    cols = iota((ER, EC), 1) % CELL
    hit = (maps[0].astype(jnp.int32) == here) & (maps[1].astype(jnp.int32) == cols)
    cm = jnp.where(hit, maps[2], 0.0)
    cm_ref[...] = cm
    tile = cm[0:TR, 0:TC]
    z_scale = jnp.where(tile > 0.0, 1.0 / (4.0 + sh_ref[...] + tile), 0.0)

    def one(k, c):
        down_cells(s_ref, k, b_ref[k] * z_scale)
        return c

    lax.fori_loop(0, K, one, 0)
    v0p = padded(pad_ref, dot_nt(bp_ref[...], m_ref[0]))
    v0p_ref[...] = v0p
    fill(msg0_ref, pack(v0p, gather_bumps(s_ref)))


def columns_kernel(g1_ref, edge_ref, w_ref, up_ref, dn_ref, y_ref, ext_ref):
    _, j = where_am_i()
    y_ref[...] = jnp.zeros_like(y_ref)

    @pl.when(j < 7)
    def _():
        y_ref[0:HROWS, :] = g1_ref[jnp.minimum(j + 1, 7), 128 : 128 + HROWS, :]

    @pl.when(j > 0)
    def _():
        y_ref[64 : 64 + HROWS, :] = g1_ref[jnp.maximum(j - 1, 0), 128 : 128 + HROWS, :]

    yt = y_ref[...].T
    lane = iota((TR, 128), 1)
    for k in range(PLANES):
        right = pltpu.roll(yt, (128 - 3 * k) % 128, 1) if k else yt
        left = pltpu.roll(yt, (61 - 3 * k) % 128, 1) if (61 - 3 * k) % 128 else yt
        w_ref[k] = jnp.where(lane < 3, right, jnp.where(lane >= 125, left, 0.0))
    first = iota((8, EC), 0) < 4
    for k in range(PLANES):
        for side in range(2):
            ext_ref[side, k, :, 0:TC] = edge_ref[k, 8 * side : 8 * side + 8, :]
            ext_ref[side, k, :, TC:EC] = w_ref[k, (TR - 8) * side : (TR - 8) * side + 8, :]
    for p in range(PAIRS):
        q = min(p + PAIRS, PLANES - 1)
        up_ref[p] = jnp.where(first, ext_ref[0, p], pltpu.roll(ext_ref[0, q], 4, 0))
        dn_ref[p] = jnp.where(first, pltpu.roll(ext_ref[1, p], 4, 0), ext_ref[1, q])


def package_all(g_ref, v_ref):
    lane = iota((8, 128), 1) // 32

    def one(c, carry):
        lo = jnp.zeros((8, 128), jnp.float32)
        hi = jnp.zeros((8, 128), jnp.float32)
        for m in range(4):
            x = g_ref[4 * c + m]
            lo = jnp.where(lane == m, pltpu.roll(x, 32 * m, 1) if m else x, lo)
            hi = jnp.where(lane == m, pltpu.roll(x, (32 * m - 32) % 128, 1) if m != 1 else x, hi)
        at = pl.ds(pl.multiple_of(128 * c, 128), 128)
        v_ref[0:8, at] = lo
        v_ref[8:16, at] = hi
        return carry

    lax.fori_loop(0, NB // 128, one, 0, unroll=4)


def own_die(g_ref, i, j):
    lane = iota((8, 128), 1)
    halves = []
    for h in range(2):
        out = jnp.zeros((8, 128), jnp.float32)
        for m in range(4):
            x = g_ref[8 * i + 4 * (j % 2) + m]
            shift = 8 * m - (64 + 32 * h + 8 * (j // 2)) + 128
            x = pltpu.roll(x, shift % 128, 1)
            out = jnp.where((lane >= 8 * m) & (lane < 8 * m + 8), x, out)
        halves.append(out)
    return jnp.concatenate(halves, axis=0)


def own_conductance(cond_ref, i, j):
    q = 8 * i + j
    row = cond_ref[pl.ds(q // 4, 1), :]
    return pltpu.roll(row, (128 - 32 * (q % 4)) % 128, 1)


def spread_package(v_ref, e_ref, x_ref, i, j):
    ln = iota((K, 128), 1)
    for lr in range(6):
        l = 4 * i + lr - 1
        at = pl.ds(pl.multiple_of(128 * lattice_chunk(l), 128), 128)
        x_ref[K * lr : K * (lr + 1), :] = jnp.where(ln // 64 == l % 2, v_ref[:, at], 0.0)
    e_ref[...] = dot_nn(x_ref[...], spread(j))


def others(x, e_ref, k, cm, rd):
    beside = pltpu.roll(x, 1, 0) + pltpu.roll(x, ER - 1, 0)
    beside = beside + pltpu.roll(x, 1, 1) + pltpu.roll(x, EC - 1, 1)
    vp = extended_rows([e_ref[pl.ds(K * lr + k, 1), :] for lr in range(6)])
    return (beside + cm * vp) * rd


def add_dot(r_ref, at, x):
    s = jnp.sum(x, axis=0, keepdims=True)
    r_ref[pl.ds(at, 1), :] = s[:, 0:128] + s[:, 128:256]


def package_step(g_ref, pm_ref, cond_ref, vp, v_ref, pad_ref, i, j):
    y = padded(pad_ref, dot_nt(v_ref[...], pm_ref[...]))
    y = y + own_conductance(cond_ref, i, j) * (vp - own_die(g_ref, i, j))
    return jnp.where(iota((K, 128), 1) < OWN, y, 0.0)


def second_kernel(
    b_ref, sh_ref, w_ref, bot_ref, top_ref, cm_ref, g_ref, g1_ref, m_ref, cond_ref, bp_ref, v0p_ref,
    v1_ref, rd_ref, dg_ref, pm_ref, v1p_ref, y1_ref, msg_ref, r_ref,
    grp_ref, xs_ref, v_ref, e_ref, x_ref, s_ref, pad_ref,
):
    i, j = where_am_i()
    first = iota((8, EC), 0) < 4
    for p in range(PAIRS):
        bot, top = bot_ref[p], top_ref[p]
        grp_ref[p] = jnp.where(first, bot, pltpu.roll(top, 4, 0))
        if p + PAIRS < PLANES:
            grp_ref[p + PAIRS] = jnp.where(first, pltpu.roll(bot, 4, 0), top)

    def gather_plane(main, k):
        xs_ref[0:TR, 0:TC] = main
        xs_ref[0:TR, TC:EC] = w_ref[k]
        xs_ref[TR:ER, :] = grp_ref[k]
        return xs_ref[...]

    sh = gather_plane(sh_ref[...], K)
    cm = cm_ref[...]
    rd_ref[...] = jnp.where(sh > 0.0, 1.0 / (4.0 + sh + cm), 0.0)
    dg_ref[...] = 4.0 + sh[0:TR, 0:TC] + cm[0:TR, 0:TC]
    for d in range(8):
        for t in range(4):
            c = 4 * d + t
            pm_ref[:, 128 * c : 128 * (c + 1)] = g1_ref[d, 32 * t : 32 * (t + 1), :]
    package_all(g_ref, v_ref)
    spread_package(v_ref, e_ref, x_ref, i, j)

    def one(k, c):
        rd = rd_ref[...]
        x0 = gather_plane(b_ref[k], k) * rd
        x1 = x0 - others(x0, e_ref, k, cm_ref[...], rd)
        v1_ref[k] = x1
        dg = dg_ref[...]
        a, b = x0[0:TR, 0:TC], x1[0:TR, 0:TC]
        add_dot(r_ref, k, dg * a * a)
        add_dot(r_ref, K + k, dg * a * b)
        add_dot(r_ref, 2 * K + k, dg * b * b)
        down_cells(s_ref, k, jnp.where(cm_ref[0:TR, 0:TC] > 0.0, b, 0.0))
        return c

    lax.fori_loop(0, K, one, 0)
    v0p = v0p_ref[...]
    bp = padded(pad_ref, bp_ref[...])
    y = package_step(g_ref, pm_ref, cond_ref, v0p, v_ref, pad_ref, i, j)
    v1p = padded(pad_ref, dot_nt(y[:, 0:OWN], m_ref[0]))
    v1p_ref[...] = v1p
    y1_ref[...] = y
    r_ref[0:K, :] += v0p * bp
    r_ref[K : 2 * K, :] += v0p * y
    r_ref[2 * K : 3 * K, :] += v1p * y
    fill(msg_ref, pack(v1p, gather_bumps(s_ref)))


def third_kernel(
    v1_ref, rd_ref, dg_ref, cm_ref, g_ref, pm_ref, m_ref, cond_ref, v1p_ref, y1_ref,
    w_ref, wp_ref, msg_ref, r_ref,
    v_ref, e_ref, x_ref, s_ref, pad_ref,
):
    i, j = where_am_i()
    package_all(g_ref, v_ref)
    spread_package(v_ref, e_ref, x_ref, i, j)

    def one(k, c):
        x1 = v1_ref[k]
        x2 = -others(x1, e_ref, k, cm_ref[...], rd_ref[...])
        w_ref[k] = x2
        dg = dg_ref[...]
        a, b = x1[0:TR, 0:TC], x2[0:TR, 0:TC]
        add_dot(r_ref, k, dg * a * b)
        add_dot(r_ref, K + k, dg * b * b)
        down_cells(s_ref, k, jnp.where(cm_ref[0:TR, 0:TC] > 0.0, b, 0.0))
        return c

    lax.fori_loop(0, K, one, 0)
    v1p = v1p_ref[...]
    y = package_step(g_ref, pm_ref, cond_ref, v1p, v_ref, pad_ref, i, j)
    wp = padded(pad_ref, dot_nt(y[:, 0:OWN], m_ref[0])) - v1p
    wp_ref[...] = wp
    r_ref[0:K, :] += wp * y1_ref[...]
    r_ref[K : 2 * K, :] += wp * (y - y1_ref[...])
    fill(msg_ref, pack(wp, gather_bumps(s_ref)))


def fourth_kernel(
    v2_ref, rd_ref, dg_ref, cm_ref, g_ref, pm_ref, cond_ref, v2p_ref, ra_ref, rb_ref,
    msg_ref,
    v_ref, e_ref, x_ref, pad_ref, r_ref,
):
    i, j = where_am_i()
    package_all(g_ref, v_ref)
    spread_package(v_ref, e_ref, x_ref, i, j)
    r_ref[...] = jnp.zeros_like(r_ref)
    r_ref[0 : 3 * K, :] = ra_ref[...]
    r_ref[3 * K : 5 * K, :] = rb_ref[...]

    def one(k, c):
        x2 = v2_ref[k]
        x3 = x2 - others(x2, e_ref, k, cm_ref[...], rd_ref[...])
        add_dot(r_ref, 5 * K + k, dg_ref[...] * x2[0:TR, 0:TC] * x3[0:TR, 0:TC])
        return c

    lax.fori_loop(0, K, one, 0)
    v2p = v2p_ref[...]
    y = package_step(g_ref, pm_ref, cond_ref, v2p, v_ref, pad_ref, i, j)
    r_ref[5 * K : 6 * K, :] += v2p * y
    sums = dot_nt(jnp.ones((8, 128), jnp.float32), r_ref[...])
    fill(msg_ref, sums[0:1])


def last_kernel(
    g_ref, b_ref, rd_ref, v1_ref, v2_ref, v0p_ref, v1p_ref, v2p_ref,
    xd_ref, xp_ref, c_ref,
):
    total = jnp.sum(g_ref[...], axis=0)
    total = jnp.broadcast_to(total, (8, 128))
    m = [pltpu.roll(total, (128 - K * n) % 128, 1) if n else total for n in range(6)]
    g00, g01, g02, g11, g12, g22 = m[1], m[2], m[3], m[2] + m[3], m[3] + m[4], m[5]
    f1, f2 = g01 / g00, g02 / g00
    a11, a12, h1 = g11 - f1 * g01, g12 - f1 * g02, g00 - f1 * m[0]
    a22, h2 = g22 - f2 * g02, g01 - g00 - f2 * m[0]
    f3 = a12 / a11
    c2 = (h2 - f3 * h1) / (a22 - f3 * a12)
    c1 = (h1 - a12 * c2) / a11
    c0 = (m[0] - g01 * c1 - g02 * c2) / g00
    rd = rd_ref[...]
    at = iota((K, 128), 0) == iota((K, 128), 1)
    cols = []
    for n, c in enumerate((c0, c1, c2)):
        col = jnp.sum(jnp.where(at, c[0:1], 0.0), axis=1, keepdims=True)
        cols.append(col)
        c_ref[n] = jnp.broadcast_to(col, (K, TC))
    xp = cols[0] * v0p_ref[...] + cols[1] * v1p_ref[...] + cols[2] * v2p_ref[...]
    xp_ref[...] = xp[:, 0:OWN]

    def one(k, carry):
        c0, c1, c2 = (c_ref[n, pl.ds(k, 1), :] for n in range(3))
        xd_ref[k] = (c0 * b_ref[k]) * rd + c1 * v1_ref[k] + c2 * v2_ref[k]
        return carry

    lax.fori_loop(0, K, one, 0)


def f32(*shape):
    return jax.ShapeDtypeStruct(shape, jnp.float32)


def vm(*shape):
    return pltpu.VMEM(shape, jnp.float32)


def call(kernel, outs, scratch, args, limit=30, **kw):
    return pl.pallas_call(
        kernel,
        out_shape=outs,
        scratch_shapes=scratch,
        compiler_params=pltpu.CompilerParams(vmem_limit_bytes=limit << 20),
        name=kernel.__name__,
        **kw,
    )(*args)


def swapped(x, axes):
    return lax.all_to_all(x, axes, 0, 0, tiled=True)


def body(
    die_current, die_shunt, pkg_current, pkg_matrix, pkg_block_inv, bump_node, bump_conductance
):
    nodes = bump_node.reshape(NB // 128, 128)
    cond = bump_conductance.reshape(NB // 128, 128)
    stage = [vm(K, NB), vm(6 * K, EC), vm(6 * K, 128), vm(K, 4 * TC), vm(K, 128)]
    gathered = f32(128, 8, 128)
    msg1, msg0, cm, edge, v0p = call(
        first_kernel,
        (f32(8, 128 + HROWS, 128), gathered, f32(ER, EC), f32(PLANES, 16, TC), f32(K, 128)),
        [vm(24, 128), vm(K, 4 * TC), vm(K, 128), vm(128, 128)],
        (die_current, die_shunt, pkg_current, pkg_matrix, pkg_block_inv, nodes, cond),
    )
    g1 = swapped(msg1, COL)
    w, up, dn = call(
        columns_kernel,
        (f32(PLANES, TR, 128), f32(PAIRS, 8, EC), f32(PAIRS, 8, EC)),
        [vm(128, 128), vm(2, PLANES, 8, EC)],
        (g1, edge),
    )
    n = lax.axis_size(ROW)
    bot = lax.ppermute(up, ROW, [(r + 1, r) for r in range(n - 1)])
    top = lax.ppermute(dn, ROW, [(r, r + 1) for r in range(n - 1)])
    g0 = swapped(msg0, ROW_COL)
    v1, rd, dg, pm, v1p, y1, msg, ra = call(
        second_kernel,
        (f32(K, ER, EC), f32(ER, EC), f32(TR, TC), f32(OWN, NB), f32(K, 128), f32(K, 128), gathered, f32(3 * K, 128)),
        [vm(PLANES + 1, 8, EC), vm(ER, EC)] + stage,
        (die_current, die_shunt, w, bot, top, cm, g0, g1, pkg_block_inv, cond, pkg_current, v0p),
    )
    g = swapped(msg, ROW_COL)
    v2, v2p, msg, rb = call(
        third_kernel,
        (f32(K, ER, EC), f32(K, 128), gathered, f32(2 * K, 128)),
        stage,
        (v1, rd, dg, cm, g, pm, pkg_block_inv, cond, v1p, y1),
    )
    g = swapped(msg, ROW_COL)
    msg = call(
        fourth_kernel,
        f32(128, 1, 128),
        stage[:3] + [vm(K, 128), vm(128, 128)],
        (v2, rd, dg, cm, g, pm, cond, v2p, ra, rb),
    )
    g = swapped(msg, ROW_COL)
    whole = lambda *s: pl.BlockSpec(s, lambda t: (0,) * len(s))
    return call(
        last_kernel,
        (f32(K, TR, TC), f32(K, OWN)),
        [vm(3, K, TC)],
        (g, die_current, rd, v1, v2, v0p, v1p, v2p),
        grid=(1,),
        in_specs=[
            whole(128, 1, 128), whole(K, TR, TC), whole(TR, TC), whole(K, TR, TC), whole(K, TR, TC),
            whole(K, 128), whole(K, 128), whole(K, 128),
        ],
        out_specs=(whole(K, TR, TC), whole(K, OWN)),
    )


def solution(mesh):
    torus = Mesh(mesh.devices.reshape(2, 4, 2, 4, 2), ROW_COL)
    placed = (
        P(None, ROW, COL),
        P(ROW, COL),
        P(None, ROW_COL),
        P(ROW, COL),
        P(ROW_COL, None, None),
        P(),
        P(),
    )
    return jax.shard_map(
        body,
        mesh=torus,
        in_specs=placed,
        out_specs=(P(None, ROW, COL), P(None, ROW_COL)),
        check_vma=False,
    )
```

time: 449 us -> 131 us (0.29); the launches traced: 443 us -> 131 us
  local copies, waits for them, and re-layouts: 145 us -> 11.2 us
  starting transfers between devices: 119 us -> 13.3 us
  other arithmetic: 74.7 us -> 0 us
  Pallas kernels: 0 us -> 25 us
  blocking collectives: 93.2 us -> 76.5 us
  matrix products: 5.78 us -> 0 us
    psum x15 -> x0, blocking collectives: 93.2 us -> none  [over_axes(): shard = lax.psum(shard, axis)]
    all_to_all x0 -> x4, blocking collectives: none -> 76.5 us  [swapped(): return lax.all_to_all(x, axes, 0, 0, tiled=True)]
    all_to_all x12 -> x1, starting transfers between devices: 74.9 us -> 7.71 us  [swapped(): return lax.all_to_all(x, axes, 0, 0, tiled=True)]
    ppermute x12 -> x2, starting transfers between devices: 43.6 us -> 5.57 us  [the longest x1 2.96 us: body(): bot = lax.ppermute(up, ROW, [(r + 1, r) for r in range(n - 1)])]
    scatter-add x3 -> x0, local copies, waits for them, and re-layouts: 33 us -> none  [apply_op(): die = die.at[:, loc_r, loc_c].add(cond_sel * (at_bumps - pkg_at))]
    sub x3 -> x0, local copies, waits for them, and re-layouts: 30 us -> none  [apply_op(): die = (4.0 + die_shunt) * vd - beside_all]
    div x3 -> x0, local copies, waits for them, and re-layouts: 28.7 us -> none  [precond(): return (rd / diag_die, zp.reshape(batch, local_n))]
    pallas_call x0 -> x6, Pallas kernels: none -> 25 us  [call(): pl.pallas_call(kernel, out_shape=outs, scratch_shapes=scratch, compiler_p...]
  transfers between devices with their start and end apart: 24 -> 3, of which waited for: 3 -> 1; matrix products, arithmetic and copies ran while one was open for 44% -> 0% of each run, Pallas kernels for 0% -> 1%
where the time goes in v1:
time: 131 us
  blocking collectives  76.5 us (58%)
  Pallas kernels  25 us (19%)
  starting transfers between devices  13.3 us (10%)
  local copies, waits for them, and re-layouts  11.2 us (9%)
  waiting for transfers between devices  3.87 us (3%)
    all_to_all x4, blocking collectives, swapped(): return lax.all_to_all(x, axes, 0, 0, tiled=True)  76.5 us
    pallas_call x6, Pallas kernels, call(): pl.pallas_call(kernel, out_shape=outs, scratch_shapes=scratch, compiler_p...  25 us
    unnamed x38, local copies, waits for them, and re-layouts  11.2 us
    all_to_all x1, starting transfers between devices, swapped(): return lax.all_to_all(x, axes, 0, 0, tiled=True)  7.71 us
    all_to_all x1, waiting for transfers between devices, swapped(): return lax.all_to_all(x, axes, 0, 0, tiled=True)  3.87 us
    ppermute x1, starting transfers between devices, body(): bot = lax.ppermute(up, ROW, [(r + 1, r) for r in range(n - 1)])  2.96 us
  transfers between devices with their start and end apart: 3, of which 1 were waited for; matrix products, arithmetic and copies ran while one was open for 0% of the time, Pallas kernels for 1%

profile of v1, /device:TPU:1, one launch (start us, length us, event | category | flops | bytes accessed | tf_op | source)
XLA Modules:
  0.0 130.7 jit_solution(646304094293526417)
XLA Ops:
  0.6 0.0 copy-start
  0.6 1.6 %copy-done = f32[16,128,256]{2,1,0:T(8,128)S(1)} copy-done((f32[16,128,256]{2,1,0:T(8,128)S(1)}, f32[16,128,256]{2,1,0:T(8,128)}, u32[]{:S(2)}) %copy-start) | copy-done | bytes 2097176
  2.2 0.0 copy-start.6
  2.2 0.9 copy-done.6
  3.1 0.0 copy-start.9
  3.1 1.0 copy-done.9
  4.2 0.0 copy-start.12
  4.2 0.7 copy-done.12
  4.9 0.0 copy-start.14
  4.9 0.7 copy-done.14
  5.6 0.0 copy-start.16
  5.6 0.7 copy-done.16
  6.3 0.0 copy-start.18
  6.3 0.7 copy-done.18
  7.0 2.0 %first_kernel.1 = (f32[8,184,128]{2,1,0:T(8,128)S(1)}, f32[128,8,128]{2,1,0:T(8,128)S(1)}, f32[136,384]{1,0:T(8,128)S(1)}, f32[17,16,256]{2,1,0:T(8,128)S(1)}, f32[16,128]{1,0:T(8,128)S(1)}) custom-call(f32[16,128,256]{2,1,0:T(8,128)S(1)} %copy-done, f32[128,256]{1,0:T(8,128)S(1)} %copy-done.6, f32[16,32]{1,0:T(8,128)S(1)} %copy-done.16, ...), custom_call_target="tpu_custom_call" | custom-call | tf_op jit(solution)/shard_map/first_kernel/pallas_call | solution.py:408
  9.1 0.0 copy-start.2
  9.1 0.7 copy-done.2
  9.8 0.0 copy-start.13
  9.8 0.0 copy-start.15
  9.8 0.0 copy-start.17
  9.8 20.7 %all_to_all.25.g1_ref = f32[8,184,128]{2,1,0:T(8,128)S(1)} all-to-all(f32[8,184,128]{2,1,0:T(8,128)S(1)} %get-tuple-element.22), channel_id=1, replica_groups=mesh['row_0'=2,'row_1'=4,'row_2'=2,'col_0'=4,'col_1'=2] {'col_0','col_1'}, dimensions={0} | all-to-all | bytes 1507328 | tf_op jit(solution)/shard_map/all_to_all | solution.py:419
  30.5 0.0 copy-done.8
  30.5 0.0 copy-done.10
  30.5 7.7 %all-to-all-start.1 = ((f32[128,8,128]{2,1,0:T(8,128)}), f32[128,8,128]{2,1,0:T(8,128)S(1)}, u32[]{:S(2)}, u32[]{:S(2)}) async-start(f32[128,8,128]{2,1,0:T(8,128)} %copy-done.8), calls=%async_computation.1 | async-start | bytes 1048576 | tf_op jit(solution)/shard_map/all_to_all | solution.py:419
  38.2 0.0 copy-start.11
  38.3 0.9 copy-done.11
  39.2 1.4 %columns_kernel.1 = (f32[17,128,128]{2,1,0:T(8,128)S(1)}, f32[9,8,384]{2,1,0:T(8,128)}, f32[9,8,384]{2,1,0:T(8,128)}) custom-call(f32[8,184,128]{2,1,0:T(8,128)S(1)} %all_to_all.25.g1_ref, f32[17,16,256]{2,1,0:T(8,128)S(1)} %copy-done.11), custom_call_target="tpu_custom_call" | custom-call | tf_op jit(solution)/shard_map/columns_kernel/pallas_call | solution.py:408
  40.6 1.0 copy-done.4
  41.6 3.0 %collective-permute-start = (f32[9,8,384]{2,1,0:T(8,128)}, f32[9,8,384]{2,1,0:T(8,128)}, u32[]{:S(2)}, u32[]{:S(2)}) collective-permute-start(f32[9,8,384]{2,1,0:T(8,128)} %get-tuple-element.25), channel_id=1, source_target_pairs={{8,0},{16,8},{24,16},{32,24},{40,32},{48,40},{56,48},{64,56},{72,6... | collective-permute-start | bytes 331784 | tf_op jit(solution)/shard_map/ppermute | solution.py:443
  44.5 2.6 %collective-permute-start.1 = (f32[9,8,384]{2,1,0:T(8,128)}, f32[9,8,384]{2,1,0:T(8,128)}, u32[]{:S(2)}, u32[]{:S(2)}) collective-permute-start(f32[9,8,384]{2,1,0:T(8,128)} %get-tuple-element.26), channel_id=1, source_target_pairs={{0,8},{8,16},{16,24},{24,32},{32,40},{40,48},{48,56},{56,64},{64,7... | collective-permute-start | bytes 331784 | tf_op jit(solution)/shard_map/ppermute | solution.py:444
  47.2 3.9 %all-to-all-done.1.g_ref = f32[128,8,128]{2,1,0:T(8,128)S(1)} async-done(((f32[128,8,128]{2,1,0:T(8,128)}), f32[128,8,128]{2,1,0:T(8,128)S(1)}, u32[]{:S(2)}, u32[]{:S(2)}) %all-to-all-start.1) | async-done | bytes 524320 | tf_op jit(solution)/shard_map/all_to_all | solution.py:419
  51.0 0.0 collective-permute-done.bot_ref
  51.0 0.0 collective-permute-done.1.top_ref
  51.0 0.0 copy-done.1
  51.0 0.0 copy-done.7
  51.0 0.0 copy-done.13
  51.1 0.0 copy-done.15
  51.1 0.0 copy-done.17
  51.1 0.0 copy-start.3
  51.1 0.9 copy-done.3
  52.0 1.2 copy-done.5
  53.3 7.6 %second_kernel.1 = (f32[16,136,384]{2,1,0:T(8,128)S(1)}, f32[136,384]{1,0:T(8,128)S(1)}, f32[128,256]{1,0:T(8,128)S(1)}, f32[32,4096]{1,0:T(8,128)S(1)}, f32[16,...) custom-call(f32[16,128,256]{2,1,0:T(8,128)S(1)} %copy-done.1, ...), custom_call_target="tpu_custom_call" | custom-call | tf_op jit(solution)/shard_map/second_kernel/pallas_call | solution.py:408
  60.9 23.5 %all_to_all.26.g_ref = f32[128,8,128]{2,1,0:T(8,128)S(1)} all-to-all(f32[128,8,128]{2,1,0:T(8,128)S(1)} %get-tuple-element.33), channel_id=1, replica_groups=mesh['row_0'=2,'row_1'=4,'row_2'=2,'col_0'=4,'col_1'=2] {'row_0','row_1'..., dimensions={0} | all-to-all | bytes 1048576 | tf_op jit(solution)/shard_map/all_to_all | solution.py:419
  84.4 6.4 %third_kernel.1 = (f32[16,136,384]{2,1,0:T(8,128)S(1)}, f32[16,128]{1,0:T(8,128)S(1)}, f32[128,8,128]{2,1,0:T(8,128)S(1)}, f32[32,128]{1,0:T(8,128)S(1)}) custom-call(f32[16,136,384]{2,1,0:T(8,128)S(1)} %get-tuple-element.30.v1_ref, f32[136,384]{1,0:T(8,128)S(1)} %get-tuple-element.31.rd_ref, f32[128,256]{1,0:T(8,128)S(1)} %get-tuple-element.32.dg_ref, ...), custom_call_target="tpu_custom_call" | custom-call | tf_op jit(solution)/shard_map/third_kernel/pallas_call | solution.py:408
  90.8 17.8 %all_to_all.27.g_ref = f32[128,8,128]{2,1,0:T(8,128)S(1)} all-to-all(f32[128,8,128]{2,1,0:T(8,128)S(1)} %get-tuple-element.38), channel_id=1, replica_groups=mesh['row_0'=2,'row_1'=4,'row_2'=2,'col_0'=4,'col_1'=2] {'row_0','row_1'..., dimensions={0} | all-to-all | bytes 1048576 | tf_op jit(solution)/shard_map/all_to_all | solution.py:419
  108.6 5.3 %fourth_kernel.1 = f32[128,1,128]{2,1,0:T(1,128)S(1)} custom-call(f32[16,136,384]{2,1,0:T(8,128)S(1)} %get-tuple-element.37.v2_ref, f32[136,384]{1,0:T(8,128)S(1)} %get-tuple-element.31.rd_ref, f32[128,256]{1,0:T(8,128)S(1)} %get-tuple-element.32.dg_ref, f32[136,384]{1,0:T(8,128)S(1)} %copy-done.3, f32[128,8,128]{2,1,0:T(8,128)S(1)} %all_to_all.27.g_ref, ...), custom_call_target="tpu_custom_call" | custom-call | tf_op jit(solution)/shard_map/fourth_kernel/pallas_call | solution.py:408
  113.9 14.5 %all_to_all.28.g_ref = f32[128,1,128]{2,1,0:T(1,128)S(1)} all-to-all(f32[128,1,128]{2,1,0:T(1,128)S(1)} %fourth_kernel.1), channel_id=1, replica_groups=mesh['row_0'=2,'row_1'=4,'row_2'=2,'col_0'=4,'col_1'=2] {'row_0','row_1'..., dimensions={0} | all-to-all | bytes 131072 | tf_op jit(solution)/shard_map/all_to_all | solution.py:419
  128.4 2.3 %last_kernel.1 = (f32[16,128,256]{2,1,0:T(8,128)}, f32[16,32]{1,0:T(8,128)}) custom-call(f32[128,1,128]{2,1,0:T(1,128)S(1)} %all_to_all.28.g_ref, f32[16,128,256]{2,1,0:T(8,128)S(1)} %copy-done.1, f32[136,384]{1,0:T(8,128)S(1)} %get-tuple-element.31.rd_ref, f32[16,136,384]{2,1,0:T(8,128)S(1)} %get-tuple-element.30.v1_ref, ...), custom_call_target="tpu_custom_call" | custom-call | tf_op jit(solution)/shard_map/last_kernel/pallas_call | solution.py:408
  (6 shorter events, 0.0 us)
Async XLA Ops:
  0.6 1.6 %copy-start = (f32[16,128,256]{2,1,0:T(8,128)S(1)}, f32[16,128,256]{2,1,0:T(8,128)}, u32[]{:S(2)}) copy-start(f32[16,128,256]{2,1,0:T(8,128)} %b_ref.5) | copy-start | bytes 6291460
  2.2 0.9 copy-start.6
  3.1 1.0 copy-start.9
  4.2 0.7 copy-start.12
  4.9 0.7 copy-start.14
  5.6 0.7 copy-start.16
  6.3 0.7 copy-start.18
  9.1 0.7 copy-start.2
  9.8 20.8 %copy-start.8 = (f32[128,8,128]{2,1,0:T(8,128)}, f32[128,8,128]{2,1,0:T(8,128)S(1)}, u32[]{:S(2)}) copy-start(f32[128,8,128]{2,1,0:T(8,128)S(1)} %get-tuple-element.28) | copy-start | bytes 1572868
  9.8 20.8 %copy-start.10 = (f32[17,16,256]{2,1,0:T(8,128)}, f32[17,16,256]{2,1,0:T(8,128)S(1)}, u32[]{:S(2)}) copy-start(f32[17,16,256]{2,1,0:T(8,128)S(1)} %get-tuple-element.23.edge_ref) | copy-start | bytes 835588
  9.8 41.3 %copy-start.1 = (f32[16,128,256]{2,1,0:T(8,128)S(1)}, f32[16,128,256]{2,1,0:T(8,128)}, u32[]{:S(2)}) copy-start(f32[16,128,256]{2,1,0:T(8,128)} %b_ref.5) | copy-start | bytes 6291460
  9.8 41.3 %copy-start.7 = (f32[128,256]{1,0:T(8,128)S(1)}, f32[128,256]{1,0:T(8,128)}, u32[]{:S(2)}) copy-start(f32[128,256]{1,0:T(8,128)} %sh_ref.3) | copy-start | bytes 393220
  9.8 41.3 %copy-start.13 = (f32[4096]{0:T(1024)S(1)}, f32[4096]{0:T(1024)}, u32[]{:S(2)}) copy-start(f32[4096]{0:T(1024)} %param.13) | copy-start | bytes 49156
  9.8 41.3 %copy-start.15 = (f32[1,32,32]{2,1,0:T(8,128)S(1)}, f32[1,32,32]{2,1,0:T(8,128)}, u32[]{:S(2)}) copy-start(f32[1,32,32]{2,1,0:T(8,128)} %m_ref.5) | copy-start | bytes 12292
  9.8 41.3 %copy-start.17 = (f32[16,32]{1,0:T(8,128)S(1)}, f32[16,32]{1,0:T(8,128)}, u32[]{:S(2)}) copy-start(f32[16,32]{1,0:T(8,128)} %bp_ref.3) | copy-start | bytes 6148
  30.5 20.5 %all-to-all-start.1 = ((f32[128,8,128]{2,1,0:T(8,128)}), f32[128,8,128]{2,1,0:T(8,128)S(1)}, u32[]{:S(2)}, u32[]{:S(2)}) async-start(f32[128,8,128]{2,1,0:T(8,128)} %copy-done.8), calls=%async_computation.1 | async-start | bytes 1048576 | tf_op jit(solution)/shard_map/all_to_all | solution.py:419
  38.2 1.0 copy-start.11
  40.6 1.0 copy-start.4
  41.6 9.5 %collective-permute-start = (f32[9,8,384]{2,1,0:T(8,128)}, f32[9,8,384]{2,1,0:T(8,128)}, u32[]{:S(2)}, u32[]{:S(2)}) collective-permute-start(f32[9,8,384]{2,1,0:T(8,128)} %get-tuple-element.25), channel_id=1, source_target_pairs={{8,0},{16,8},{24,16},{32,24},{40,32},{48,40},{56,48},{64,56},{72,6... | collective-permute-start | bytes 331784 | tf_op jit(solution)/shard_map/ppermute | solution.py:443
  44.5 6.5 %collective-permute-start.1 = (f32[9,8,384]{2,1,0:T(8,128)}, f32[9,8,384]{2,1,0:T(8,128)}, u32[]{:S(2)}, u32[]{:S(2)}) collective-permute-start(f32[9,8,384]{2,1,0:T(8,128)} %get-tuple-element.26), channel_id=1, source_target_pairs={{0,8},{8,16},{16,24},{24,32},{32,40},{40,48},{48,56},{56,64},{64,7... | collective-permute-start | bytes 331784 | tf_op jit(solution)/shard_map/ppermute | solution.py:444
  51.1 0.9 copy-start.3
  52.0 1.2 copy-start.5

commit v2 on v1

v2 whole, which is shorter than its diff:
```python
import functools

import jax
import jax.numpy as jnp
from jax import lax
from jax.experimental import pallas as pl
from jax.experimental.pallas import tpu as pltpu
from jax.sharding import Mesh
from jax.sharding import PartitionSpec as P

ROW = ("row_0", "row_1", "row_2")
COL = ("col_0", "col_1")
ROW_COL = ("row_0", "row_1", "row_2", "col_0", "col_1")

K = 16
TR, TC = 128, 256
ER, EC = 136, 384
CELL = 32
PLANES = K + 1
PAIRS = 9
HROWS = 56
OWN = 32
NB = 4096
HI = lax.Precision.HIGHEST


def iota(shape, dim):
    return lax.broadcasted_iota(jnp.int32, shape, dim)


def where_am_i():
    i = (lax.axis_index("row_0") * 4 + lax.axis_index("row_1")) * 2 + lax.axis_index("row_2")
    j = lax.axis_index("col_0") * 2 + lax.axis_index("col_1")
    return i, j


def dot_nt(a, b):
    return lax.dot_general(
        a, b, (((1,), (1,)), ((), ())), precision=HI, preferred_element_type=jnp.float32
    )


def dot_nn(a, b):
    return jnp.dot(a, b, precision=HI, preferred_element_type=jnp.float32)


def spread(j):
    group = iota((128, EC), 1) // CELL
    cell = jnp.where(group <= 8, 8 * j + group, jnp.where(group == 11, 8 * j - 1, -5))
    return (iota((128, EC), 0) % 64 == cell).astype(jnp.float32)


def lattice_chunk(l):
    return jnp.clip(l // 2, 0, NB // 128 - 1)


def extended_rows(parts):
    body = [jnp.broadcast_to(p, (CELL, EC)) for p in parts[1:5]]
    edge = jnp.where(iota((8, EC), 0) < 4, parts[5], parts[0])
    return jnp.concatenate(body + [edge], axis=0)


def padded(scr, x):
    scr[...] = jnp.zeros_like(scr)
    scr[:, 0 : x.shape[1]] = x
    return scr[...]


def pack(vp, vd):
    lane = iota((8, 128), 1)
    hi = pltpu.roll(vp[8:16], 32, 1)
    out = jnp.where(lane < 32, vp[0:8], hi)
    out = jnp.where(lane < 64, out, pltpu.roll(vd[0:8], 64, 1))
    return jnp.where(lane < 96, out, pltpu.roll(vd[8:16], 96, 1))


def gather_bumps(s_ref):
    at = iota((4 * TC, 128), 0)
    pick = (at // TC * 8 + at % TC // CELL == iota((4 * TC, 128), 1)).astype(jnp.float32)
    return dot_nn(s_ref[...], pick)


def down_cells(s_ref, k, z):
    for lr in range(4):
        rows = z[CELL * lr : CELL * (lr + 1)]
        s_ref[pl.ds(k, 1), TC * lr : TC * (lr + 1)] = jnp.sum(rows, axis=0, keepdims=True)


SENDS = 8


def send(msg_hbm, pay_ref, sems, pay):
    n = pay_ref.shape[0]
    for d in range(n):
        pay_ref[d] = pay
    copies = [
        pltpu.make_async_copy(pay_ref, msg_hbm.at[n * c : n * (c + 1)], sems.at[c]) for c in range(SENDS)
    ]
    for c in copies:
        c.start()
    for c in copies:
        c.wait()


def load_kernel(mv, b_ref, sh_ref, p_ref, msg_hbm, edge_ref, z_ref, sems):
    _, j = where_am_i()
    lane = iota((TR, 128), 1)
    z = jnp.zeros((TR, 128), jnp.float32)
    mv.wait(1)
    for k in [K] + list(range(K)):
        if k < K and k % 4 == 0:
            mv.wait(0, k // 4)
        src = b_ref.at[k] if k < K else sh_ref
        lo = pltpu.roll(src[:, 0:128], 3 * k, 1) if k else src[:, 0:128]
        up = pltpu.roll(src[:, 128:256], (64 + 3 * k - 125) % 128, 1)
        z = jnp.where((lane >= 3 * k) & (lane < 3 * k + 3), lo, z)
        z = jnp.where((lane >= 64 + 3 * k) & (lane < 67 + 3 * k), up, z)
        edge_ref[k, 0:8, :] = src[0:8, :]
        edge_ref[k, 8:16, :] = src[TR - 8 : TR, :]
    mv.flush(1)
    mv.wait(2)
    rows = [
        pltpu.make_async_copy(
            p_ref.at[:, :, 128 * t : 128 * (t + 1)],
            msg_hbm.at[:, 32 * t : 32 * (t + 1), :],
            sems.at[t],
        )
        for t in range(4)
    ]
    for c in rows:
        c.start()
    z_ref[...] = z.T
    side = lambda at, to, n: pltpu.make_async_copy(
        z_ref.at[at : at + HROWS, :], msg_hbm.at[to, 128 : 128 + HROWS, :], sems.at[n]
    )
    sides = [side(0, jnp.maximum(j - 1, 0), 4), side(64, jnp.minimum(j + 1, 7), 5)]
    for c in sides:
        c.start()
    for c in sides + rows:
        c.wait()


def start_kernel(
    mv, b_ref, sh_ref, bp_ref, m_ref, node_ref, cond_ref,
    msg_hbm, cm_ref, v0p_ref,
    a_ref, s_ref, pad_ref, pay_ref, sems,
):
    i, j = where_am_i()
    for n in (4, 5):
        mv.wait(n)
    a_ref[...] = jnp.zeros_like(a_ref)
    ln = iota((1, 128), 1)
    for lr in range(6):
        l = 4 * i + lr - 1
        chunk = lattice_chunk(l)
        ok = (ln // 64 == l % 2) & (l >= 0) & (l < 64)
        nd = node_ref[pl.ds(chunk, 1), :]
        a_ref[lr : lr + 1, :] = jnp.where(ok, nd // 2048 - CELL * l, 0).astype(jnp.float32)
        a_ref[8 + lr : 9 + lr, :] = jnp.where(ok, nd % 2048 - CELL * (ln % 64), 0).astype(jnp.float32)
        a_ref[16 + lr : 17 + lr, :] = jnp.where(ok, cond_ref[pl.ds(chunk, 1), :], 0.0)
    wide = dot_nn(a_ref[...], spread(j))
    maps = [extended_rows([wide[8 * n + lr : 8 * n + lr + 1] for lr in range(6)]) for n in range(3)]
    row = iota((ER, EC), 0)
    here = jnp.where(row < TR, row % CELL, jnp.where(row < TR + 4, row - TR, row - TR + 24))
    cols = iota((ER, EC), 1) % CELL
    hit = (maps[0].astype(jnp.int32) == here) & (maps[1].astype(jnp.int32) == cols)
    cm = jnp.where(hit, maps[2], 0.0)
    cm_ref[...] = cm
    mv.flush(1)
    mv.wait(1)
    here = cm[0:TR, 0:TC]
    z_scale = jnp.where(here > 0.0, 1.0 / (4.0 + sh_ref[...] + here), 0.0)

    def one(k, c):
        down_cells(s_ref, k, b_ref[k] * z_scale)
        return c

    mv.wait(0)
    lax.fori_loop(0, K, one, 0)
    mv.wait(2)
    mv.wait(3)
    v0p = padded(pad_ref, dot_nt(bp_ref[...], m_ref[0]))
    v0p_ref[...] = v0p
    mv.flush(2)
    send(msg_hbm, pay_ref, sems, pack(v0p, gather_bumps(s_ref)))


def columns_kernel(mv, g1_ref, edge_ref, w_ref, up_ref, dn_ref, y_ref, ext_ref):
    _, j = where_am_i()
    y_ref[...] = jnp.zeros_like(y_ref)

    @pl.when(j < 7)
    def _():
        y_ref[0:HROWS, :] = g1_ref[jnp.minimum(j + 1, 7), 128 : 128 + HROWS, :]

    @pl.when(j > 0)
    def _():
        y_ref[64 : 64 + HROWS, :] = g1_ref[jnp.maximum(j - 1, 0), 128 : 128 + HROWS, :]

    yt = y_ref[...].T
    lane = iota((TR, 128), 1)
    for k in range(PLANES):
        right = pltpu.roll(yt, (128 - 3 * k) % 128, 1) if k else yt
        left = pltpu.roll(yt, (61 - 3 * k) % 128, 1) if (61 - 3 * k) % 128 else yt
        w_ref[k] = jnp.where(lane < 3, right, jnp.where(lane >= 125, left, 0.0))
    first = iota((8, EC), 0) < 4
    mv.wait(1)
    for k in range(PLANES):
        for side in range(2):
            ext_ref[side, k, :, 0:TC] = edge_ref[k, 8 * side : 8 * side + 8, :]
            ext_ref[side, k, :, TC:EC] = w_ref[k, (TR - 8) * side : (TR - 8) * side + 8, :]
    for p in range(PAIRS):
        q = min(p + PAIRS, PLANES - 1)
        up_ref[p] = jnp.where(first, ext_ref[0, p], pltpu.roll(ext_ref[0, q], 4, 0))
        dn_ref[p] = jnp.where(first, pltpu.roll(ext_ref[1, p], 4, 0), ext_ref[1, q])
    mv.flush(0)


def whole_plane(xs_ref, main, w_ref, grp_ref, k):
    xs_ref[0:TR, 0:TC] = main
    xs_ref[0:TR, TC:EC] = w_ref[k]
    xs_ref[TR:ER, :] = grp_ref[k]
    return xs_ref[...]


def package_all(g_ref, v_ref):
    lane = iota((8, 128), 1) // 32

    def one(c, carry):
        lo = jnp.zeros((8, 128), jnp.float32)
        hi = jnp.zeros((8, 128), jnp.float32)
        for m in range(4):
            x = g_ref[4 * c + m]
            lo = jnp.where(lane == m, pltpu.roll(x, 32 * m, 1) if m else x, lo)
            hi = jnp.where(lane == m, pltpu.roll(x, (32 * m - 32) % 128, 1) if m != 1 else x, hi)
        at = pl.ds(pl.multiple_of(128 * c, 128), 128)
        v_ref[0:8, at] = lo
        v_ref[8:16, at] = hi
        return carry

    lax.fori_loop(0, NB // 128, one, 0, unroll=4)


def own_die(g_ref, i, j):
    lane = iota((8, 128), 1)
    halves = []
    for h in range(2):
        out = jnp.zeros((8, 128), jnp.float32)
        for m in range(4):
            x = g_ref[8 * i + 4 * (j % 2) + m]
            shift = 8 * m - (64 + 32 * h + 8 * (j // 2)) + 128
            x = pltpu.roll(x, shift % 128, 1)
            out = jnp.where((lane >= 8 * m) & (lane < 8 * m + 8), x, out)
        halves.append(out)
    return jnp.concatenate(halves, axis=0)


def own_conductance(cond_ref, i, j):
    q = 8 * i + j
    row = cond_ref[pl.ds(q // 4, 1), :]
    return pltpu.roll(row, (128 - 32 * (q % 4)) % 128, 1)


def around(v_ref, x_ref, i):
    ln = iota((K, 128), 1)
    for lr in range(6):
        l = 4 * i + lr - 1
        at = pl.ds(pl.multiple_of(128 * lattice_chunk(l), 128), 128)
        x_ref[K * lr : K * (lr + 1), :] = jnp.where(ln // 64 == l % 2, v_ref[:, at], 0.0)


def coupled(e_ref, k):
    return extended_rows([e_ref[pl.ds(K * lr + k, 1), :] for lr in range(6)])


def beside(x):
    out = pltpu.roll(x, 1, 0) + pltpu.roll(x, ER - 1, 0)
    return out + pltpu.roll(x, 1, 1) + pltpu.roll(x, EC - 1, 1)


def add_dot(r_ref, at, x):
    s = jnp.sum(x, axis=0, keepdims=True)
    r_ref[pl.ds(at, 1), :] = s[:, 0:128] + s[:, 128:256]


def tile(x):
    return x[0:TR, 0:TC]


def prepare_kernel(
    mv, b_ref, sh_ref, w_ref, bot_ref, top_ref, cm_ref, g1_ref,
    grp_ref, bump_ref, rd_ref, dg_ref, cr_ref, pm_ref,
    xs_ref, s_ref,
):
    for d in range(8):
        for t in range(4):
            c = 4 * d + t
            pm_ref[:, 128 * c : 128 * (c + 1)] = g1_ref[d, 32 * t : 32 * (t + 1), :]
    mv.flush(5)
    mv.wait(1)
    mv.wait(5)
    first = iota((8, EC), 0) < 4
    for p in range(PAIRS):
        bot, top = bot_ref[p], top_ref[p]
        grp_ref[p] = jnp.where(first, bot, pltpu.roll(top, 4, 0))
        if p + PAIRS < PLANES:
            grp_ref[p + PAIRS] = jnp.where(first, pltpu.roll(bot, 4, 0), top)
    mv.flush(0)
    mv.wait(2)
    sh = whole_plane(xs_ref, sh_ref[...], w_ref, grp_ref, K)
    cm = cm_ref[...]
    rd = jnp.where(sh > 0.0, 1.0 / (4.0 + sh + cm), 0.0)
    rd_ref[...] = rd
    cr_ref[...] = cm * rd
    dg_ref[...] = 4.0 + tile(sh) + tile(cm)
    for n in (2, 3, 4):
        mv.flush(n)

    def one(k, c):
        rd = rd_ref[...]
        x0 = whole_plane(xs_ref, b_ref[k], w_ref, grp_ref, k) * rd
        pre = x0 - beside(x0) * rd
        down_cells(s_ref, k, jnp.where(tile(cm_ref) > 0.0, tile(pre), 0.0))
        return c

    for c in range(CHUNKS):
        mv.wait(0, c)
        lax.fori_loop(4 * c, 4 * c + 4, one, 0)
    s_ref[K : K + 8, :] = jnp.zeros((8, 4 * TC), jnp.float32)
    down_cells(s_ref, K, tile(cm_ref))
    down_cells(s_ref, K + 1, tile(cr_ref))
    bump_ref[...] = gather_bumps(s_ref)
    mv.flush(1)


def package_kernel(
    step, mv, g_ref, pm_ref, m_ref, cond_ref, bump_ref, const_ref, vp_ref,
    out_ref, vd_ref, y_ref, x_ref, msg_hbm,
    v_ref, pad_ref, pay_ref, sems,
):
    i, j = where_am_i()
    package_all(g_ref, v_ref)
    for n in range(1, 7):
        if n in mv.ins:
            mv.wait(n)
    vp = vp_ref[...]
    y = padded(pad_ref, dot_nt(v_ref[...], pm_ref[...]))
    y = y + own_conductance(cond_ref, i, j) * (vp - own_die(g_ref, i, j))
    y = jnp.where(iota((K, 128), 1) < OWN, y, 0.0)
    out = padded(pad_ref, dot_nt(y[:, 0:OWN], m_ref[0]))
    if step == 2:
        out = out - vp
    vd = bump_ref[0:K, :] - const_ref[K + 1 : K + 2, :] * at_tile(v_ref, i, j)
    y_ref[...] = y
    out_ref[...] = out
    vd_ref[...] = vd
    around(v_ref, x_ref, i)
    for n in range(4):
        mv.flush(n)
    send(msg_hbm, pay_ref, sems, pack(out, vd))


def at_tile(v_ref, i, j):
    ln = iota((K, 128), 1)
    out = jnp.zeros((K, 128), jnp.float32)
    for lr in range(4):
        l = 4 * i + lr
        at = pl.ds(pl.multiple_of(128 * lattice_chunk(l), 128), 128)
        x = pltpu.roll(v_ref[:, at], (8 * lr - 64 * (l % 2) - 8 * j + 256) % 128, 1)
        out = jnp.where((ln >= 8 * lr) & (ln < 8 * lr + 8), x, out)
    return out


def second_kernel(
    mv, b_ref, w_ref, grp_ref, rd_ref, dg_ref, cr_ref, x_ref, bp_ref, v0p_ref, v1p_ref, y1_ref,
    v1_ref, bump_ref, r_ref,
    e_ref, s_ref, pad_ref, xs_ref,
):
    i, j = where_am_i()
    for n in range(1, 11):
        mv.wait(n)
    e_ref[...] = dot_nn(x_ref[...], spread(j))

    def one(k, c):
        rd, dg = rd_ref[...], dg_ref[...]
        x0 = whole_plane(xs_ref, b_ref[k], w_ref, grp_ref, k) * rd
        x1 = x0 - (beside(x0) * rd + cr_ref[...] * coupled(e_ref, k))
        v1_ref[k] = x1
        down_cells(s_ref, k, jnp.where(tile(cr_ref) > 0.0, tile(-beside(x1) * rd), 0.0))
        a, b = tile(x0), tile(x1)
        add_dot(r_ref, k, dg * a * a)
        add_dot(r_ref, K + k, dg * a * b)
        add_dot(r_ref, 2 * K + k, dg * b * b)
        return c

    for c in range(CHUNKS):
        mv.wait(0, c)
        lax.fori_loop(4 * c, 4 * c + 4, one, 0)
        mv.flush(0, c)
    bump_ref[...] = gather_bumps(s_ref)
    v0p, v1p, y1 = v0p_ref[...], v1p_ref[...], y1_ref[...]
    bp = padded(pad_ref, bp_ref[...])
    r_ref[0:K, :] += v0p * bp
    r_ref[K : 2 * K, :] += v0p * y1
    r_ref[2 * K : 3 * K, :] += v1p * y1
    mv.flush(2)


def third_kernel(
    mv, v1_ref, rd_ref, dg_ref, cr_ref, x_ref, wp_ref, y1_ref, y2_ref, ra_ref,
    wt_ref, r_ref,
    e_ref,
):
    i, j = where_am_i()
    for n in range(1, 9):
        mv.wait(n)
    e_ref[...] = dot_nn(x_ref[...], spread(j))
    r_ref[6 * K :, :] = jnp.zeros((2 * K, 128), jnp.float32)
    r_ref[0 : 3 * K, :] = ra_ref[...]

    def one(k, c):
        dg = dg_ref[...]
        x1 = v1_ref[k]
        w = -(beside(x1) * rd_ref[...] + cr_ref[...] * coupled(e_ref, k))
        a, b = tile(x1), tile(w)
        wt_ref[k] = b
        add_dot(r_ref, 3 * K + k, dg * a * b)
        add_dot(r_ref, 4 * K + k, dg * b * b)
        add_dot(r_ref, 5 * K + k, dg * b * (b - tile(beside(w)) * tile(rd_ref)))
        return c

    for c in range(CHUNKS):
        mv.wait(0, c)
        lax.fori_loop(4 * c, 4 * c + 4, one, 0)
        mv.flush(0, c)
    wp, y1, y2 = wp_ref[...], y1_ref[...], y2_ref[...]
    r_ref[3 * K : 4 * K, :] += wp * y1
    r_ref[4 * K : 5 * K, :] += wp * (y2 - y1)


def fourth_kernel(
    mv, g_ref, pm_ref, cond_ref, const_ref, wp_ref, wd_ref, ra_ref,
    msg_ref,
    v_ref, pad_ref, r_ref,
):
    i, j = where_am_i()
    package_all(g_ref, v_ref)
    for n in range(1, 6):
        mv.wait(n)
    wp = wp_ref[...]
    y = padded(pad_ref, dot_nt(v_ref[...], pm_ref[...]))
    y = y + own_conductance(cond_ref, i, j) * (wp - own_die(g_ref, i, j))
    y = jnp.where(iota((K, 128), 1) < OWN, y, 0.0)
    r_ref[...] = ra_ref[...]
    r_ref[5 * K : 6 * K, :] += wp * y - const_ref[K : K + 1, :] * wd_ref[...] * at_tile(v_ref, i, j)
    sums = dot_nt(jnp.ones((8, 128), jnp.float32), r_ref[...])

    def one(d, c):
        msg_ref[d] = sums[0:1]
        return c

    lax.fori_loop(0, msg_ref.shape[0], one, 0, unroll=8)


def last_kernel(
    mv, g_ref, b_ref, rd_ref, v1_ref, v2_ref, v0p_ref, v1p_ref, v2p_ref,
    xd_ref, xp_ref, c_ref,
):
    total = jnp.sum(g_ref[...], axis=0)
    total = jnp.broadcast_to(total, (8, 128))
    m = [pltpu.roll(total, (128 - K * n) % 128, 1) if n else total for n in range(6)]
    g00, g01, g02, g11, g12, g22 = m[1], m[2], m[3], m[2] + m[3], m[3] + m[4], m[5]
    f1, f2 = g01 / g00, g02 / g00
    a11, a12, h1 = g11 - f1 * g01, g12 - f1 * g02, g00 - f1 * m[0]
    a22, h2 = g22 - f2 * g02, g01 - g00 - f2 * m[0]
    f3 = a12 / a11
    c2 = (h2 - f3 * h1) / (a22 - f3 * a12)
    c1 = (h1 - a12 * c2) / a11
    c0 = (m[0] - g01 * c1 - g02 * c2) / g00
    rd = tile(rd_ref)
    at = iota((K, 128), 0) == iota((K, 128), 1)
    cols = []
    for n, c in enumerate((c0, c1, c2)):
        col = jnp.sum(jnp.where(at, c[0:1], 0.0), axis=1, keepdims=True)
        cols.append(col)
        c_ref[n] = jnp.broadcast_to(col, (K, TC))
    xp = cols[0] * v0p_ref[...] + cols[1] * v1p_ref[...] + cols[2] * v2p_ref[...]
    xp_ref[...] = xp[:, 0:OWN]

    def one(k, carry):
        c0, c1, c2 = (c_ref[n, pl.ds(k, 1), :] for n in range(3))
        xd_ref[k] = (c0 * b_ref[k]) * rd + c1 * tile(v1_ref.at[k]) + c2 * v2_ref[k]
        return carry

    lax.fori_loop(0, K, one, 0)


def f32(*shape):
    return jax.ShapeDtypeStruct(shape, jnp.float32)


def vm(*shape):
    return pltpu.VMEM(shape, jnp.float32)


CHUNKS = 4


class Moves:
    def __init__(self):
        self.ins, self.outs, self.pending = {}, {}, []

    def wait(self, n, chunk=None):
        for c in [chunk] if chunk is not None else range(len(self.ins[n])):
            self.ins[n][c].wait()
            self.ins[n][c] = None

    def flush(self, n, chunk=None):
        for c in [chunk] if chunk is not None else range(len(self.outs[n])):
            self.outs[n][c].start()
            self.pending.append(self.outs[n][c])


def parts(ref, mode):
    if mode == "h":
        return [ref]
    step = ref.shape[0] // CHUNKS
    return [ref.at[step * c : step * (c + 1)] for c in range(CHUNKS)]


def call(kernel, ins, outs, scratch, limit=14, **kw):
    imode, omode = [m for _, m in ins], [m for _, m in outs]
    moved = [jax.ShapeDtypeStruct(x.shape, x.dtype) for x, m in ins + outs if m in "hc"]
    count = sum({"h": 1, "c": CHUNKS}.get(m, 0) for m in imode + omode)

    def wrapped(*refs):
        ni, no, nm = len(ins), len(outs), len(moved)
        hbm, bufs, sems, own = refs[: ni + no], list(refs[ni + no :][:nm]), refs[ni + no + nm], refs[ni + no + nm + 1 :]
        mv, given, sem = Moves(), [], 0
        for n, (ref, mode) in enumerate(zip(hbm, imode + omode)):
            if mode not in "hc":
                given.append(ref)
                continue
            buf = bufs.pop(0)
            given.append(buf)
            copies = []
            for x, y in zip(parts(ref, mode), parts(buf, mode)):
                x, y = (x, y) if n < ni else (y, x)
                copies.append(pltpu.make_async_copy(x, y, sems.at[sem]))
                sem += 1
            (mv.ins if n < ni else mv.outs)[n if n < ni else n - ni] = copies
        for copies in sorted(mv.ins.values(), key=len):
            for c in copies:
                c.start()
        kernel(mv, *given, *own)
        for copies in mv.ins.values():
            assert all(c is None for c in copies)
        for c in mv.pending:
            c.wait()

    space = lambda m: pl.BlockSpec(memory_space=pltpu.VMEM if m == "v" else pltpu.HBM)
    return pl.pallas_call(
        wrapped,
        out_shape=tuple(x if m == "v" else pltpu.HBM(x.shape, x.dtype) for x, m in outs),
        in_specs=[space(m) for m in imode],
        out_specs=tuple(space(m) for m in omode),
        scratch_shapes=[pltpu.VMEM(x.shape, x.dtype) for x in moved]
        + [pltpu.SemaphoreType.DMA((max(count, 1),))] + scratch,
        compiler_params=pltpu.CompilerParams(vmem_limit_bytes=limit << 20),
        name=getattr(kernel, "func", kernel).__name__,
        **kw,
    )(*[x if m == "v" else pltpu.with_memory_space_constraint(x, pltpu.HBM) for x, m in ins])


def swapped(x, axes):
    return lax.all_to_all(x, axes, 0, 0, tiled=True)


def body(
    die_current, die_shunt, pkg_current, pkg_matrix, pkg_block_inv, bump_node, bump_conductance
):
    nodes = bump_node.reshape(NB // 128, 128)
    cond = bump_conductance.reshape(NB // 128, 128)
    b, sh, bp, m = die_current, die_shunt, pkg_current, pkg_block_inv
    gathered, small, ext, die = f32(128, 8, 128), f32(K, 128), f32(K, ER, EC), f32(K, TR, TC)
    lattice = f32(6 * K, 128)
    payload = [vm(128 // SENDS, 8, 128), pltpu.SemaphoreType.DMA((SENDS,))]
    msg1, edge = call(
        load_kernel,
        [(b, "c"), (sh, "h"), (pkg_matrix.reshape(8, OWN, 512), "h")],
        [(f32(8, 128 + HROWS, 128), "r"), (f32(PLANES, 16, TC), "h")],
        [vm(128, 128), pltpu.SemaphoreType.DMA((6,))],
    )
    g1 = swapped(msg1, COL)
    msg, cm, v0p = call(
        start_kernel,
        [(b, "h"), (sh, "h"), (bp, "h"), (m, "h"), (nodes, "h"), (cond, "h")],
        [(gathered, "r"), (f32(ER, EC), "h"), (small, "h")],
        [vm(24, 128), vm(K, 4 * TC), vm(K, 128)] + payload,
    )
    g = swapped(msg, ROW_COL)
    side, up, dn = call(
        columns_kernel,
        [(g1, "v"), (edge, "h")],
        [(f32(PLANES, TR, 128), "h"), (f32(PAIRS, 8, EC), "v"), (f32(PAIRS, 8, EC), "v")],
        [vm(128, 128), vm(2, PLANES, 8, EC)],
    )
    n = lax.axis_size(ROW)
    bot = lax.ppermute(up, ROW, [(r + 1, r) for r in range(n - 1)])
    top = lax.ppermute(dn, ROW, [(r, r + 1) for r in range(n - 1)])
    grp, bump1, rd, dg, cr, pm = call(
        prepare_kernel,
        [(b, "c"), (sh, "h"), (side, "h"), (bot, "v"), (top, "v"), (cm, "h"), (g1, "v")],
        [
            (f32(PLANES, 8, EC), "h"), (f32(K + 8, 128), "h"), (f32(ER, EC), "h"),
            (f32(TR, TC), "h"), (f32(ER, EC), "h"), (f32(OWN, NB), "h"),
        ],
        [vm(ER, EC), vm(K + 8, 4 * TC)],
    )
    step = [vm(K, NB), vm(K, 128)] + payload
    results = [(small, "h"), (small, "h"), (small, "h"), (lattice, "h"), (gathered, "r")]
    v1p, _, y1, near, msg = call(
        functools.partial(package_kernel, 1),
        [(g, "v"), (pm, "h"), (m, "h"), (cond, "h"), (bump1, "h"), (bump1, "h"), (v0p, "h")],
        results,
        step,
    )
    g = swapped(msg, ROW_COL)
    v1, bump2, r = call(
        second_kernel,
        [(b, "c")] + [(x, "h") for x in (side, grp, rd, dg, cr, near, bp, v0p, v1p, y1)],
        [(ext, "c"), (small, "v"), (f32(3 * K, 128), "h")],
        [vm(6 * K, EC), vm(K, 4 * TC), vm(K, 128), vm(ER, EC)],
    )
    wp, wd, y2, near, msg = call(
        functools.partial(package_kernel, 2),
        [(g, "v"), (pm, "h"), (m, "h"), (cond, "h"), (bump2, "v"), (bump1, "h"), (v1p, "h")],
        results,
        step,
    )
    g = swapped(msg, ROW_COL)
    w, r = call(
        third_kernel,
        [(v1, "c")] + [(x, "h") for x in (rd, dg, cr, near, wp, y1, y2, r)],
        [(die, "c"), (f32(128, 128), "v")],
        [vm(6 * K, EC)],
    )
    (msg,) = call(
        fourth_kernel,
        [(g, "v")] + [(x, "h") for x in (pm, cond, bump1, wp, wd)] + [(r, "v")],
        [(f32(128, 1, 128), "v")],
        [vm(K, NB), vm(K, 128), vm(128, 128)],
    )
    g = swapped(msg, ROW_COL)
    return call(
        last_kernel,
        [(x, "v") for x in (g, b, rd, v1, w, v0p, v1p, wp)],
        [(die, "v"), (f32(K, OWN), "v")],
        [vm(3, K, TC)],
    )


def solution(mesh):
    torus = Mesh(mesh.devices.reshape(2, 4, 2, 4, 2), ROW_COL)
    placed = (
        P(None, ROW, COL),
        P(ROW, COL),
        P(None, ROW_COL),
        P(ROW, COL),
        P(ROW_COL, None, None),
        P(),
        P(),
    )
    return jax.shard_map(
        body,
        mesh=torus,
        in_specs=placed,
        out_specs=(P(None, ROW, COL), P(None, ROW_COL)),
        check_vma=False,
    )
```

time: 131 us -> 120 us (0.916)
  blocking collectives: 76.5 us -> 14.5 us
  starting transfers between devices: 13.3 us -> 39 us
  waiting for transfers between devices: 3.87 us -> 20.4 us
  Pallas kernels: 25 us -> 41.1 us
  local copies, waits for them, and re-layouts: 11.2 us -> 3.55 us
    all_to_all x4 -> x1, blocking collectives: 76.5 us -> 14.5 us  [swapped(): return lax.all_to_all(x, axes, 0, 0, tiled=True)]
    all_to_all x1 -> x4, starting transfers between devices: 7.71 us -> 33.4 us  [swapped(): return lax.all_to_all(x, axes, 0, 0, tiled=True)]
    pallas_call x6 -> x10, Pallas kernels: 25 us -> 41.1 us  [call(): pl.pallas_call(wrapped, out_shape=tuple((x if m == 'v' else pltpu.HBM(x.s...]
    all_to_all x1 -> x4, waiting for transfers between devices: 3.87 us -> 18.1 us  [swapped(): return lax.all_to_all(x, axes, 0, 0, tiled=True)]
    unnamed x38 -> x14, local copies, waits for them, and re-layouts: 11.2 us -> 3.55 us
    ppermute x1, waiting for transfers between devices: 0.01 us -> 2.16 us  [body(): bot = lax.ppermute(up, ROW, [(r + 1, r) for r in range(n - 1)])]
  transfers between devices with their start and end apart: 3 -> 6, of which waited for: 1 -> 5; matrix products, arithmetic and copies ran while one was open for 0% -> 0% of each run, Pallas kernels for 1% -> 24%
where the time goes in v2:
time: 120 us; the launch traced here: 119 us
  Pallas kernels  41.1 us (34%)
  starting transfers between devices  39 us (32%)
  waiting for transfers between devices  20.4 us (17%)
  blocking collectives  14.5 us (12%)
  local copies, waits for them, and re-layouts  3.55 us (3%)
    pallas_call x10, Pallas kernels, call(): pl.pallas_call(wrapped, out_shape=tuple((x if m == 'v' else pltpu.HBM(x.s...  41.1 us
    all_to_all x4, starting transfers between devices, swapped(): return lax.all_to_all(x, axes, 0, 0, tiled=True)  33.4 us
    all_to_all x4, waiting for transfers between devices, swapped(): return lax.all_to_all(x, axes, 0, 0, tiled=True)  18.1 us
    all_to_all x1, blocking collectives, swapped(): return lax.all_to_all(x, axes, 0, 0, tiled=True)  14.5 us
    unnamed x14, local copies, waits for them, and re-layouts  3.55 us
    ppermute x1, starting transfers between devices, body(): bot = lax.ppermute(up, ROW, [(r + 1, r) for r in range(n - 1)])  2.98 us
    ppermute x1, starting transfers between devices, body(): top = lax.ppermute(dn, ROW, [(r, r + 1) for r in range(n - 1)])  2.61 us
  transfers between devices with their start and end apart: 6, of which 5 were waited for; matrix products, arithmetic and copies ran while one was open for 0% of the time, Pallas kernels for 24%

profile of v2, /device:TPU:1, one launch (start us, length us, event | category | flops | bytes accessed | tf_op | source)
XLA Modules:
  0.0 119.3 jit_solution(2707529551487198050)
XLA Ops:
  0.6 3.0 %load_kernel.1 = (f32[8,184,128]{2,1,0:T(8,128)}, f32[17,16,256]{2,1,0:T(8,128)}) custom-call(f32[16,128,256]{2,1,0:T(8,128)} %refs_1_.7, f32[128,256]{1,0:T(8,128)} %refs_1_.6, f32[8,32,512]{2,1,0:T(8,128)} %bitcast.3), custom_call_target="tpu_custom_call" | custom-call | tf_op jit(solution)/shard_map/load_kernel/pallas_call | solution.py:562
  3.6 7.5 %all-to-all-start.1 = ((f32[8,184,128]{2,1,0:T(8,128)}), f32[8,184,128]{2,1,0:T(8,128)S(1)}, u32[]{:S(2)}, u32[]{:S(2)}) async-start(f32[8,184,128]{2,1,0:T(8,128)} %get-tuple-element.31), calls=%async_computation.1 | async-start | bytes 1507328 | tf_op jit(solution)/shard_map/all_to_all | solution.py:576
  11.1 3.6 %start_kernel.1 = (f32[128,8,128]{2,1,0:T(8,128)}, f32[136,384]{1,0:T(8,128)}, f32[16,128]{1,0:T(8,128)}) custom-call(f32[16,128,256]{2,1,0:T(8,128)} %refs_1_.7, f32[128,256]{1,0:T(8,128)} %refs_1_.6, f32[16,32]{1,0:T(8,128)} %refs_7_.1, f32[1,32,32]{2,1,0:T(8,128)} %refs_2_.5, s32[32,128]{1,0:T(8,128)} %bitcast.8, f32[32,128]{1,0:T(8,128)} %bitcast.4), custom_call_target="tpu_custom_call" | custom-call | tf_op jit(solution)/shard_map/start_kernel/pallas_call | solution.py:562
  14.7 9.3 %all-to-all-done.1.refs_0_.refs_6_ = f32[8,184,128]{2,1,0:T(8,128)S(1)} async-done(((f32[8,184,128]{2,1,0:T(8,128)}), f32[8,184,128]{2,1,0:T(8,128)S(1)}, u32[]{:S(2)}, u32[]{:S(2)}) %all-to-all-start.1) | async-done | bytes 753696 | tf_op jit(solution)/shard_map/all_to_all | solution.py:576
  24.0 7.9 %all-to-all-start = ((f32[128,8,128]{2,1,0:T(8,128)}), f32[128,8,128]{2,1,0:T(8,128)S(1)}, u32[]{:S(2)}, u32[]{:S(2)}) async-start(f32[128,8,128]{2,1,0:T(8,128)} %get-tuple-element.30), calls=%async_computation | async-start | bytes 1048576 | tf_op jit(solution)/shard_map/all_to_all | solution.py:576
  31.9 2.0 %columns_kernel.1 = (f32[17,128,128]{2,1,0:T(8,128)}, f32[9,8,384]{2,1,0:T(8,128)S(1)}, f32[9,8,384]{2,1,0:T(8,128)S(1)}) custom-call(f32[8,184,128]{2,1,0:T(8,128)S(1)} %all-to-all-done.1.refs_0_.refs_6_, f32[17,16,256]{2,1,0:T(8,128)} %get-tuple-element.32.refs_1_), custom_call_target="tpu_custom_call" | custom-call | tf_op jit(solution)/shard_map/columns_kernel/pallas_call | solution.py:562
  33.9 3.0 %collective-permute-start = (f32[9,8,384]{2,1,0:T(8,128)S(1)}, f32[9,8,384]{2,1,0:T(8,128)S(1)}, u32[]{:S(2)}, u32[]{:S(2)}) collective-permute-start(f32[9,8,384]{2,1,0:T(8,128)S(1)} %get-tuple-element.34), channel_id=1, source_target_pairs={{8,0},{16,8},{24,16},{32,24},{40,32},{48,40},{56,48},{64,56},{72,6... | collective-permute-start | bytes 331784 | tf_op jit(solution)/shard_map/ppermute | solution.py:609
  36.9 2.6 %collective-permute-start.1 = (f32[9,8,384]{2,1,0:T(8,128)S(1)}, f32[9,8,384]{2,1,0:T(8,128)S(1)}, u32[]{:S(2)}, u32[]{:S(2)}) collective-permute-start(f32[9,8,384]{2,1,0:T(8,128)S(1)} %get-tuple-element.35), channel_id=1, source_target_pairs={{0,8},{8,16},{16,24},{24,32},{32,40},{40,48},{48,56},{56,64},{64,7... | collective-permute-start | bytes 331784 | tf_op jit(solution)/shard_map/ppermute | solution.py:610
  39.5 2.2 %collective-permute-done.refs_3_ = f32[9,8,384]{2,1,0:T(8,128)S(1)} collective-permute-done((f32[9,8,384]{2,1,0:T(8,128)S(1)}, f32[9,8,384]{2,1,0:T(8,128)S(1)}, u32[]{:S(2)}, u32[]{:S(2)}) %collective-permute-start) | collective-permute-done | bytes 110624 | tf_op jit(solution)/shard_map/ppermute | solution.py:609
  41.7 0.2 collective-permute-done.1.refs_4_
  41.8 5.9 %prepare_kernel.1 = (f32[17,8,384]{2,1,0:T(8,128)}, f32[24,128]{1,0:T(8,128)}, f32[136,384]{1,0:T(8,128)}, f32[128,256]{1,0:T(8,128)}, f32[136,384]{1,0:T(8,128)}, /*index=5*/f32[32,4096]{1,0:T(8,128)}) custom-call(f32[16,128,256]{2,1,0:T(8,128)} %refs_1_.7, f32[128,256]{1,0:T(8,128)} %refs_1_.6, f32[17,128,128]{2,1,0:T(8,128)} %get-tuple-element.33.refs_2_.refs_1_, ...), custom_call_target="tpu_custom_call" | custom-call | tf_op jit(solution)/shard_map/prepare_kernel/pallas_call | solution.py:562
  47.7 0.0 all-to-all-done.refs_0_
  47.7 2.8 %package_kernel.2 = (f32[16,128]{1,0:T(8,128)}, f32[16,128]{1,0:T(8,128)}, f32[16,128]{1,0:T(8,128)}, f32[96,128]{1,0:T(8,128)}, f32[128,8,128]{2,1,0:T(8,128)}) custom-call(f32[128,8,128]{2,1,0:T(8,128)S(1)} %all-to-all-done.refs_0_, f32[32,4096]{1,0:T(8,128)} %get-tuple-element.37.refs_1_, f32[1,32,32]{2,1,0:T(8,128)} %refs_2_.5, f32[32,128]{1,0:T(8,128)} %bitcast.5, ...), custom_call_target="tpu_custom_call" | custom-call | tf_op jit(solution)/shard_map/package_kernel/pallas_call | solution.py:562
  50.6 12.2 %all-to-all-start.2 = ((f32[128,8,128]{2,1,0:T(8,128)}), f32[128,8,128]{2,1,0:T(8,128)S(1)}, u32[]{:S(2)}, u32[]{:S(2)}) async-start(f32[128,8,128]{2,1,0:T(8,128)} %get-tuple-element.40), calls=%async_computation.2 | async-start | bytes 1048576 | tf_op jit(solution)/shard_map/all_to_all | solution.py:576
  62.8 8.8 %second_kernel.1 = (f32[16,136,384]{2,1,0:T(8,128)}, f32[16,128]{1,0:T(8,128)S(1)}, f32[48,128]{1,0:T(8,128)}) custom-call(f32[16,128,256]{2,1,0:T(8,128)} %refs_1_.7, f32[17,128,128]{2,1,0:T(8,128)} %get-tuple-element.33.refs_2_.refs_1_, f32[17,8,384]{2,1,0:T(8,128)} %get-tuple-element.41.refs_2_, f32[136,384]{1,0:T(8,128)} %get-tuple-element.42.refs_3_.refs_1_.refs_2_, ...), custom_call_target="tpu_custom_call" | custom-call | tf_op jit(solution)/shard_map/second_kernel/pallas_call | solution.py:562
  71.6 4.0 %all-to-all-done.2.refs_0_ = f32[128,8,128]{2,1,0:T(8,128)S(1)} async-done(((f32[128,8,128]{2,1,0:T(8,128)}), f32[128,8,128]{2,1,0:T(8,128)S(1)}, u32[]{:S(2)}, u32[]{:S(2)}) %all-to-all-start.2) | async-done | bytes 524320 | tf_op jit(solution)/shard_map/all_to_all | solution.py:576
  75.6 2.8 %package_kernel.3 = (f32[16,128]{1,0:T(8,128)}, f32[16,128]{1,0:T(8,128)}, f32[16,128]{1,0:T(8,128)}, f32[96,128]{1,0:T(8,128)}, f32[128,8,128]{2,1,0:T(8,128)}) custom-call(f32[128,8,128]{2,1,0:T(8,128)S(1)} %all-to-all-done.2.refs_0_, f32[32,4096]{1,0:T(8,128)} %get-tuple-element.37.refs_1_, f32[1,32,32]{2,1,0:T(8,128)} %refs_2_.5, f32[32,128]{1,0:T(8,128)} %bitcast.6, ...), custom_call_target="tpu_custom_call" | custom-call | tf_op jit(solution)/shard_map/package_kernel/pallas_call | solution.py:562
  78.4 5.8 %all-to-all-start.3 = ((f32[128,8,128]{2,1,0:T(8,128)}), f32[128,8,128]{2,1,0:T(8,128)S(1)}, u32[]{:S(2)}, u32[]{:S(2)}) async-start(f32[128,8,128]{2,1,0:T(8,128)} %get-tuple-element.49), calls=%async_computation.3 | async-start | bytes 1048576 | tf_op jit(solution)/shard_map/all_to_all | solution.py:576
  84.2 0.0 copy-start
  84.2 0.0 copy-start.3
  84.2 0.0 copy-start.4
  84.2 0.0 copy-start.5
  84.3 0.0 copy-start.6
  84.3 7.9 %third_kernel.1 = (f32[16,128,256]{2,1,0:T(8,128)}, f32[128,128]{1,0:T(8,128)S(1)}) custom-call(f32[16,136,384]{2,1,0:T(8,128)} %get-tuple-element.52.refs_0_.refs_3_, f32[136,384]{1,0:T(8,128)} %get-tuple-element.42.refs_3_.refs_1_.refs_2_, f32[128,256]{1,0:T(8,128)} %get-tuple-element.43.refs_4_.refs_2_, f32[136,384]{1,0:T(8,128)} %get-tuple-element.44.refs_5_.refs_3_, ...), custom_call_target="tpu_custom_call" | custom-call | tf_op jit(solution)/shard_map/third_kernel/pallas_call | solution.py:562
  92.2 4.8 %all-to-all-done.3.refs_0_ = f32[128,8,128]{2,1,0:T(8,128)S(1)} async-done(((f32[128,8,128]{2,1,0:T(8,128)}), f32[128,8,128]{2,1,0:T(8,128)S(1)}, u32[]{:S(2)}, u32[]{:S(2)}) %all-to-all-start.3) | async-done | bytes 524320 | tf_op jit(solution)/shard_map/all_to_all | solution.py:576
  97.0 2.1 %fourth_kernel.1 = f32[128,1,128]{2,1,0:T(1,128)S(1)} custom-call(f32[128,8,128]{2,1,0:T(8,128)S(1)} %all-to-all-done.3.refs_0_, f32[32,4096]{1,0:T(8,128)} %get-tuple-element.37.refs_1_, f32[32,128]{1,0:T(8,128)} %bitcast.7, f32[24,128]{1,0:T(8,128)} %get-tuple-element.38.refs_4_.refs_5_.refs_3_, f32[16,128]{1,0:T(8,128)} %get-tuple-element.50.refs_5_.refs_4_.refs_7_, ...), custom_call_target="tpu_custom_call" | custom-call | tf_op jit(solution)/shard_map/fourth_kernel/pallas_call | solution.py:562
  99.1 14.5 %all_to_all.25.refs_0_ = f32[128,1,128]{2,1,0:T(1,128)S(1)} all-to-all(f32[128,1,128]{2,1,0:T(1,128)S(1)} %fourth_kernel.1), channel_id=1, replica_groups=mesh['row_0'=2,'row_1'=4,'row_2'=2,'col_0'=4,'col_1'=2] {'row_0','row_1'..., dimensions={0} | all-to-all | bytes 131072 | tf_op jit(solution)/shard_map/all_to_all | solution.py:576
  113.6 0.0 copy-done
  113.6 0.0 copy-done.3
  113.6 0.0 copy-done.4
  113.6 0.0 copy-done.5
  113.6 0.0 copy-done.6
  113.6 0.0 copy-start.1
  113.6 1.9 %copy-done.1 = f32[16,136,384]{2,1,0:T(8,128)S(1)} copy-done((f32[16,136,384]{2,1,0:T(8,128)S(1)}, f32[16,136,384]{2,1,0:T(8,128)}, u32[]{:S(2)}) %copy-start.1) | copy-done | bytes 3342360
  115.5 0.0 copy-start.2
  115.5 1.6 %copy-done.2 = f32[16,128,256]{2,1,0:T(8,128)S(1)} copy-done((f32[16,128,256]{2,1,0:T(8,128)S(1)}, f32[16,128,256]{2,1,0:T(8,128)}, u32[]{:S(2)}) %copy-start.2) | copy-done | bytes 2097176
  117.1 2.2 %last_kernel.1 = (f32[16,128,256]{2,1,0:T(8,128)}, f32[16,32]{1,0:T(8,128)}) custom-call(f32[128,1,128]{2,1,0:T(1,128)S(1)} %all_to_all.25.refs_0_, f32[16,128,256]{2,1,0:T(8,128)S(1)} %copy-done, f32[136,384]{1,0:T(8,128)S(1)} %copy-done.3, f32[16,136,384]{2,1,0:T(8,128)S(1)} %copy-done.1, f32[16,128,256]{2,1,0:T(8,128)S(1)} %copy-done.2, ...), custom_call_target="tpu_custom_call" | custom-call | tf_op jit(solution)/shard_map/last_kernel/pallas_call | solution.py:562
Async XLA Ops:
  3.6 20.4 %all-to-all-start.1 = ((f32[8,184,128]{2,1,0:T(8,128)}), f32[8,184,128]{2,1,0:T(8,128)S(1)}, u32[]{:S(2)}, u32[]{:S(2)}) async-start(f32[8,184,128]{2,1,0:T(8,128)} %get-tuple-element.31), calls=%async_computation.1 | async-start | bytes 1507328 | tf_op jit(solution)/shard_map/all_to_all | solution.py:576
  24.0 23.7 %all-to-all-start = ((f32[128,8,128]{2,1,0:T(8,128)}), f32[128,8,128]{2,1,0:T(8,128)S(1)}, u32[]{:S(2)}, u32[]{:S(2)}) async-start(f32[128,8,128]{2,1,0:T(8,128)} %get-tuple-element.30), calls=%async_computation | async-start | bytes 1048576 | tf_op jit(solution)/shard_map/all_to_all | solution.py:576
  33.9 7.8 %collective-permute-start = (f32[9,8,384]{2,1,0:T(8,128)S(1)}, f32[9,8,384]{2,1,0:T(8,128)S(1)}, u32[]{:S(2)}, u32[]{:S(2)}) collective-permute-start(f32[9,8,384]{2,1,0:T(8,128)S(1)} %get-tuple-element.34), channel_id=1, source_target_pairs={{8,0},{16,8},{24,16},{32,24},{40,32},{48,40},{56,48},{64,56},{72,6... | collective-permute-start | bytes 331784 | tf_op jit(solution)/shard_map/ppermute | solution.py:609
  36.9 4.9 %collective-permute-start.1 = (f32[9,8,384]{2,1,0:T(8,128)S(1)}, f32[9,8,384]{2,1,0:T(8,128)S(1)}, u32[]{:S(2)}, u32[]{:S(2)}) collective-permute-start(f32[9,8,384]{2,1,0:T(8,128)S(1)} %get-tuple-element.35), channel_id=1, source_target_pairs={{0,8},{8,16},{16,24},{24,32},{32,40},{40,48},{48,56},{56,64},{64,7... | collective-permute-start | bytes 331784 | tf_op jit(solution)/shard_map/ppermute | solution.py:610
  50.6 25.0 %all-to-all-start.2 = ((f32[128,8,128]{2,1,0:T(8,128)}), f32[128,8,128]{2,1,0:T(8,128)S(1)}, u32[]{:S(2)}, u32[]{:S(2)}) async-start(f32[128,8,128]{2,1,0:T(8,128)} %get-tuple-element.40), calls=%async_computation.2 | async-start | bytes 1048576 | tf_op jit(solution)/shard_map/all_to_all | solution.py:576
  78.4 18.6 %all-to-all-start.3 = ((f32[128,8,128]{2,1,0:T(8,128)}), f32[128,8,128]{2,1,0:T(8,128)S(1)}, u32[]{:S(2)}, u32[]{:S(2)}) async-start(f32[128,8,128]{2,1,0:T(8,128)} %get-tuple-element.49), calls=%async_computation.3 | async-start | bytes 1048576 | tf_op jit(solution)/shard_map/all_to_all | solution.py:576
  84.2 29.3 %copy-start = (f32[16,128,256]{2,1,0:T(8,128)S(1)}, f32[16,128,256]{2,1,0:T(8,128)}, u32[]{:S(2)}) copy-start(f32[16,128,256]{2,1,0:T(8,128)} %refs_1_.7) | copy-start | bytes 6291460
  84.2 29.3 %copy-start.3 = (f32[136,384]{1,0:T(8,128)S(1)}, f32[136,384]{1,0:T(8,128)}, u32[]{:S(2)}) copy-start(f32[136,384]{1,0:T(8,128)} %get-tuple-element.42.refs_3_.refs_1_.refs_2_) | copy-start | bytes 626692
  84.2 29.3 %copy-start.4 = (f32[16,128]{1,0:T(8,128)S(1)}, f32[16,128]{1,0:T(8,128)}, u32[]{:S(2)}) copy-start(f32[16,128]{1,0:T(8,128)} %get-tuple-element.39.refs_6_.refs_8_.refs_5_) | copy-start | bytes 24580
  84.2 29.3 %copy-start.5 = (f32[16,128]{1,0:T(8,128)S(1)}, f32[16,128]{1,0:T(8,128)}, u32[]{:S(2)}) copy-start(f32[16,128]{1,0:T(8,128)} %get-tuple-element.46.refs_9_.refs_6_) | copy-start | bytes 24580
  84.3 29.3 %copy-start.6 = (f32[16,128]{1,0:T(8,128)S(1)}, f32[16,128]{1,0:T(8,128)}, u32[]{:S(2)}) copy-start(f32[16,128]{1,0:T(8,128)} %get-tuple-element.50.refs_5_.refs_4_.refs_7_) | copy-start | bytes 24580
  113.6 1.9 %copy-start.1 = (f32[16,136,384]{2,1,0:T(8,128)S(1)}, f32[16,136,384]{2,1,0:T(8,128)}, u32[]{:S(2)}) copy-start(f32[16,136,384]{2,1,0:T(8,128)} %get-tuple-element.52.refs_0_.refs_3_) | copy-start | bytes 10027012
  115.5 1.6 %copy-start.2 = (f32[16,128,256]{2,1,0:T(8,128)S(1)}, f32[16,128,256]{2,1,0:T(8,128)}, u32[]{:S(2)}) copy-start(f32[16,128,256]{2,1,0:T(8,128)} %get-tuple-element.57.refs_4_) | copy-start | bytes 6291460

commit v3 on v2

--- a/solution.py
+++ b/solution.py
@@ -142,8 +142,8 @@
 
 def start_kernel(
     mv, b_ref, sh_ref, bp_ref, m_ref, node_ref, cond_ref,
-    msg_hbm, cm_ref, v0p_ref,
-    a_ref, s_ref, pad_ref, pay_ref, sems,
+    msg_hbm, cm_ref, v0p_ref, bump_ref,
+    a_ref, s_ref, t_ref, w_ref, pad_ref, pay_ref, sems,
 ):
     i, j = where_am_i()
     for n in (4, 5):
@@ -169,14 +169,30 @@
     mv.flush(1)
     mv.wait(1)
     here = cm[0:TR, 0:TC]
-    z_scale = jnp.where(here > 0.0, 1.0 / (4.0 + sh_ref[...] + here), 0.0)
+    rd = 1.0 / (4.0 + sh_ref[...] + here)
+    at_bump = jnp.where(here > 0.0, rd, 0.0)
+    row, col = iota((TR, TC), 0), iota((TR, TC), 1)
+    w_ref[0] = rd
+    w_ref[1] = at_bump
+    for n, inside in enumerate((row > 0, row < TR - 1, col > 0, col < TC - 1)):
+        w_ref[2 + n] = jnp.where(inside, at_bump, 0.0)
 
     def one(k, c):
-        down_cells(s_ref, k, b_ref[k] * z_scale)
+        x = b_ref[k] * w_ref[0]
+        at = b_ref[k] * w_ref[1]
+        down_cells(s_ref, k, at)
+        near = pltpu.roll(x, 1, 0) * w_ref[2] + pltpu.roll(x, TR - 1, 0) * w_ref[3]
+        near = near + pltpu.roll(x, 1, 1) * w_ref[4] + pltpu.roll(x, TC - 1, 1) * w_ref[5]
+        down_cells(t_ref, k, at - near)
         return c
 
     mv.wait(0)
     lax.fori_loop(0, K, one, 0)
+    t_ref[K : K + 8, :] = jnp.zeros((8, 4 * TC), jnp.float32)
+    down_cells(t_ref, K, here)
+    down_cells(t_ref, K + 1, here * rd)
+    bump_ref[...] = gather_bumps(t_ref)
+    mv.flush(3)
     mv.wait(2)
     mv.wait(3)
     v0p = padded(pad_ref, dot_nt(bp_ref[...], m_ref[0]))
@@ -213,7 +229,6 @@
         q = min(p + PAIRS, PLANES - 1)
         up_ref[p] = jnp.where(first, ext_ref[0, p], pltpu.roll(ext_ref[0, q], 4, 0))
         dn_ref[p] = jnp.where(first, pltpu.roll(ext_ref[1, p], 4, 0), ext_ref[1, q])
-    mv.flush(0)
 
 
 def whole_plane(xs_ref, main, w_ref, grp_ref, k):
@@ -287,50 +302,54 @@
     return x[0:TR, 0:TC]
 
 
-def prepare_kernel(
-    mv, b_ref, sh_ref, w_ref, bot_ref, top_ref, cm_ref, g1_ref,
-    grp_ref, bump_ref, rd_ref, dg_ref, cr_ref, pm_ref,
-    xs_ref, s_ref,
+def edges_kernel(
+    mv, sh_ref, w_ref, bot_ref, top_ref, cm_ref, g1_ref, inner_ref,
+    w_hbm, grp_ref, bump_ref, pm_ref,
+    s_ref, t_ref, sem,
 ):
+    keep = pltpu.make_async_copy(w_ref, w_hbm, sem.at[0])
+    keep.start()
     for d in range(8):
         for t in range(4):
             c = 4 * d + t
             pm_ref[:, 128 * c : 128 * (c + 1)] = g1_ref[d, 32 * t : 32 * (t + 1), :]
-    mv.flush(5)
-    mv.wait(1)
-    mv.wait(5)
+    mv.flush(3)
     first = iota((8, EC), 0) < 4
     for p in range(PAIRS):
         bot, top = bot_ref[p], top_ref[p]
         grp_ref[p] = jnp.where(first, bot, pltpu.roll(top, 4, 0))
         if p + PAIRS < PLANES:
             grp_ref[p + PAIRS] = jnp.where(first, pltpu.roll(bot, 4, 0), top)
-    mv.flush(0)
-    mv.wait(2)
-    sh = whole_plane(xs_ref, sh_ref[...], w_ref, grp_ref, K)
-    cm = cm_ref[...]
-    rd = jnp.where(sh > 0.0, 1.0 / (4.0 + sh + cm), 0.0)
-    rd_ref[...] = rd
-    cr_ref[...] = cm * rd
-    dg_ref[...] = 4.0 + tile(sh) + tile(cm)
-    for n in (2, 3, 4):
-        mv.flush(n)
-
-    def one(k, c):
-        rd = rd_ref[...]
-        x0 = whole_plane(xs_ref, b_ref[k], w_ref, grp_ref, k) * rd
-        pre = x0 - beside(x0) * rd
-        down_cells(s_ref, k, jnp.where(tile(cm_ref) > 0.0, tile(pre), 0.0))
-        return c
-
-    for c in range(CHUNKS):
-        mv.wait(0, c)
-        lax.fori_loop(4 * c, 4 * c + 4, one, 0)
-    s_ref[K : K + 8, :] = jnp.zeros((8, 4 * TC), jnp.float32)
-    down_cells(s_ref, K, tile(cm_ref))
-    down_cells(s_ref, K + 1, tile(cr_ref))
-    bump_ref[...] = gather_bumps(s_ref)
     mv.flush(1)
+    for n in (0, 4, 6):
+        mv.wait(n)
+    inverse = lambda sh, cm: jnp.where(sh > 0.0, 1.0 / (4.0 + sh + cm), 0.0)
+    cm = tile(cm_ref)
+    at_bump = jnp.where(cm > 0.0, inverse(sh_ref[...], cm), 0.0)
+    ends = inverse(grp_ref[K], cm_ref[TR:ER, :])
+    above = ends[7:8, 0:TC] * at_bump[0:1]
+    below = ends[0:1, 0:TC] * at_bump[TR - 1 : TR]
+    lane = iota((TR, 128), 1)
+    sides = jnp.where(lane == 0, pltpu.roll(at_bump[:, 128:256], 1, 1), 0.0)
+    sides = jnp.where(lane == 127, pltpu.roll(at_bump[:, 0:128], 127, 1), sides)
+    sides = sides * inverse(w_ref[K], cm_ref[0:TR, TC:EC])
+    s_ref[...] = jnp.zeros_like(s_ref)
+    for k in range(K):
+        s_ref[k : k + 1, 0:TC] = grp_ref[k, 7:8, 0:TC] * above
+        s_ref[k : k + 1, 3 * TC : 4 * TC] = grp_ref[k, 0:1, 0:TC] * below
+        z = w_ref[k] * sides
+        for lr in range(4):
+            t_ref[k : k + 1, 128 * lr : 128 * (lr + 1)] = jnp.sum(
+                z[CELL * lr : CELL * (lr + 1)], axis=0, keepdims=True
+            )
+    at, to = iota((512, 128), 0), iota((512, 128), 1)
+    right = (at % 128 == 0) & (to == at // 128 * 8 + 7)
+    left = (at % 128 == 127) & (to == at // 128 * 8)
+    halo = gather_bumps(s_ref) + dot_nn(t_ref[...], (left | right).astype(jnp.float32))
+    bump_ref[0:K, :] = inner_ref[0:K, :] - halo
+    bump_ref[K:, :] = inner_ref[K:, :]
+    mv.flush(2)
+    keep.wait()
 
 
 def package_kernel(
@@ -372,13 +391,21 @@
 
 
 def second_kernel(
-    mv, b_ref, w_ref, grp_ref, rd_ref, dg_ref, cr_ref, x_ref, bp_ref, v0p_ref, v1p_ref, y1_ref,
-    v1_ref, bump_ref, r_ref,
+    mv, b_ref, sh_ref, w_ref, grp_ref, cm_ref, x_ref, bp_ref, v0p_ref, v1p_ref, y1_ref,
+    v1_ref, bump_ref, r_ref, rd_ref, dg_ref, cr_ref,
     e_ref, s_ref, pad_ref, xs_ref,
 ):
     i, j = where_am_i()
-    for n in range(1, 11):
+    for n in range(1, 10):
         mv.wait(n)
+    sh = whole_plane(xs_ref, sh_ref[...], w_ref, grp_ref, K)
+    cm = cm_ref[...]
+    rd = jnp.where(sh > 0.0, 1.0 / (4.0 + sh + cm), 0.0)
+    rd_ref[...] = rd
+    cr_ref[...] = cm * rd
+    dg_ref[...] = 4.0 + tile(sh) + tile(cm)
+    for n in (3, 4, 5):
+        mv.flush(n)
     e_ref[...] = dot_nn(x_ref[...], spread(j))
 
     def one(k, c):
@@ -439,11 +466,17 @@
 
 
 def fourth_kernel(
-    mv, g_ref, pm_ref, cond_ref, const_ref, wp_ref, wd_ref, ra_ref,
-    msg_ref,
-    v_ref, pad_ref, r_ref,
+    mv, g_ref, pm_ref, cond_ref, const_ref, wp_ref, wd_ref, ra_ref, v1_hbm, w_hbm,
+    msg_ref, v1_ref, w_ref,
+    v_ref, pad_ref, r_ref, sems,
 ):
     i, j = where_am_i()
+    loads = [
+        pltpu.make_async_copy(v1_hbm.at[:, 0:TR, 0:TC], v1_ref, sems.at[0]),
+        pltpu.make_async_copy(w_hbm, w_ref, sems.at[1]),
+    ]
+    for c in loads:
+        c.start()
     package_all(g_ref, v_ref)
     for n in range(1, 6):
         mv.wait(n)
@@ -460,6 +493,8 @@
         return c
 
     lax.fori_loop(0, msg_ref.shape[0], one, 0, unroll=8)
+    for c in loads:
+        c.wait()
 
 
 def last_kernel(
@@ -489,10 +524,12 @@
 
     def one(k, carry):
         c0, c1, c2 = (c_ref[n, pl.ds(k, 1), :] for n in range(3))
-        xd_ref[k] = (c0 * b_ref[k]) * rd + c1 * tile(v1_ref.at[k]) + c2 * v2_ref[k]
+        xd_ref[k] = (c0 * b_ref[k]) * rd + c1 * v1_ref[k] + c2 * v2_ref[k]
         return carry
 
-    lax.fori_loop(0, K, one, 0)
+    for c in range(CHUNKS):
+        lax.fori_loop(4 * c, 4 * c + 4, one, 0)
+        mv.flush(0, c)
 
 
 def f32(*shape):
@@ -592,30 +629,30 @@
         [vm(128, 128), pltpu.SemaphoreType.DMA((6,))],
     )
     g1 = swapped(msg1, COL)
-    msg, cm, v0p = call(
+    msg, cm, v0p, bump1 = call(
         start_kernel,
         [(b, "h"), (sh, "h"), (bp, "h"), (m, "h"), (nodes, "h"), (cond, "h")],
-        [(gathered, "r"), (f32(ER, EC), "h"), (small, "h")],
-        [vm(24, 128), vm(K, 4 * TC), vm(K, 128)] + payload,
+        [(gathered, "r"), (f32(ER, EC), "h"), (small, "h"), (f32(K + 8, 128), "h")],
+        [vm(24, 128), vm(K, 4 * TC), vm(K + 8, 4 * TC), vm(6, TR, TC), vm(K, 128)] + payload,
     )
     g = swapped(msg, ROW_COL)
     side, up, dn = call(
         columns_kernel,
         [(g1, "v"), (edge, "h")],
-        [(f32(PLANES, TR, 128), "h"), (f32(PAIRS, 8, EC), "v"), (f32(PAIRS, 8, EC), "v")],
+        [(f32(PLANES, TR, 128), "v"), (f32(PAIRS, 8, EC), "v"), (f32(PAIRS, 8, EC), "v")],
         [vm(128, 128), vm(2, PLANES, 8, EC)],
     )
     n = lax.axis_size(ROW)
     bot = lax.ppermute(up, ROW, [(r + 1, r) for r in range(n - 1)])
     top = lax.ppermute(dn, ROW, [(r, r + 1) for r in range(n - 1)])
-    grp, bump1, rd, dg, cr, pm = call(
-        prepare_kernel,
-        [(b, "c"), (sh, "h"), (side, "h"), (bot, "v"), (top, "v"), (cm, "h"), (g1, "v")],
+    side, grp, bump1, pm = call(
+        edges_kernel,
+        [(sh, "h"), (side, "v"), (bot, "v"), (top, "v"), (cm, "h"), (g1, "v"), (bump1, "h")],
         [
-            (f32(PLANES, 8, EC), "h"), (f32(K + 8, 128), "h"), (f32(ER, EC), "h"),
-            (f32(TR, TC), "h"), (f32(ER, EC), "h"), (f32(OWN, NB), "h"),
+            (f32(PLANES, TR, 128), "r"), (f32(PLANES, 8, EC), "h"), (f32(K + 8, 128), "h"),
+            (f32(OWN, NB), "h"),
         ],
-        [vm(ER, EC), vm(K + 8, 4 * TC)],
+        [vm(K, 4 * TC), vm(K, 512), pltpu.SemaphoreType.DMA((1,))],
     )
     step = [vm(K, NB), vm(K, 128)] + payload
     results = [(small, "h"), (small, "h"), (small, "h"), (lattice, "h"), (gathered, "r")]
@@ -626,10 +663,13 @@
         step,
     )
     g = swapped(msg, ROW_COL)
-    v1, bump2, r = call(
+    v1, bump2, r, rd, dg, cr = call(
         second_kernel,
-        [(b, "c")] + [(x, "h") for x in (side, grp, rd, dg, cr, near, bp, v0p, v1p, y1)],
-        [(ext, "c"), (small, "v"), (f32(3 * K, 128), "h")],
+        [(b, "c")] + [(x, "h") for x in (sh, side, grp, cm, near, bp, v0p, v1p, y1)],
+        [
+            (ext, "c"), (small, "v"), (f32(3 * K, 128), "h"), (f32(ER, EC), "h"),
+            (f32(TR, TC), "h"), (f32(ER, EC), "h"),
+        ],
         [vm(6 * K, EC), vm(K, 4 * TC), vm(K, 128), vm(ER, EC)],
     )
     wp, wd, y2, near, msg = call(
@@ -645,17 +685,17 @@
         [(die, "c"), (f32(128, 128), "v")],
         [vm(6 * K, EC)],
     )
-    (msg,) = call(
+    msg, v1, w = call(
         fourth_kernel,
-        [(g, "v")] + [(x, "h") for x in (pm, cond, bump1, wp, wd)] + [(r, "v")],
-        [(f32(128, 1, 128), "v")],
-        [vm(K, NB), vm(K, 128), vm(128, 128)],
+        [(g, "v")] + [(x, "h") for x in (pm, cond, bump1, wp, wd)] + [(r, "v"), (v1, "r"), (w, "r")],
+        [(f32(128, 1, 128), "v"), (die, "v"), (die, "v")],
+        [vm(K, NB), vm(K, 128), vm(128, 128), pltpu.SemaphoreType.DMA((2,))],
     )
     g = swapped(msg, ROW_COL)
     return call(
         last_kernel,
         [(x, "v") for x in (g, b, rd, v1, w, v0p, v1p, wp)],
-        [(die, "v"), (f32(K, OWN), "v")],
+        [(die, "c"), (f32(K, OWN), "v")],
         [vm(3, K, TC)],
     )
 

time: 120 us -> 113 us (0.942)
  local copies, waits for them, and re-layouts: 3.55 us -> 0.02 us
  starting transfers between devices: 39 us -> 37.8 us
    unnamed x14 -> x10, local copies, waits for them, and re-layouts: 3.55 us -> 0.02 us
    all_to_all x4, waiting for transfers between devices: 18.1 us -> 16.2 us  [swapped(): return lax.all_to_all(x, axes, 0, 0, tiled=True)]
  transfers between devices with their start and end apart: 6 -> 6, of which waited for: 5 -> 6; matrix products, arithmetic and copies ran while one was open for 0% -> 0% of each run, Pallas kernels for 24% -> 23%
where the time goes in v3:
time: 113 us; the launch traced here: 112 us
  Pallas kernels  40 us (35%)
  starting transfers between devices  37.8 us (33%)
  waiting for transfers between devices  19.2 us (17%)
  blocking collectives  14.5 us (13%)
    pallas_call x10, Pallas kernels, call(): pl.pallas_call(wrapped, out_shape=tuple((x if m == 'v' else pltpu.HBM(x.s...  40 us
    all_to_all x4, starting transfers between devices, swapped(): return lax.all_to_all(x, axes, 0, 0, tiled=True)  32.2 us
    all_to_all x4, waiting for transfers between devices, swapped(): return lax.all_to_all(x, axes, 0, 0, tiled=True)  16.2 us
    all_to_all x1, blocking collectives, swapped(): return lax.all_to_all(x, axes, 0, 0, tiled=True)  14.5 us
    ppermute x1, starting transfers between devices, body(): bot = lax.ppermute(up, ROW, [(r + 1, r) for r in range(n - 1)])  2.98 us
    ppermute x1, waiting for transfers between devices, body(): bot = lax.ppermute(up, ROW, [(r + 1, r) for r in range(n - 1)])  2.62 us
    ppermute x1, starting transfers between devices, body(): top = lax.ppermute(dn, ROW, [(r, r + 1) for r in range(n - 1)])  2.61 us
  transfers between devices with their start and end apart: 6, of which 6 were waited for; matrix products, arithmetic and copies ran while one was open for 0% of the time, Pallas kernels for 23%

profile of v3, /device:TPU:1, one launch (start us, length us, event | category | flops | bytes accessed | tf_op | source)
XLA Modules:
  0.0 112.3 jit_solution(12491787170759504381)
XLA Ops:
  0.6 3.0 %load_kernel.1 = (f32[8,184,128]{2,1,0:T(8,128)}, f32[17,16,256]{2,1,0:T(8,128)}) custom-call(f32[16,128,256]{2,1,0:T(8,128)} %refs_1_.7, f32[128,256]{1,0:T(8,128)} %refs_1_.6, f32[8,32,512]{2,1,0:T(8,128)} %bitcast.3), custom_call_target="tpu_custom_call" | custom-call | tf_op jit(solution)/shard_map/load_kernel/pallas_call | solution.py:599
  3.6 7.5 %all-to-all-start.1 = ((f32[8,184,128]{2,1,0:T(8,128)}), f32[8,184,128]{2,1,0:T(8,128)S(1)}, u32[]{:S(2)}, u32[]{:S(2)}) async-start(f32[8,184,128]{2,1,0:T(8,128)} %get-tuple-element.36), calls=%async_computation.1 | async-start | bytes 1507328 | tf_op jit(solution)/shard_map/all_to_all | solution.py:613
  11.1 6.1 %start_kernel.1 = (f32[128,8,128]{2,1,0:T(8,128)}, f32[136,384]{1,0:T(8,128)}, f32[16,128]{1,0:T(8,128)}, f32[24,128]{1,0:T(8,128)}) custom-call(f32[16,128,256]{2,1,0:T(8,128)} %refs_1_.7, f32[128,256]{1,0:T(8,128)} %refs_1_.6, f32[16,32]{1,0:T(8,128)} %refs_6_.1, f32[1,32,32]{2,1,0:T(8,128)} %refs_2_.5, s32[32,128]{1,0:T(8,128)} %bitcast.8, f32[32,128]{1,0:T(8,128)} %bitcast.4), custom_call_target="tpu_custom_call" | custom-call | tf_op jit(solution)/shard_map/start_kernel/pallas_call | solution.py:599
  17.2 6.8 %all-to-all-done.1.refs_0_.refs_5_ = f32[8,184,128]{2,1,0:T(8,128)S(1)} async-done(((f32[8,184,128]{2,1,0:T(8,128)}), f32[8,184,128]{2,1,0:T(8,128)S(1)}, u32[]{:S(2)}, u32[]{:S(2)}) %all-to-all-start.1) | async-done | bytes 753696 | tf_op jit(solution)/shard_map/all_to_all | solution.py:613
  24.0 7.9 %all-to-all-start = ((f32[128,8,128]{2,1,0:T(8,128)}), f32[128,8,128]{2,1,0:T(8,128)S(1)}, u32[]{:S(2)}, u32[]{:S(2)}) async-start(f32[128,8,128]{2,1,0:T(8,128)} %get-tuple-element.35), calls=%async_computation | async-start | bytes 1048576 | tf_op jit(solution)/shard_map/all_to_all | solution.py:613
  31.9 1.0 columns_kernel.1
  32.9 3.0 %collective-permute-start = (f32[9,8,384]{2,1,0:T(8,128)S(1)}, f32[9,8,384]{2,1,0:T(8,128)S(1)}, u32[]{:S(2)}, u32[]{:S(2)}) collective-permute-start(f32[9,8,384]{2,1,0:T(8,128)S(1)} %get-tuple-element.39), channel_id=1, source_target_pairs={{8,0},{16,8},{24,16},{32,24},{40,32},{48,40},{56,48},{64,56},{72,6... | collective-permute-start | bytes 331784 | tf_op jit(solution)/shard_map/ppermute | solution.py:646
  35.9 2.6 %collective-permute-start.1 = (f32[9,8,384]{2,1,0:T(8,128)S(1)}, f32[9,8,384]{2,1,0:T(8,128)S(1)}, u32[]{:S(2)}, u32[]{:S(2)}) collective-permute-start(f32[9,8,384]{2,1,0:T(8,128)S(1)} %get-tuple-element.40), channel_id=1, source_target_pairs={{0,8},{8,16},{16,24},{24,32},{32,40},{40,48},{48,56},{56,64},{64,7... | collective-permute-start | bytes 331784 | tf_op jit(solution)/shard_map/ppermute | solution.py:647
  38.5 2.6 %collective-permute-done.refs_2_ = f32[9,8,384]{2,1,0:T(8,128)S(1)} collective-permute-done((f32[9,8,384]{2,1,0:T(8,128)S(1)}, f32[9,8,384]{2,1,0:T(8,128)S(1)}, u32[]{:S(2)}, u32[]{:S(2)}) %collective-permute-start) | collective-permute-done | bytes 110624 | tf_op jit(solution)/shard_map/ppermute | solution.py:646
  41.1 0.4 collective-permute-done.1.refs_3_
  41.6 2.7 %edges_kernel.1 = (f32[17,128,128]{2,1,0:T(8,128)}, f32[17,8,384]{2,1,0:T(8,128)}, f32[24,128]{1,0:T(8,128)}, f32[32,4096]{1,0:T(8,128)}) custom-call(f32[128,256]{1,0:T(8,128)} %refs_1_.6, f32[17,128,128]{2,1,0:T(8,128)S(1)} %get-tuple-element.38.refs_1_, f32[9,8,384]{2,1,0:T(8,128)S(1)} %collective-permute-done.refs_2_, ...), custom_call_target="tpu_custom_call" | custom-call | tf_op jit(solution)/shard_map/edges_kernel/pallas_call | solution.py:599
  44.3 0.5 all-to-all-done.refs_0_
  44.7 2.8 %package_kernel.2 = (f32[16,128]{1,0:T(8,128)}, f32[16,128]{1,0:T(8,128)}, f32[16,128]{1,0:T(8,128)}, f32[96,128]{1,0:T(8,128)}, f32[128,8,128]{2,1,0:T(8,128)}) custom-call(f32[128,8,128]{2,1,0:T(8,128)S(1)} %all-to-all-done.refs_0_, f32[32,4096]{1,0:T(8,128)} %get-tuple-element.43.refs_1_, f32[1,32,32]{2,1,0:T(8,128)} %refs_2_.5, f32[32,128]{1,0:T(8,128)} %bitcast.5, ...), custom_call_target="tpu_custom_call" | custom-call | tf_op jit(solution)/shard_map/package_kernel/pallas_call | solution.py:599
  47.5 11.0 %all-to-all-start.2 = ((f32[128,8,128]{2,1,0:T(8,128)}), f32[128,8,128]{2,1,0:T(8,128)S(1)}, u32[]{:S(2)}, u32[]{:S(2)}) async-start(f32[128,8,128]{2,1,0:T(8,128)} %get-tuple-element.46), calls=%async_computation.2 | async-start | bytes 1048576 | tf_op jit(solution)/shard_map/all_to_all | solution.py:613
  58.6 8.8 %second_kernel.1 = (f32[16,136,384]{2,1,0:T(8,128)}, f32[16,128]{1,0:T(8,128)S(1)}, f32[48,128]{1,0:T(8,128)}, f32[136,384]{1,0:T(8,128)}, f32[128,256]{1,0:T(8,128)}, /*index=5*/f32[136,384]{1,0:T(8,128)}) custom-call(f32[16,128,256]{2,1,0:T(8,128)} %refs_1_.7, f32[128,256]{1,0:T(8,128)} %refs_1_.6, f32[17,128,128]{2,1,0:T(8,128)} %get-tuple-element.47.refs_2_, ...), custom_call_target="tpu_custom_call" | custom-call | tf_op jit(solution)/shard_map/second_kernel/pallas_call | solution.py:599
  67.4 4.0 %all-to-all-done.2.refs_0_ = f32[128,8,128]{2,1,0:T(8,128)S(1)} async-done(((f32[128,8,128]{2,1,0:T(8,128)}), f32[128,8,128]{2,1,0:T(8,128)S(1)}, u32[]{:S(2)}, u32[]{:S(2)}) %all-to-all-start.2) | async-done | bytes 524320 | tf_op jit(solution)/shard_map/all_to_all | solution.py:613
  71.4 2.8 %package_kernel.3 = (f32[16,128]{1,0:T(8,128)}, f32[16,128]{1,0:T(8,128)}, f32[16,128]{1,0:T(8,128)}, f32[96,128]{1,0:T(8,128)}, f32[128,8,128]{2,1,0:T(8,128)}) custom-call(f32[128,8,128]{2,1,0:T(8,128)S(1)} %all-to-all-done.2.refs_0_, f32[32,4096]{1,0:T(8,128)} %get-tuple-element.43.refs_1_, f32[1,32,32]{2,1,0:T(8,128)} %refs_2_.5, f32[32,128]{1,0:T(8,128)} %bitcast.6, ...), custom_call_target="tpu_custom_call" | custom-call | tf_op jit(solution)/shard_map/package_kernel/pallas_call | solution.py:599
  74.2 5.8 %all-to-all-start.3 = ((f32[128,8,128]{2,1,0:T(8,128)}), f32[128,8,128]{2,1,0:T(8,128)S(1)}, u32[]{:S(2)}, u32[]{:S(2)}) async-start(f32[128,8,128]{2,1,0:T(8,128)} %get-tuple-element.53), calls=%async_computation.3 | async-start | bytes 1048576 | tf_op jit(solution)/shard_map/all_to_all | solution.py:613
  80.0 7.8 %third_kernel.1 = (f32[16,128,256]{2,1,0:T(8,128)}, f32[128,128]{1,0:T(8,128)S(1)}) custom-call(f32[16,136,384]{2,1,0:T(8,128)} %get-tuple-element.56.refs_0_.refs_7_, f32[136,384]{1,0:T(8,128)} %get-tuple-element.57.refs_1_.refs_2_, f32[128,256]{1,0:T(8,128)} %get-tuple-element.58.refs_2_, f32[136,384]{1,0:T(8,128)} %get-tuple-element.59.refs_3_, ...), custom_call_target="tpu_custom_call" | custom-call | tf_op jit(solution)/shard_map/third_kernel/pallas_call | solution.py:599
  87.8 5.0 %all-to-all-done.3.refs_0_ = f32[128,8,128]{2,1,0:T(8,128)S(1)} async-done(((f32[128,8,128]{2,1,0:T(8,128)}), f32[128,8,128]{2,1,0:T(8,128)S(1)}, u32[]{:S(2)}, u32[]{:S(2)}) %all-to-all-start.3) | async-done | bytes 524320 | tf_op jit(solution)/shard_map/all_to_all | solution.py:613
  92.8 0.0 copy-start
  92.8 0.0 copy-start.1
  92.8 0.0 copy-start.2
  92.8 0.0 copy-start.3
  92.8 0.0 copy-start.4
  92.8 2.6 %fourth_kernel.1 = (f32[128,1,128]{2,1,0:T(1,128)S(1)}, f32[16,128,256]{2,1,0:T(8,128)S(1)}, f32[16,128,256]{2,1,0:T(8,128)S(1)}) custom-call(f32[128,8,128]{2,1,0:T(8,128)S(1)} %all-to-all-done.3.refs_0_, f32[32,4096]{1,0:T(8,128)} %get-tuple-element.43.refs_1_, f32[32,128]{1,0:T(8,128)} %bitcast.7, f32[24,128]{1,0:T(8,128)} %get-tuple-element.44.refs_4_.refs_5_.refs_3_, ...), custom_call_target="tpu_custom_call" | custom-call | tf_op jit(solution)/shard_map/fourth_kernel/pallas_call | solution.py:599
  95.4 14.5 %all_to_all.25.refs_0_ = f32[128,1,128]{2,1,0:T(1,128)S(1)} all-to-all(f32[128,1,128]{2,1,0:T(1,128)S(1)} %get-tuple-element.65), channel_id=1, replica_groups=mesh['row_0'=2,'row_1'=4,'row_2'=2,'col_0'=4,'col_1'=2] {'row_0','row_1'..., dimensions={0} | all-to-all | bytes 131072 | tf_op jit(solution)/shard_map/all_to_all | solution.py:613
  109.9 0.0 copy-done
  109.9 0.0 copy-done.1
  109.9 0.0 copy-done.2
  109.9 0.0 copy-done.3
  109.9 0.0 copy-done.4
  109.9 2.4 %last_kernel.1 = (f32[16,128,256]{2,1,0:T(8,128)}, f32[16,32]{1,0:T(8,128)}) custom-call(f32[128,1,128]{2,1,0:T(1,128)S(1)} %all_to_all.25.refs_0_, f32[16,128,256]{2,1,0:T(8,128)S(1)} %copy-done, f32[136,384]{1,0:T(8,128)S(1)} %copy-done.1, f32[16,128,256]{2,1,0:T(8,128)S(1)} %get-tuple-element.66.refs_3_, f32[16,128,256]{2,1,0:T(8,128)S(1)} %get-tuple-element.67.refs_4_, ...), custom_call_target="tpu_custom_call" | custom-call | tf_op jit(solution)/shard_map/last_kernel/pallas_call | solution.py:599
Async XLA Ops:
  3.6 20.4 %all-to-all-start.1 = ((f32[8,184,128]{2,1,0:T(8,128)}), f32[8,184,128]{2,1,0:T(8,128)S(1)}, u32[]{:S(2)}, u32[]{:S(2)}) async-start(f32[8,184,128]{2,1,0:T(8,128)} %get-tuple-element.36), calls=%async_computation.1 | async-start | bytes 1507328 | tf_op jit(solution)/shard_map/all_to_all | solution.py:613
  24.0 20.7 %all-to-all-start = ((f32[128,8,128]{2,1,0:T(8,128)}), f32[128,8,128]{2,1,0:T(8,128)S(1)}, u32[]{:S(2)}, u32[]{:S(2)}) async-start(f32[128,8,128]{2,1,0:T(8,128)} %get-tuple-element.35), calls=%async_computation | async-start | bytes 1048576 | tf_op jit(solution)/shard_map/all_to_all | solution.py:613
  32.9 8.2 %collective-permute-start = (f32[9,8,384]{2,1,0:T(8,128)S(1)}, f32[9,8,384]{2,1,0:T(8,128)S(1)}, u32[]{:S(2)}, u32[]{:S(2)}) collective-permute-start(f32[9,8,384]{2,1,0:T(8,128)S(1)} %get-tuple-element.39), channel_id=1, source_target_pairs={{8,0},{16,8},{24,16},{32,24},{40,32},{48,40},{56,48},{64,56},{72,6... | collective-permute-start | bytes 331784 | tf_op jit(solution)/shard_map/ppermute | solution.py:646
  35.9 5.7 %collective-permute-start.1 = (f32[9,8,384]{2,1,0:T(8,128)S(1)}, f32[9,8,384]{2,1,0:T(8,128)S(1)}, u32[]{:S(2)}, u32[]{:S(2)}) collective-permute-start(f32[9,8,384]{2,1,0:T(8,128)S(1)} %get-tuple-element.40), channel_id=1, source_target_pairs={{0,8},{8,16},{16,24},{24,32},{32,40},{40,48},{48,56},{56,64},{64,7... | collective-permute-start | bytes 331784 | tf_op jit(solution)/shard_map/ppermute | solution.py:647
  47.5 23.8 %all-to-all-start.2 = ((f32[128,8,128]{2,1,0:T(8,128)}), f32[128,8,128]{2,1,0:T(8,128)S(1)}, u32[]{:S(2)}, u32[]{:S(2)}) async-start(f32[128,8,128]{2,1,0:T(8,128)} %get-tuple-element.46), calls=%async_computation.2 | async-start | bytes 1048576 | tf_op jit(solution)/shard_map/all_to_all | solution.py:613
  74.2 18.6 %all-to-all-start.3 = ((f32[128,8,128]{2,1,0:T(8,128)}), f32[128,8,128]{2,1,0:T(8,128)S(1)}, u32[]{:S(2)}, u32[]{:S(2)}) async-start(f32[128,8,128]{2,1,0:T(8,128)} %get-tuple-element.53), calls=%async_computation.3 | async-start | bytes 1048576 | tf_op jit(solution)/shard_map/all_to_all | solution.py:613
  92.8 17.1 %copy-start = (f32[16,128,256]{2,1,0:T(8,128)S(1)}, f32[16,128,256]{2,1,0:T(8,128)}, u32[]{:S(2)}) copy-start(f32[16,128,256]{2,1,0:T(8,128)} %refs_1_.7) | copy-start | bytes 6291460
  92.8 17.1 %copy-start.1 = (f32[136,384]{1,0:T(8,128)S(1)}, f32[136,384]{1,0:T(8,128)}, u32[]{:S(2)}) copy-start(f32[136,384]{1,0:T(8,128)} %get-tuple-element.57.refs_1_.refs_2_) | copy-start | bytes 626692
  92.8 17.1 %copy-start.2 = (f32[16,128]{1,0:T(8,128)S(1)}, f32[16,128]{1,0:T(8,128)}, u32[]{:S(2)}) copy-start(f32[16,128]{1,0:T(8,128)} %get-tuple-element.45.refs_6_.refs_7_.refs_5_) | copy-start | bytes 24580
  92.8 17.1 %copy-start.3 = (f32[16,128]{1,0:T(8,128)S(1)}, f32[16,128]{1,0:T(8,128)}, u32[]{:S(2)}) copy-start(f32[16,128]{1,0:T(8,128)} %get-tuple-element.50.refs_8_.refs_6_) | copy-start | bytes 24580
  92.8 17.1 %copy-start.4 = (f32[16,128]{1,0:T(8,128)S(1)}, f32[16,128]{1,0:T(8,128)}, u32[]{:S(2)}) copy-start(f32[16,128]{1,0:T(8,128)} %get-tuple-element.54.refs_5_.refs_4_.refs_7_) | copy-start | bytes 24580

commit v4 on v3

--- a/solution.py
+++ b/solution.py
@@ -72,6 +72,14 @@
     out = jnp.where(lane < 32, vp[0:8], hi)
     out = jnp.where(lane < 64, out, pltpu.roll(vd[0:8], 64, 1))
     return jnp.where(lane < 96, out, pltpu.roll(vd[8:16], 96, 1))
+
+
+def pack_package(vp):
+    lane = iota((4, 128), 1)
+    out = vp[0:4]
+    for m in range(1, 4):
+        out = jnp.where(lane // 32 == m, pltpu.roll(vp, 32 * m, 1)[4 * m : 4 * m + 4], out)
+    return out
 
 
 def gather_bumps(s_ref):
@@ -251,6 +259,23 @@
         at = pl.ds(pl.multiple_of(128 * c, 128), 128)
         v_ref[0:8, at] = lo
         v_ref[8:16, at] = hi
+        return carry
+
+    lax.fori_loop(0, NB // 128, one, 0, unroll=4)
+
+
+def package_only(g_ref, v_ref):
+    lane = iota((4, 128), 1) // 32
+
+    def one(c, carry):
+        xs = [g_ref[4 * c + d] for d in range(4)]
+        at = pl.ds(pl.multiple_of(128 * c, 128), 128)
+        for m in range(4):
+            out = xs[m]
+            for d in range(4):
+                if d != m:
+                    out = jnp.where(lane == d, pltpu.roll(xs[d], (32 * (d - m)) % 128, 1), out)
+            v_ref[4 * m : 4 * m + 4, at] = out
         return carry
 
     lax.fori_loop(0, NB // 128, one, 0, unroll=4)
@@ -376,7 +401,7 @@
     around(v_ref, x_ref, i)
     for n in range(4):
         mv.flush(n)
-    send(msg_hbm, pay_ref, sems, pack(out, vd))
+    send(msg_hbm, pay_ref, sems, pack(out, vd) if step == 1 else pack_package(out))
 
 
 def at_tile(v_ref, i, j):
@@ -392,7 +417,7 @@
 
 def second_kernel(
     mv, b_ref, sh_ref, w_ref, grp_ref, cm_ref, x_ref, bp_ref, v0p_ref, v1p_ref, y1_ref,
-    v1_ref, bump_ref, r_ref, rd_ref, dg_ref, cr_ref,
+    v1_ref, bump_ref, r_ref, rd_ref, dg_ref, cr_ref, next_ref,
     e_ref, s_ref, pad_ref, xs_ref,
 ):
     i, j = where_am_i()
@@ -412,8 +437,10 @@
         rd, dg = rd_ref[...], dg_ref[...]
         x0 = whole_plane(xs_ref, b_ref[k], w_ref, grp_ref, k) * rd
         x1 = x0 - (beside(x0) * rd + cr_ref[...] * coupled(e_ref, k))
-        v1_ref[k] = x1
-        down_cells(s_ref, k, jnp.where(tile(cr_ref) > 0.0, tile(-beside(x1) * rd), 0.0))
+        v1_ref[k] = tile(x1)
+        near = -beside(x1) * rd
+        next_ref[k] = near
+        down_cells(s_ref, k, jnp.where(tile(cr_ref) > 0.0, tile(near), 0.0))
         a, b = tile(x0), tile(x1)
         add_dot(r_ref, k, dg * a * a)
         add_dot(r_ref, K + k, dg * a * b)
@@ -424,6 +451,7 @@
         mv.wait(0, c)
         lax.fori_loop(4 * c, 4 * c + 4, one, 0)
         mv.flush(0, c)
+        mv.flush(6, c)
     bump_ref[...] = gather_bumps(s_ref)
     v0p, v1p, y1 = v0p_ref[...], v1p_ref[...], y1_ref[...]
     bp = padded(pad_ref, bp_ref[...])
@@ -434,12 +462,12 @@
 
 
 def third_kernel(
-    mv, v1_ref, rd_ref, dg_ref, cr_ref, x_ref, wp_ref, y1_ref, y2_ref, ra_ref,
+    mv, next_ref, v1_ref, rd_ref, dg_ref, cr_ref, x_ref, wp_ref, y1_ref, y2_ref, ra_ref,
     wt_ref, r_ref,
     e_ref,
 ):
     i, j = where_am_i()
-    for n in range(1, 9):
+    for n in range(2, 10):
         mv.wait(n)
     e_ref[...] = dot_nn(x_ref[...], spread(j))
     r_ref[6 * K :, :] = jnp.zeros((2 * K, 128), jnp.float32)
@@ -447,9 +475,8 @@
 
     def one(k, c):
         dg = dg_ref[...]
-        x1 = v1_ref[k]
-        w = -(beside(x1) * rd_ref[...] + cr_ref[...] * coupled(e_ref, k))
-        a, b = tile(x1), tile(w)
+        w = next_ref[k] - cr_ref[...] * coupled(e_ref, k)
+        a, b = v1_ref[k], tile(w)
         wt_ref[k] = b
         add_dot(r_ref, 3 * K + k, dg * a * b)
         add_dot(r_ref, 4 * K + k, dg * b * b)
@@ -458,6 +485,7 @@
 
     for c in range(CHUNKS):
         mv.wait(0, c)
+        mv.wait(1, c)
         lax.fori_loop(4 * c, 4 * c + 4, one, 0)
         mv.flush(0, c)
     wp, y1, y2 = wp_ref[...], y1_ref[...], y2_ref[...]
@@ -472,20 +500,20 @@
 ):
     i, j = where_am_i()
     loads = [
-        pltpu.make_async_copy(v1_hbm.at[:, 0:TR, 0:TC], v1_ref, sems.at[0]),
+        pltpu.make_async_copy(v1_hbm, v1_ref, sems.at[0]),
         pltpu.make_async_copy(w_hbm, w_ref, sems.at[1]),
     ]
     for c in loads:
         c.start()
-    package_all(g_ref, v_ref)
+    package_only(g_ref, v_ref)
     for n in range(1, 6):
         mv.wait(n)
     wp = wp_ref[...]
-    y = padded(pad_ref, dot_nt(v_ref[...], pm_ref[...]))
-    y = y + own_conductance(cond_ref, i, j) * (wp - own_die(g_ref, i, j))
+    y = padded(pad_ref, dot_nt(v_ref[...], pm_ref[...])) + own_conductance(cond_ref, i, j) * wp
     y = jnp.where(iota((K, 128), 1) < OWN, y, 0.0)
     r_ref[...] = ra_ref[...]
-    r_ref[5 * K : 6 * K, :] += wp * y - const_ref[K : K + 1, :] * wd_ref[...] * at_tile(v_ref, i, j)
+    both = const_ref[K : K + 1, :] * wd_ref[...] * at_tile(v_ref, i, j)
+    r_ref[5 * K : 6 * K, :] += wp * y - 2.0 * both
     sums = dot_nt(jnp.ones((8, 128), jnp.float32), r_ref[...])
 
     def one(d, c):
@@ -622,6 +650,7 @@
     gathered, small, ext, die = f32(128, 8, 128), f32(K, 128), f32(K, ER, EC), f32(K, TR, TC)
     lattice = f32(6 * K, 128)
     payload = [vm(128 // SENDS, 8, 128), pltpu.SemaphoreType.DMA((SENDS,))]
+    alone = [vm(128 // SENDS, 4, 128)] + payload[1:]
     msg1, edge = call(
         load_kernel,
         [(b, "c"), (sh, "h"), (pkg_matrix.reshape(8, OWN, 512), "h")],
@@ -654,34 +683,34 @@
         ],
         [vm(K, 4 * TC), vm(K, 512), pltpu.SemaphoreType.DMA((1,))],
     )
-    step = [vm(K, NB), vm(K, 128)] + payload
-    results = [(small, "h"), (small, "h"), (small, "h"), (lattice, "h"), (gathered, "r")]
+    step = [vm(K, NB), vm(K, 128)]
+    results = [(small, "h"), (small, "h"), (small, "h"), (lattice, "h")]
     v1p, _, y1, near, msg = call(
         functools.partial(package_kernel, 1),
         [(g, "v"), (pm, "h"), (m, "h"), (cond, "h"), (bump1, "h"), (bump1, "h"), (v0p, "h")],
-        results,
-        step,
+        results + [(gathered, "r")],
+        step + payload,
     )
     g = swapped(msg, ROW_COL)
-    v1, bump2, r, rd, dg, cr = call(
+    v1, bump2, r, rd, dg, cr, near1 = call(
         second_kernel,
         [(b, "c")] + [(x, "h") for x in (sh, side, grp, cm, near, bp, v0p, v1p, y1)],
         [
-            (ext, "c"), (small, "v"), (f32(3 * K, 128), "h"), (f32(ER, EC), "h"),
-            (f32(TR, TC), "h"), (f32(ER, EC), "h"),
+            (die, "c"), (small, "v"), (f32(3 * K, 128), "h"), (f32(ER, EC), "h"),
+            (f32(TR, TC), "h"), (f32(ER, EC), "h"), (ext, "c"),
         ],
         [vm(6 * K, EC), vm(K, 4 * TC), vm(K, 128), vm(ER, EC)],
     )
     wp, wd, y2, near, msg = call(
         functools.partial(package_kernel, 2),
         [(g, "v"), (pm, "h"), (m, "h"), (cond, "h"), (bump2, "v"), (bump1, "h"), (v1p, "h")],
-        results,
-        step,
+        results + [(f32(128, 4, 128), "r")],
+        step + alone,
     )
     g = swapped(msg, ROW_COL)
     w, r = call(
         third_kernel,
-        [(v1, "c")] + [(x, "h") for x in (rd, dg, cr, near, wp, y1, y2, r)],
+        [(near1, "c"), (v1, "c")] + [(x, "h") for x in (rd, dg, cr, near, wp, y1, y2, r)],
         [(die, "c"), (f32(128, 128), "v")],
         [vm(6 * K, EC)],
     )

time: 113 us -> 111 us (0.982)
  Pallas kernels: 40 us -> 38.8 us
    pallas_call x10, Pallas kernels: 40 us -> 38.8 us  [call(): pl.pallas_call(wrapped, out_shape=tuple((x if m == 'v' else pltpu.HBM(x.s...]
where the time goes in v4:
time: 111 us
  Pallas kernels  38.8 us (35%)
  starting transfers between devices  37.9 us (34%)
  waiting for transfers between devices  18.2 us (16%)
  blocking collectives  15 us (14%)
    pallas_call x10, Pallas kernels, call(): pl.pallas_call(wrapped, out_shape=tuple((x if m == 'v' else pltpu.HBM(x.s...  38.8 us
    all_to_all x4, starting transfers between devices, swapped(): return lax.all_to_all(x, axes, 0, 0, tiled=True)  32.4 us
    all_to_all x4, waiting for transfers between devices, swapped(): return lax.all_to_all(x, axes, 0, 0, tiled=True)  15.1 us
    all_to_all x1, blocking collectives, swapped(): return lax.all_to_all(x, axes, 0, 0, tiled=True)  15 us
    ppermute x1, starting transfers between devices, body(): bot = lax.ppermute(up, ROW, [(r + 1, r) for r in range(n - 1)])  2.98 us
    ppermute x1, waiting for transfers between devices, body(): bot = lax.ppermute(up, ROW, [(r + 1, r) for r in range(n - 1)])  2.62 us
    ppermute x1, starting transfers between devices, body(): top = lax.ppermute(dn, ROW, [(r, r + 1) for r in range(n - 1)])  2.61 us
  transfers between devices with their start and end apart: 6, of which 6 were waited for; matrix products, arithmetic and copies ran while one was open for 0% of the time, Pallas kernels for 23%

profile of v4, /device:TPU:1, one launch (start us, length us, event | category | flops | bytes accessed | tf_op | source)
XLA Modules:
  0.0 110.7 jit_solution(6244406143316967600)
XLA Ops:
  0.6 3.0 %load_kernel.1 = (f32[8,184,128]{2,1,0:T(8,128)}, f32[17,16,256]{2,1,0:T(8,128)}) custom-call(f32[16,128,256]{2,1,0:T(8,128)} %refs_1_.7, f32[128,256]{1,0:T(8,128)} %refs_1_.6, f32[8,32,512]{2,1,0:T(8,128)} %bitcast.3), custom_call_target="tpu_custom_call" | custom-call | tf_op jit(solution)/shard_map/load_kernel/pallas_call | solution.py:627
  3.6 7.5 %all-to-all-start.1 = ((f32[8,184,128]{2,1,0:T(8,128)}), f32[8,184,128]{2,1,0:T(8,128)S(1)}, u32[]{:S(2)}, u32[]{:S(2)}) async-start(f32[8,184,128]{2,1,0:T(8,128)} %get-tuple-element.37), calls=%async_computation.1 | async-start | bytes 1507328 | tf_op jit(solution)/shard_map/all_to_all | solution.py:641
  11.1 6.1 %start_kernel.1 = (f32[128,8,128]{2,1,0:T(8,128)}, f32[136,384]{1,0:T(8,128)}, f32[16,128]{1,0:T(8,128)}, f32[24,128]{1,0:T(8,128)}) custom-call(f32[16,128,256]{2,1,0:T(8,128)} %refs_1_.7, f32[128,256]{1,0:T(8,128)} %refs_1_.6, f32[16,32]{1,0:T(8,128)} %refs_6_.1, f32[1,32,32]{2,1,0:T(8,128)} %refs_2_.5, s32[32,128]{1,0:T(8,128)} %bitcast.8, f32[32,128]{1,0:T(8,128)} %bitcast.4), custom_call_target="tpu_custom_call" | custom-call | tf_op jit(solution)/shard_map/start_kernel/pallas_call | solution.py:627
  17.2 6.8 %all-to-all-done.1.refs_0_.refs_5_ = f32[8,184,128]{2,1,0:T(8,128)S(1)} async-done(((f32[8,184,128]{2,1,0:T(8,128)}), f32[8,184,128]{2,1,0:T(8,128)S(1)}, u32[]{:S(2)}, u32[]{:S(2)}) %all-to-all-start.1) | async-done | bytes 753696 | tf_op jit(solution)/shard_map/all_to_all | solution.py:641
  24.0 7.9 %all-to-all-start = ((f32[128,8,128]{2,1,0:T(8,128)}), f32[128,8,128]{2,1,0:T(8,128)S(1)}, u32[]{:S(2)}, u32[]{:S(2)}) async-start(f32[128,8,128]{2,1,0:T(8,128)} %get-tuple-element.36), calls=%async_computation | async-start | bytes 1048576 | tf_op jit(solution)/shard_map/all_to_all | solution.py:641
  31.9 1.0 columns_kernel.1
  32.9 3.0 %collective-permute-start = (f32[9,8,384]{2,1,0:T(8,128)S(1)}, f32[9,8,384]{2,1,0:T(8,128)S(1)}, u32[]{:S(2)}, u32[]{:S(2)}) collective-permute-start(f32[9,8,384]{2,1,0:T(8,128)S(1)} %get-tuple-element.40), channel_id=1, source_target_pairs={{8,0},{16,8},{24,16},{32,24},{40,32},{48,40},{56,48},{64,56},{72,6... | collective-permute-start | bytes 331784 | tf_op jit(solution)/shard_map/ppermute | solution.py:675
  35.9 2.6 %collective-permute-start.1 = (f32[9,8,384]{2,1,0:T(8,128)S(1)}, f32[9,8,384]{2,1,0:T(8,128)S(1)}, u32[]{:S(2)}, u32[]{:S(2)}) collective-permute-start(f32[9,8,384]{2,1,0:T(8,128)S(1)} %get-tuple-element.41), channel_id=1, source_target_pairs={{0,8},{8,16},{16,24},{24,32},{32,40},{40,48},{48,56},{56,64},{64,7... | collective-permute-start | bytes 331784 | tf_op jit(solution)/shard_map/ppermute | solution.py:676
  38.5 2.6 %collective-permute-done.refs_2_ = f32[9,8,384]{2,1,0:T(8,128)S(1)} collective-permute-done((f32[9,8,384]{2,1,0:T(8,128)S(1)}, f32[9,8,384]{2,1,0:T(8,128)S(1)}, u32[]{:S(2)}, u32[]{:S(2)}) %collective-permute-start) | collective-permute-done | bytes 110624 | tf_op jit(solution)/shard_map/ppermute | solution.py:675
  41.1 0.4 collective-permute-done.1.refs_3_
  41.6 2.7 %edges_kernel.1 = (f32[17,128,128]{2,1,0:T(8,128)}, f32[17,8,384]{2,1,0:T(8,128)}, f32[24,128]{1,0:T(8,128)}, f32[32,4096]{1,0:T(8,128)}) custom-call(f32[128,256]{1,0:T(8,128)} %refs_1_.6, f32[17,128,128]{2,1,0:T(8,128)S(1)} %get-tuple-element.39.refs_1_, f32[9,8,384]{2,1,0:T(8,128)S(1)} %collective-permute-done.refs_2_, ...), custom_call_target="tpu_custom_call" | custom-call | tf_op jit(solution)/shard_map/edges_kernel/pallas_call | solution.py:627
  44.3 0.5 all-to-all-done.refs_0_
  44.7 2.8 %package_kernel.2 = (f32[16,128]{1,0:T(8,128)}, f32[16,128]{1,0:T(8,128)}, f32[16,128]{1,0:T(8,128)}, f32[96,128]{1,0:T(8,128)}, f32[128,8,128]{2,1,0:T(8,128)}) custom-call(f32[128,8,128]{2,1,0:T(8,128)S(1)} %all-to-all-done.refs_0_, f32[32,4096]{1,0:T(8,128)} %get-tuple-element.44.refs_1_, f32[1,32,32]{2,1,0:T(8,128)} %refs_2_.5, f32[32,128]{1,0:T(8,128)} %bitcast.5, ...), custom_call_target="tpu_custom_call" | custom-call | tf_op jit(solution)/shard_map/package_kernel/pallas_call | solution.py:627
  47.5 11.0 %all-to-all-start.2 = ((f32[128,8,128]{2,1,0:T(8,128)}), f32[128,8,128]{2,1,0:T(8,128)S(1)}, u32[]{:S(2)}, u32[]{:S(2)}) async-start(f32[128,8,128]{2,1,0:T(8,128)} %get-tuple-element.47), calls=%async_computation.2 | async-start | bytes 1048576 | tf_op jit(solution)/shard_map/all_to_all | solution.py:641
  58.5 8.9 %second_kernel.1 = (f32[16,128,256]{2,1,0:T(8,128)}, f32[16,128]{1,0:T(8,128)S(1)}, f32[48,128]{1,0:T(8,128)}, f32[136,384]{1,0:T(8,128)}, f32[128,256]{1,0:T(8,...) custom-call(f32[16,128,256]{2,1,0:T(8,128)} %refs_1_.7, f32[128,256]{1,0:T(8,128)} %refs_1_.6, ...), custom_call_target="tpu_custom_call" | custom-call | tf_op jit(solution)/shard_map/second_kernel/pallas_call | solution.py:627
  67.5 3.9 %all-to-all-done.2.refs_0_ = f32[128,8,128]{2,1,0:T(8,128)S(1)} async-done(((f32[128,8,128]{2,1,0:T(8,128)}), f32[128,8,128]{2,1,0:T(8,128)S(1)}, u32[]{:S(2)}, u32[]{:S(2)}) %all-to-all-start.2) | async-done | bytes 524320 | tf_op jit(solution)/shard_map/all_to_all | solution.py:641
  71.3 2.7 %package_kernel.3 = (f32[16,128]{1,0:T(8,128)}, f32[16,128]{1,0:T(8,128)}, f32[16,128]{1,0:T(8,128)}, f32[96,128]{1,0:T(8,128)}, f32[128,4,128]{2,1,0:T(4,128)}) custom-call(f32[128,8,128]{2,1,0:T(8,128)S(1)} %all-to-all-done.2.refs_0_, f32[32,4096]{1,0:T(8,128)} %get-tuple-element.44.refs_1_, f32[1,32,32]{2,1,0:T(8,128)} %refs_2_.5, f32[32,128]{1,0:T(8,128)} %bitcast.6, ...), custom_call_target="tpu_custom_call" | custom-call | tf_op jit(solution)/shard_map/package_kernel/pallas_call | solution.py:627
  74.1 5.9 %all-to-all-start.3 = ((f32[128,4,128]{2,1,0:T(4,128)}), f32[128,4,128]{2,1,0:T(4,128)S(1)}, u32[]{:S(2)}, u32[]{:S(2)}) async-start(f32[128,4,128]{2,1,0:T(4,128)} %get-tuple-element.54), calls=%async_computation.3 | async-start | bytes 524288 | tf_op jit(solution)/shard_map/all_to_all | solution.py:641
  80.0 6.4 %third_kernel.1 = (f32[16,128,256]{2,1,0:T(8,128)}, f32[128,128]{1,0:T(8,128)S(1)}) custom-call(f32[16,136,384]{2,1,0:T(8,128)} %get-tuple-element.57.refs_0_, f32[16,128,256]{2,1,0:T(8,128)} %get-tuple-element.58.refs_1_.refs_7_, f32[136,384]{1,0:T(8,128)} %get-tuple-element.59.refs_2_, f32[128,256]{1,0:T(8,128)} %get-tuple-element.60.refs_3_, ...), custom_call_target="tpu_custom_call" | custom-call | tf_op jit(solution)/shard_map/third_kernel/pallas_call | solution.py:627
  86.4 4.0 %all-to-all-done.3.refs_0_ = f32[128,4,128]{2,1,0:T(4,128)S(1)} async-done(((f32[128,4,128]{2,1,0:T(4,128)}), f32[128,4,128]{2,1,0:T(4,128)S(1)}, u32[]{:S(2)}, u32[]{:S(2)}) %all-to-all-start.3) | async-done | bytes 262176 | tf_op jit(solution)/shard_map/all_to_all | solution.py:641
  90.5 0.0 copy-start
  90.5 0.0 copy-start.1
  90.5 0.0 copy-start.2
  90.5 0.0 copy-start.3
  90.5 0.0 copy-start.4
  90.5 2.7 %fourth_kernel.1 = (f32[128,1,128]{2,1,0:T(1,128)S(1)}, f32[16,128,256]{2,1,0:T(8,128)S(1)}, f32[16,128,256]{2,1,0:T(8,128)S(1)}) custom-call(f32[128,4,128]{2,1,0:T(4,128)S(1)} %all-to-all-done.3.refs_0_, f32[32,4096]{1,0:T(8,128)} %get-tuple-element.44.refs_1_, f32[32,128]{1,0:T(8,128)} %bitcast.7, f32[24,128]{1,0:T(8,128)} %get-tuple-element.45.refs_4_.refs_5_.refs_3_, ...), custom_call_target="tpu_custom_call" | custom-call | tf_op jit(solution)/shard_map/fourth_kernel/pallas_call | solution.py:627
  93.2 15.0 %all_to_all.25.refs_0_ = f32[128,1,128]{2,1,0:T(1,128)S(1)} all-to-all(f32[128,1,128]{2,1,0:T(1,128)S(1)} %get-tuple-element.67), channel_id=1, replica_groups=mesh['row_0'=2,'row_1'=4,'row_2'=2,'col_0'=4,'col_1'=2] {'row_0','row_1'..., dimensions={0} | all-to-all | bytes 131072 | tf_op jit(solution)/shard_map/all_to_all | solution.py:641
  108.3 0.0 copy-done
  108.3 0.0 copy-done.1
  108.3 0.0 copy-done.2
  108.3 0.0 copy-done.3
  108.3 0.0 copy-done.4
  108.3 2.4 %last_kernel.1 = (f32[16,128,256]{2,1,0:T(8,128)}, f32[16,32]{1,0:T(8,128)}) custom-call(f32[128,1,128]{2,1,0:T(1,128)S(1)} %all_to_all.25.refs_0_, f32[16,128,256]{2,1,0:T(8,128)S(1)} %copy-done, f32[136,384]{1,0:T(8,128)S(1)} %copy-done.1, f32[16,128,256]{2,1,0:T(8,128)S(1)} %get-tuple-element.68.refs_3_, f32[16,128,256]{2,1,0:T(8,128)S(1)} %get-tuple-element.69.refs_4_, ...), custom_call_target="tpu_custom_call" | custom-call | tf_op jit(solution)/shard_map/last_kernel/pallas_call | solution.py:627
Async XLA Ops:
  3.6 20.4 %all-to-all-start.1 = ((f32[8,184,128]{2,1,0:T(8,128)}), f32[8,184,128]{2,1,0:T(8,128)S(1)}, u32[]{:S(2)}, u32[]{:S(2)}) async-start(f32[8,184,128]{2,1,0:T(8,128)} %get-tuple-element.37), calls=%async_computation.1 | async-start | bytes 1507328 | tf_op jit(solution)/shard_map/all_to_all | solution.py:641
  24.0 20.7 %all-to-all-start = ((f32[128,8,128]{2,1,0:T(8,128)}), f32[128,8,128]{2,1,0:T(8,128)S(1)}, u32[]{:S(2)}, u32[]{:S(2)}) async-start(f32[128,8,128]{2,1,0:T(8,128)} %get-tuple-element.36), calls=%async_computation | async-start | bytes 1048576 | tf_op jit(solution)/shard_map/all_to_all | solution.py:641
  32.9 8.2 %collective-permute-start = (f32[9,8,384]{2,1,0:T(8,128)S(1)}, f32[9,8,384]{2,1,0:T(8,128)S(1)}, u32[]{:S(2)}, u32[]{:S(2)}) collective-permute-start(f32[9,8,384]{2,1,0:T(8,128)S(1)} %get-tuple-element.40), channel_id=1, source_target_pairs={{8,0},{16,8},{24,16},{32,24},{40,32},{48,40},{56,48},{64,56},{72,6... | collective-permute-start | bytes 331784 | tf_op jit(solution)/shard_map/ppermute | solution.py:675
  35.9 5.7 %collective-permute-start.1 = (f32[9,8,384]{2,1,0:T(8,128)S(1)}, f32[9,8,384]{2,1,0:T(8,128)S(1)}, u32[]{:S(2)}, u32[]{:S(2)}) collective-permute-start(f32[9,8,384]{2,1,0:T(8,128)S(1)} %get-tuple-element.41), channel_id=1, source_target_pairs={{0,8},{8,16},{16,24},{24,32},{32,40},{40,48},{48,56},{56,64},{64,7... | collective-permute-start | bytes 331784 | tf_op jit(solution)/shard_map/ppermute | solution.py:676
  47.5 23.8 %all-to-all-start.2 = ((f32[128,8,128]{2,1,0:T(8,128)}), f32[128,8,128]{2,1,0:T(8,128)S(1)}, u32[]{:S(2)}, u32[]{:S(2)}) async-start(f32[128,8,128]{2,1,0:T(8,128)} %get-tuple-element.47), calls=%async_computation.2 | async-start | bytes 1048576 | tf_op jit(solution)/shard_map/all_to_all | solution.py:641
  74.1 16.4 %all-to-all-start.3 = ((f32[128,4,128]{2,1,0:T(4,128)}), f32[128,4,128]{2,1,0:T(4,128)S(1)}, u32[]{:S(2)}, u32[]{:S(2)}) async-start(f32[128,4,128]{2,1,0:T(4,128)} %get-tuple-element.54), calls=%async_computation.3 | async-start | bytes 524288 | tf_op jit(solution)/shard_map/all_to_all | solution.py:641
  90.5 17.8 %copy-start = (f32[16,128,256]{2,1,0:T(8,128)S(1)}, f32[16,128,256]{2,1,0:T(8,128)}, u32[]{:S(2)}) copy-start(f32[16,128,256]{2,1,0:T(8,128)} %refs_1_.7) | copy-start | bytes 6291460
  90.5 17.8 %copy-start.1 = (f32[136,384]{1,0:T(8,128)S(1)}, f32[136,384]{1,0:T(8,128)}, u32[]{:S(2)}) copy-start(f32[136,384]{1,0:T(8,128)} %get-tuple-element.59.refs_2_) | copy-start | bytes 626692
  90.5 17.8 %copy-start.2 = (f32[16,128]{1,0:T(8,128)S(1)}, f32[16,128]{1,0:T(8,128)}, u32[]{:S(2)}) copy-start(f32[16,128]{1,0:T(8,128)} %get-tuple-element.46.refs_6_.refs_7_.refs_5_) | copy-start | bytes 24580
  90.5 17.8 %copy-start.3 = (f32[16,128]{1,0:T(8,128)S(1)}, f32[16,128]{1,0:T(8,128)}, u32[]{:S(2)}) copy-start(f32[16,128]{1,0:T(8,128)} %get-tuple-element.51.refs_8_.refs_6_) | copy-start | bytes 24580
  90.5 17.8 %copy-start.4 = (f32[16,128]{1,0:T(8,128)S(1)}, f32[16,128]{1,0:T(8,128)}, u32[]{:S(2)}) copy-start(f32[16,128]{1,0:T(8,128)} %get-tuple-element.55.refs_6_.refs_4_.refs_7_) | copy-start | bytes 24580

commit v5 on v4

--- a/solution.py
+++ b/solution.py
@@ -106,12 +106,22 @@
     ]
     for c in copies:
         c.start()
-    for c in copies:
-        c.wait()
+    return copies
 
 
 def load_kernel(mv, b_ref, sh_ref, p_ref, msg_hbm, edge_ref, z_ref, sems):
     _, j = where_am_i()
+    mv.wait(2)
+    rows = [
+        pltpu.make_async_copy(
+            p_ref.at[:, :, 128 * t : 128 * (t + 1)],
+            msg_hbm.at[:, 32 * t : 32 * (t + 1), :],
+            sems.at[t],
+        )
+        for t in range(4)
+    ]
+    for c in rows:
+        c.start()
     lane = iota((TR, 128), 1)
     z = jnp.zeros((TR, 128), jnp.float32)
     mv.wait(1)
@@ -126,17 +136,6 @@
         edge_ref[k, 0:8, :] = src[0:8, :]
         edge_ref[k, 8:16, :] = src[TR - 8 : TR, :]
     mv.flush(1)
-    mv.wait(2)
-    rows = [
-        pltpu.make_async_copy(
-            p_ref.at[:, :, 128 * t : 128 * (t + 1)],
-            msg_hbm.at[:, 32 * t : 32 * (t + 1), :],
-            sems.at[t],
-        )
-        for t in range(4)
-    ]
-    for c in rows:
-        c.start()
     z_ref[...] = z.T
     side = lambda at, to, n: pltpu.make_async_copy(
         z_ref.at[at : at + HROWS, :], msg_hbm.at[to, 128 : 128 + HROWS, :], sems.at[n]
@@ -206,7 +205,8 @@
     v0p = padded(pad_ref, dot_nt(bp_ref[...], m_ref[0]))
     v0p_ref[...] = v0p
     mv.flush(2)
-    send(msg_hbm, pay_ref, sems, pack(v0p, gather_bumps(s_ref)))
+    for c in send(msg_hbm, pay_ref, sems, pack(v0p, gather_bumps(s_ref))):
+        c.wait()
 
 
 def columns_kernel(mv, g1_ref, edge_ref, w_ref, up_ref, dn_ref, y_ref, ext_ref):
@@ -338,7 +338,6 @@
         for t in range(4):
             c = 4 * d + t
             pm_ref[:, 128 * c : 128 * (c + 1)] = g1_ref[d, 32 * t : 32 * (t + 1), :]
-    mv.flush(3)
     first = iota((8, EC), 0) < 4
     for p in range(PAIRS):
         bot, top = bot_ref[p], top_ref[p]
@@ -395,13 +394,15 @@
     if step == 2:
         out = out - vp
     vd = bump_ref[0:K, :] - const_ref[K + 1 : K + 2, :] * at_tile(v_ref, i, j)
+    sent = send(msg_hbm, pay_ref, sems, pack(out, vd) if step == 1 else pack_package(out))
     y_ref[...] = y
     out_ref[...] = out
     vd_ref[...] = vd
     around(v_ref, x_ref, i)
     for n in range(4):
         mv.flush(n)
-    send(msg_hbm, pay_ref, sems, pack(out, vd) if step == 1 else pack_package(out))
+    for c in sent:
+        c.wait()
 
 
 def at_tile(v_ref, i, j):
@@ -506,7 +507,7 @@
     for c in loads:
         c.start()
     package_only(g_ref, v_ref)
-    for n in range(1, 6):
+    for n in range(2, 6):
         mv.wait(n)
     wp = wp_ref[...]
     y = padded(pad_ref, dot_nt(v_ref[...], pm_ref[...])) + own_conductance(cond_ref, i, j) * wp
@@ -679,7 +680,7 @@
         [(sh, "h"), (side, "v"), (bot, "v"), (top, "v"), (cm, "h"), (g1, "v"), (bump1, "h")],
         [
             (f32(PLANES, TR, 128), "r"), (f32(PLANES, 8, EC), "h"), (f32(K + 8, 128), "h"),
-            (f32(OWN, NB), "h"),
+            (f32(OWN, NB), "v"),
         ],
         [vm(K, 4 * TC), vm(K, 512), pltpu.SemaphoreType.DMA((1,))],
     )
@@ -687,7 +688,7 @@
     results = [(small, "h"), (small, "h"), (small, "h"), (lattice, "h")]
     v1p, _, y1, near, msg = call(
         functools.partial(package_kernel, 1),
-        [(g, "v"), (pm, "h"), (m, "h"), (cond, "h"), (bump1, "h"), (bump1, "h"), (v0p, "h")],
+        [(g, "v"), (pm, "v"), (m, "h"), (cond, "h"), (bump1, "h"), (bump1, "h"), (v0p, "h")],
         results + [(gathered, "r")],
         step + payload,
     )
@@ -703,7 +704,7 @@
     )
     wp, wd, y2, near, msg = call(
         functools.partial(package_kernel, 2),
-        [(g, "v"), (pm, "h"), (m, "h"), (cond, "h"), (bump2, "v"), (bump1, "h"), (v1p, "h")],
+        [(g, "v"), (pm, "v"), (m, "h"), (cond, "h"), (bump2, "v"), (bump1, "h"), (v1p, "h")],
         results + [(f32(128, 4, 128), "r")],
         step + alone,
     )
@@ -716,7 +717,7 @@
     )
     msg, v1, w = call(
         fourth_kernel,
-        [(g, "v")] + [(x, "h") for x in (pm, cond, bump1, wp, wd)] + [(r, "v"), (v1, "r"), (w, "r")],
+        [(g, "v"), (pm, "v")] + [(x, "h") for x in (cond, bump1, wp, wd)] + [(r, "v"), (v1, "r"), (w, "r")],
         [(f32(128, 1, 128), "v"), (die, "v"), (die, "v")],
         [vm(K, NB), vm(K, 128), vm(128, 128), pltpu.SemaphoreType.DMA((2,))],
     )

time: 111 us -> 111 us (level)
  no operation moved by 1% of the time
where the time goes in v5:
time: 111 us; the launch traced here: 110 us
  starting transfers between devices  38 us (34%)
  Pallas kernels  37.9 us (34%)
  waiting for transfers between devices  18.1 us (16%)
  blocking collectives  15 us (14%)
    pallas_call x10, Pallas kernels, call(): pl.pallas_call(wrapped, out_shape=tuple((x if m == 'v' else pltpu.HBM(x.s...  37.9 us
    all_to_all x4, starting transfers between devices, swapped(): return lax.all_to_all(x, axes, 0, 0, tiled=True)  32.4 us
    all_to_all x4, waiting for transfers between devices, swapped(): return lax.all_to_all(x, axes, 0, 0, tiled=True)  15.1 us
    all_to_all x1, blocking collectives, swapped(): return lax.all_to_all(x, axes, 0, 0, tiled=True)  15 us
    ppermute x1, starting transfers between devices, body(): bot = lax.ppermute(up, ROW, [(r + 1, r) for r in range(n - 1)])  2.98 us
    ppermute x1, waiting for transfers between devices, body(): bot = lax.ppermute(up, ROW, [(r + 1, r) for r in range(n - 1)])  2.62 us
    ppermute x1, starting transfers between devices, body(): top = lax.ppermute(dn, ROW, [(r, r + 1) for r in range(n - 1)])  2.61 us
  transfers between devices with their start and end apart: 6, of which 6 were waited for; matrix products, arithmetic and copies ran while one was open for 0% of the time, Pallas kernels for 23%

profile of v5, /device:TPU:1, one launch (start us, length us, event | category | flops | bytes accessed | tf_op | source)
XLA Modules:
  0.0 109.9 jit_solution(2730947625386826438)
XLA Ops:
  0.6 2.9 %load_kernel.1 = (f32[8,184,128]{2,1,0:T(8,128)}, f32[17,16,256]{2,1,0:T(8,128)}) custom-call(f32[16,128,256]{2,1,0:T(8,128)} %refs_1_.7, f32[128,256]{1,0:T(8,128)} %refs_1_.6, f32[8,32,512]{2,1,0:T(8,128)} %bitcast.3), custom_call_target="tpu_custom_call" | custom-call | tf_op jit(solution)/shard_map/load_kernel/pallas_call | solution.py:628
  3.5 7.5 %all-to-all-start.1 = ((f32[8,184,128]{2,1,0:T(8,128)}), f32[8,184,128]{2,1,0:T(8,128)S(1)}, u32[]{:S(2)}, u32[]{:S(2)}) async-start(f32[8,184,128]{2,1,0:T(8,128)} %get-tuple-element.37), calls=%async_computation.1 | async-start | bytes 1507328 | tf_op jit(solution)/shard_map/all_to_all | solution.py:642
  11.0 6.1 %start_kernel.1 = (f32[128,8,128]{2,1,0:T(8,128)}, f32[136,384]{1,0:T(8,128)}, f32[16,128]{1,0:T(8,128)}, f32[24,128]{1,0:T(8,128)}) custom-call(f32[16,128,256]{2,1,0:T(8,128)} %refs_1_.7, f32[128,256]{1,0:T(8,128)} %refs_1_.6, f32[16,32]{1,0:T(8,128)} %refs_6_.1, f32[1,32,32]{2,1,0:T(8,128)} %refs_2_.5, s32[32,128]{1,0:T(8,128)} %bitcast.8, f32[32,128]{1,0:T(8,128)} %bitcast.4), custom_call_target="tpu_custom_call" | custom-call | tf_op jit(solution)/shard_map/start_kernel/pallas_call | solution.py:628
  17.1 6.8 %all-to-all-done.1.refs_0_.refs_5_ = f32[8,184,128]{2,1,0:T(8,128)S(1)} async-done(((f32[8,184,128]{2,1,0:T(8,128)}), f32[8,184,128]{2,1,0:T(8,128)S(1)}, u32[]{:S(2)}, u32[]{:S(2)}) %all-to-all-start.1) | async-done | bytes 753696 | tf_op jit(solution)/shard_map/all_to_all | solution.py:642
  23.9 7.9 %all-to-all-start = ((f32[128,8,128]{2,1,0:T(8,128)}), f32[128,8,128]{2,1,0:T(8,128)S(1)}, u32[]{:S(2)}, u32[]{:S(2)}) async-start(f32[128,8,128]{2,1,0:T(8,128)} %get-tuple-element.36), calls=%async_computation | async-start | bytes 1048576 | tf_op jit(solution)/shard_map/all_to_all | solution.py:642
  31.8 1.0 columns_kernel.1
  32.8 3.0 %collective-permute-start = (f32[9,8,384]{2,1,0:T(8,128)S(1)}, f32[9,8,384]{2,1,0:T(8,128)S(1)}, u32[]{:S(2)}, u32[]{:S(2)}) collective-permute-start(f32[9,8,384]{2,1,0:T(8,128)S(1)} %get-tuple-element.40), channel_id=1, source_target_pairs={{8,0},{16,8},{24,16},{32,24},{40,32},{48,40},{56,48},{64,56},{72,6... | collective-permute-start | bytes 331784 | tf_op jit(solution)/shard_map/ppermute | solution.py:676
  35.8 2.6 %collective-permute-start.1 = (f32[9,8,384]{2,1,0:T(8,128)S(1)}, f32[9,8,384]{2,1,0:T(8,128)S(1)}, u32[]{:S(2)}, u32[]{:S(2)}) collective-permute-start(f32[9,8,384]{2,1,0:T(8,128)S(1)} %get-tuple-element.41), channel_id=1, source_target_pairs={{0,8},{8,16},{16,24},{24,32},{32,40},{40,48},{48,56},{56,64},{64,7... | collective-permute-start | bytes 331784 | tf_op jit(solution)/shard_map/ppermute | solution.py:677
  38.4 2.6 %collective-permute-done.refs_2_ = f32[9,8,384]{2,1,0:T(8,128)S(1)} collective-permute-done((f32[9,8,384]{2,1,0:T(8,128)S(1)}, f32[9,8,384]{2,1,0:T(8,128)S(1)}, u32[]{:S(2)}, u32[]{:S(2)}) %collective-permute-start) | collective-permute-done | bytes 110624 | tf_op jit(solution)/shard_map/ppermute | solution.py:676
  41.0 0.4 collective-permute-done.1.refs_3_
  41.4 2.7 %edges_kernel.1 = (f32[17,128,128]{2,1,0:T(8,128)}, f32[17,8,384]{2,1,0:T(8,128)}, f32[24,128]{1,0:T(8,128)}, f32[32,4096]{1,0:T(8,128)S(1)}) custom-call(f32[128,256]{1,0:T(8,128)} %refs_1_.6, f32[17,128,128]{2,1,0:T(8,128)S(1)} %get-tuple-element.39.refs_1_, f32[9,8,384]{2,1,0:T(8,128)S(1)} %collective-permute-done.refs_2_, ...), custom_call_target="tpu_custom_call" | custom-call | tf_op jit(solution)/shard_map/edges_kernel/pallas_call | solution.py:628
  44.1 0.5 all-to-all-done.refs_0_
  44.6 2.5 %package_kernel.2 = (f32[16,128]{1,0:T(8,128)}, f32[16,128]{1,0:T(8,128)}, f32[16,128]{1,0:T(8,128)}, f32[96,128]{1,0:T(8,128)}, f32[128,8,128]{2,1,0:T(8,128)}) custom-call(f32[128,8,128]{2,1,0:T(8,128)S(1)} %all-to-all-done.refs_0_, f32[32,4096]{1,0:T(8,128)S(1)} %get-tuple-element.44.refs_1_, f32[1,32,32]{2,1,0:T(8,128)} %refs_2_.5, f32[32,128]{1,0:T(8,128)} %bitcast.5, ...), custom_call_target="tpu_custom_call" | custom-call | tf_op jit(solution)/shard_map/package_kernel/pallas_call | solution.py:628
  47.1 11.0 %all-to-all-start.2 = ((f32[128,8,128]{2,1,0:T(8,128)}), f32[128,8,128]{2,1,0:T(8,128)S(1)}, u32[]{:S(2)}, u32[]{:S(2)}) async-start(f32[128,8,128]{2,1,0:T(8,128)} %get-tuple-element.47), calls=%async_computation.2 | async-start | bytes 1048576 | tf_op jit(solution)/shard_map/all_to_all | solution.py:642
  58.2 8.9 %second_kernel.1 = (f32[16,128,256]{2,1,0:T(8,128)}, f32[16,128]{1,0:T(8,128)S(1)}, f32[48,128]{1,0:T(8,128)}, f32[136,384]{1,0:T(8,128)}, f32[128,256]{1,0:T(8,...) custom-call(f32[16,128,256]{2,1,0:T(8,128)} %refs_1_.7, f32[128,256]{1,0:T(8,128)} %refs_1_.6, ...), custom_call_target="tpu_custom_call" | custom-call | tf_op jit(solution)/shard_map/second_kernel/pallas_call | solution.py:628
  67.1 3.9 %all-to-all-done.2.refs_0_ = f32[128,8,128]{2,1,0:T(8,128)S(1)} async-done(((f32[128,8,128]{2,1,0:T(8,128)}), f32[128,8,128]{2,1,0:T(8,128)S(1)}, u32[]{:S(2)}, u32[]{:S(2)}) %all-to-all-start.2) | async-done | bytes 524320 | tf_op jit(solution)/shard_map/all_to_all | solution.py:642
  70.9 2.4 %package_kernel.3 = (f32[16,128]{1,0:T(8,128)}, f32[16,128]{1,0:T(8,128)}, f32[16,128]{1,0:T(8,128)}, f32[96,128]{1,0:T(8,128)}, f32[128,4,128]{2,1,0:T(4,128)}) custom-call(f32[128,8,128]{2,1,0:T(8,128)S(1)} %all-to-all-done.2.refs_0_, f32[32,4096]{1,0:T(8,128)S(1)} %get-tuple-element.44.refs_1_, f32[1,32,32]{2,1,0:T(8,128)} %refs_2_.5, f32[32,128]{1,0:T(8,128)} %bitcast.6, ...), custom_call_target="tpu_custom_call" | custom-call | tf_op jit(solution)/shard_map/package_kernel/pallas_call | solution.py:628
  73.4 5.9 %all-to-all-start.3 = ((f32[128,4,128]{2,1,0:T(4,128)}), f32[128,4,128]{2,1,0:T(4,128)S(1)}, u32[]{:S(2)}, u32[]{:S(2)}) async-start(f32[128,4,128]{2,1,0:T(4,128)} %get-tuple-element.54), calls=%async_computation.3 | async-start | bytes 524288 | tf_op jit(solution)/shard_map/all_to_all | solution.py:642
  79.3 6.4 %third_kernel.1 = (f32[16,128,256]{2,1,0:T(8,128)}, f32[128,128]{1,0:T(8,128)S(1)}) custom-call(f32[16,136,384]{2,1,0:T(8,128)} %get-tuple-element.57.refs_0_, f32[16,128,256]{2,1,0:T(8,128)} %get-tuple-element.58.refs_1_.refs_7_, f32[136,384]{1,0:T(8,128)} %get-tuple-element.59.refs_2_, f32[128,256]{1,0:T(8,128)} %get-tuple-element.60.refs_3_, ...), custom_call_target="tpu_custom_call" | custom-call | tf_op jit(solution)/shard_map/third_kernel/pallas_call | solution.py:628
  85.8 4.0 %all-to-all-done.3.refs_0_ = f32[128,4,128]{2,1,0:T(4,128)S(1)} async-done(((f32[128,4,128]{2,1,0:T(4,128)}), f32[128,4,128]{2,1,0:T(4,128)S(1)}, u32[]{:S(2)}, u32[]{:S(2)}) %all-to-all-start.3) | async-done | bytes 262176 | tf_op jit(solution)/shard_map/all_to_all | solution.py:642
  89.8 0.0 copy-start
  89.8 0.0 copy-start.1
  89.8 0.0 copy-start.2
  89.8 0.0 copy-start.3
  89.8 0.0 copy-start.4
  89.8 2.6 %fourth_kernel.1 = (f32[128,1,128]{2,1,0:T(1,128)S(1)}, f32[16,128,256]{2,1,0:T(8,128)S(1)}, f32[16,128,256]{2,1,0:T(8,128)S(1)}) custom-call(f32[128,4,128]{2,1,0:T(4,128)S(1)} %all-to-all-done.3.refs_0_, f32[32,4096]{1,0:T(8,128)S(1)} %get-tuple-element.44.refs_1_, f32[32,128]{1,0:T(8,128)} %bitcast.7, ...), custom_call_target="tpu_custom_call" | custom-call | tf_op jit(solution)/shard_map/fourth_kernel/pallas_call | solution.py:628
  92.4 15.0 %all_to_all.25.refs_0_ = f32[128,1,128]{2,1,0:T(1,128)S(1)} all-to-all(f32[128,1,128]{2,1,0:T(1,128)S(1)} %get-tuple-element.67), channel_id=1, replica_groups=mesh['row_0'=2,'row_1'=4,'row_2'=2,'col_0'=4,'col_1'=2] {'row_0','row_1'..., dimensions={0} | all-to-all | bytes 131072 | tf_op jit(solution)/shard_map/all_to_all | solution.py:642
  107.5 0.0 copy-done
  107.5 0.0 copy-done.1
  107.5 0.0 copy-done.2
  107.5 0.0 copy-done.3
  107.5 0.0 copy-done.4
  107.5 2.4 %last_kernel.1 = (f32[16,128,256]{2,1,0:T(8,128)}, f32[16,32]{1,0:T(8,128)}) custom-call(f32[128,1,128]{2,1,0:T(1,128)S(1)} %all_to_all.25.refs_0_, f32[16,128,256]{2,1,0:T(8,128)S(1)} %copy-done, f32[136,384]{1,0:T(8,128)S(1)} %copy-done.1, f32[16,128,256]{2,1,0:T(8,128)S(1)} %get-tuple-element.68.refs_3_, f32[16,128,256]{2,1,0:T(8,128)S(1)} %get-tuple-element.69.refs_4_, ...), custom_call_target="tpu_custom_call" | custom-call | tf_op jit(solution)/shard_map/last_kernel/pallas_call | solution.py:628
Async XLA Ops:
  3.5 20.4 %all-to-all-start.1 = ((f32[8,184,128]{2,1,0:T(8,128)}), f32[8,184,128]{2,1,0:T(8,128)S(1)}, u32[]{:S(2)}, u32[]{:S(2)}) async-start(f32[8,184,128]{2,1,0:T(8,128)} %get-tuple-element.37), calls=%async_computation.1 | async-start | bytes 1507328 | tf_op jit(solution)/shard_map/all_to_all | solution.py:642
  23.9 20.7 %all-to-all-start = ((f32[128,8,128]{2,1,0:T(8,128)}), f32[128,8,128]{2,1,0:T(8,128)S(1)}, u32[]{:S(2)}, u32[]{:S(2)}) async-start(f32[128,8,128]{2,1,0:T(8,128)} %get-tuple-element.36), calls=%async_computation | async-start | bytes 1048576 | tf_op jit(solution)/shard_map/all_to_all | solution.py:642
  32.8 8.2 %collective-permute-start = (f32[9,8,384]{2,1,0:T(8,128)S(1)}, f32[9,8,384]{2,1,0:T(8,128)S(1)}, u32[]{:S(2)}, u32[]{:S(2)}) collective-permute-start(f32[9,8,384]{2,1,0:T(8,128)S(1)} %get-tuple-element.40), channel_id=1, source_target_pairs={{8,0},{16,8},{24,16},{32,24},{40,32},{48,40},{56,48},{64,56},{72,6... | collective-permute-start | bytes 331784 | tf_op jit(solution)/shard_map/ppermute | solution.py:676
  35.8 5.7 %collective-permute-start.1 = (f32[9,8,384]{2,1,0:T(8,128)S(1)}, f32[9,8,384]{2,1,0:T(8,128)S(1)}, u32[]{:S(2)}, u32[]{:S(2)}) collective-permute-start(f32[9,8,384]{2,1,0:T(8,128)S(1)} %get-tuple-element.41), channel_id=1, source_target_pairs={{0,8},{8,16},{16,24},{24,32},{32,40},{40,48},{48,56},{56,64},{64,7... | collective-permute-start | bytes 331784 | tf_op jit(solution)/shard_map/ppermute | solution.py:677
  47.1 23.8 %all-to-all-start.2 = ((f32[128,8,128]{2,1,0:T(8,128)}), f32[128,8,128]{2,1,0:T(8,128)S(1)}, u32[]{:S(2)}, u32[]{:S(2)}) async-start(f32[128,8,128]{2,1,0:T(8,128)} %get-tuple-element.47), calls=%async_computation.2 | async-start | bytes 1048576 | tf_op jit(solution)/shard_map/all_to_all | solution.py:642
  73.4 16.4 %all-to-all-start.3 = ((f32[128,4,128]{2,1,0:T(4,128)}), f32[128,4,128]{2,1,0:T(4,128)S(1)}, u32[]{:S(2)}, u32[]{:S(2)}) async-start(f32[128,4,128]{2,1,0:T(4,128)} %get-tuple-element.54), calls=%async_computation.3 | async-start | bytes 524288 | tf_op jit(solution)/shard_map/all_to_all | solution.py:642
  89.8 17.7 %copy-start = (f32[16,128,256]{2,1,0:T(8,128)S(1)}, f32[16,128,256]{2,1,0:T(8,128)}, u32[]{:S(2)}) copy-start(f32[16,128,256]{2,1,0:T(8,128)} %refs_1_.7) | copy-start | bytes 6291460
  89.8 17.7 %copy-start.1 = (f32[136,384]{1,0:T(8,128)S(1)}, f32[136,384]{1,0:T(8,128)}, u32[]{:S(2)}) copy-start(f32[136,384]{1,0:T(8,128)} %get-tuple-element.59.refs_2_) | copy-start | bytes 626692
  89.8 17.7 %copy-start.2 = (f32[16,128]{1,0:T(8,128)S(1)}, f32[16,128]{1,0:T(8,128)}, u32[]{:S(2)}) copy-start(f32[16,128]{1,0:T(8,128)} %get-tuple-element.46.refs_6_.refs_7_.refs_5_) | copy-start | bytes 24580
  89.8 17.7 %copy-start.3 = (f32[16,128]{1,0:T(8,128)S(1)}, f32[16,128]{1,0:T(8,128)}, u32[]{:S(2)}) copy-start(f32[16,128]{1,0:T(8,128)} %get-tuple-element.51.refs_8_.refs_6_) | copy-start | bytes 24580
  89.8 17.7 %copy-start.4 = (f32[16,128]{1,0:T(8,128)S(1)}, f32[16,128]{1,0:T(8,128)}, u32[]{:S(2)}) copy-start(f32[16,128]{1,0:T(8,128)} %get-tuple-element.55.refs_6_.refs_4_.refs_7_) | copy-start | bytes 24580

commit v6 on v5

--- a/solution.py
+++ b/solution.py
@@ -261,7 +261,7 @@
         v_ref[8:16, at] = hi
         return carry
 
-    lax.fori_loop(0, NB // 128, one, 0, unroll=4)
+    lax.fori_loop(0, NB // 128, one, 0, unroll=16)
 
 
 def package_only(g_ref, v_ref):
@@ -278,7 +278,7 @@
             v_ref[4 * m : 4 * m + 4, at] = out
         return carry
 
-    lax.fori_loop(0, NB // 128, one, 0, unroll=4)
+    lax.fori_loop(0, NB // 128, one, 0, unroll=16)
 
 
 def own_die(g_ref, i, j):

time: 111 us -> 111 us (level)
  no operation moved by 1% of the time
where the time goes in v6:
time: 111 us; the launch traced here: 110 us
  Pallas kernels  37.9 us (34%)
  starting transfers between devices  37.9 us (34%)
  waiting for transfers between devices  18.1 us (16%)
  blocking collectives  15 us (14%)
    pallas_call x10, Pallas kernels, call(): pl.pallas_call(wrapped, out_shape=tuple((x if m == 'v' else pltpu.HBM(x.s...  37.9 us
    all_to_all x4, starting transfers between devices, swapped(): return lax.all_to_all(x, axes, 0, 0, tiled=True)  32.4 us
    all_to_all x4, waiting for transfers between devices, swapped(): return lax.all_to_all(x, axes, 0, 0, tiled=True)  15.1 us
    all_to_all x1, blocking collectives, swapped(): return lax.all_to_all(x, axes, 0, 0, tiled=True)  15 us
    ppermute x1, starting transfers between devices, body(): bot = lax.ppermute(up, ROW, [(r + 1, r) for r in range(n - 1)])  2.98 us
    ppermute x1, waiting for transfers between devices, body(): bot = lax.ppermute(up, ROW, [(r + 1, r) for r in range(n - 1)])  2.62 us
    ppermute x1, starting transfers between devices, body(): top = lax.ppermute(dn, ROW, [(r, r + 1) for r in range(n - 1)])  2.61 us
  transfers between devices with their start and end apart: 6, of which 6 were waited for; matrix products, arithmetic and copies ran while one was open for 0% of the time, Pallas kernels for 23%

profile of v6, /device:TPU:1, one launch (start us, length us, event | category | flops | bytes accessed | tf_op | source)
XLA Modules:
  0.0 109.8 jit_solution(10793511461390705505)
XLA Ops:
  0.6 2.9 %load_kernel.1 = (f32[8,184,128]{2,1,0:T(8,128)}, f32[17,16,256]{2,1,0:T(8,128)}) custom-call(f32[16,128,256]{2,1,0:T(8,128)} %refs_1_.7, f32[128,256]{1,0:T(8,128)} %refs_1_.6, f32[8,32,512]{2,1,0:T(8,128)} %bitcast.3), custom_call_target="tpu_custom_call" | custom-call | tf_op jit(solution)/shard_map/load_kernel/pallas_call | solution.py:628
  3.5 7.5 %all-to-all-start.1 = ((f32[8,184,128]{2,1,0:T(8,128)}), f32[8,184,128]{2,1,0:T(8,128)S(1)}, u32[]{:S(2)}, u32[]{:S(2)}) async-start(f32[8,184,128]{2,1,0:T(8,128)} %get-tuple-element.37), calls=%async_computation.1 | async-start | bytes 1507328 | tf_op jit(solution)/shard_map/all_to_all | solution.py:642
  11.0 6.1 %start_kernel.1 = (f32[128,8,128]{2,1,0:T(8,128)}, f32[136,384]{1,0:T(8,128)}, f32[16,128]{1,0:T(8,128)}, f32[24,128]{1,0:T(8,128)}) custom-call(f32[16,128,256]{2,1,0:T(8,128)} %refs_1_.7, f32[128,256]{1,0:T(8,128)} %refs_1_.6, f32[16,32]{1,0:T(8,128)} %refs_6_.1, f32[1,32,32]{2,1,0:T(8,128)} %refs_2_.5, s32[32,128]{1,0:T(8,128)} %bitcast.8, f32[32,128]{1,0:T(8,128)} %bitcast.4), custom_call_target="tpu_custom_call" | custom-call | tf_op jit(solution)/shard_map/start_kernel/pallas_call | solution.py:628
  17.1 6.8 %all-to-all-done.1.refs_0_.refs_5_ = f32[8,184,128]{2,1,0:T(8,128)S(1)} async-done(((f32[8,184,128]{2,1,0:T(8,128)}), f32[8,184,128]{2,1,0:T(8,128)S(1)}, u32[]{:S(2)}, u32[]{:S(2)}) %all-to-all-start.1) | async-done | bytes 753696 | tf_op jit(solution)/shard_map/all_to_all | solution.py:642
  23.9 7.9 %all-to-all-start = ((f32[128,8,128]{2,1,0:T(8,128)}), f32[128,8,128]{2,1,0:T(8,128)S(1)}, u32[]{:S(2)}, u32[]{:S(2)}) async-start(f32[128,8,128]{2,1,0:T(8,128)} %get-tuple-element.36), calls=%async_computation | async-start | bytes 1048576 | tf_op jit(solution)/shard_map/all_to_all | solution.py:642
  31.8 1.0 columns_kernel.1
  32.8 3.0 %collective-permute-start = (f32[9,8,384]{2,1,0:T(8,128)S(1)}, f32[9,8,384]{2,1,0:T(8,128)S(1)}, u32[]{:S(2)}, u32[]{:S(2)}) collective-permute-start(f32[9,8,384]{2,1,0:T(8,128)S(1)} %get-tuple-element.40), channel_id=1, source_target_pairs={{8,0},{16,8},{24,16},{32,24},{40,32},{48,40},{56,48},{64,56},{72,6... | collective-permute-start | bytes 331784 | tf_op jit(solution)/shard_map/ppermute | solution.py:676
  35.8 2.6 %collective-permute-start.1 = (f32[9,8,384]{2,1,0:T(8,128)S(1)}, f32[9,8,384]{2,1,0:T(8,128)S(1)}, u32[]{:S(2)}, u32[]{:S(2)}) collective-permute-start(f32[9,8,384]{2,1,0:T(8,128)S(1)} %get-tuple-element.41), channel_id=1, source_target_pairs={{0,8},{8,16},{16,24},{24,32},{32,40},{40,48},{48,56},{56,64},{64,7... | collective-permute-start | bytes 331784 | tf_op jit(solution)/shard_map/ppermute | solution.py:677
  38.4 2.6 %collective-permute-done.refs_2_ = f32[9,8,384]{2,1,0:T(8,128)S(1)} collective-permute-done((f32[9,8,384]{2,1,0:T(8,128)S(1)}, f32[9,8,384]{2,1,0:T(8,128)S(1)}, u32[]{:S(2)}, u32[]{:S(2)}) %collective-permute-start) | collective-permute-done | bytes 110624 | tf_op jit(solution)/shard_map/ppermute | solution.py:676
  41.0 0.4 collective-permute-done.1.refs_3_
  41.4 2.7 %edges_kernel.1 = (f32[17,128,128]{2,1,0:T(8,128)}, f32[17,8,384]{2,1,0:T(8,128)}, f32[24,128]{1,0:T(8,128)}, f32[32,4096]{1,0:T(8,128)S(1)}) custom-call(f32[128,256]{1,0:T(8,128)} %refs_1_.6, f32[17,128,128]{2,1,0:T(8,128)S(1)} %get-tuple-element.39.refs_1_, f32[9,8,384]{2,1,0:T(8,128)S(1)} %collective-permute-done.refs_2_, ...), custom_call_target="tpu_custom_call" | custom-call | tf_op jit(solution)/shard_map/edges_kernel/pallas_call | solution.py:628
  44.1 0.5 all-to-all-done.refs_0_
  44.6 2.5 %package_kernel.2 = (f32[16,128]{1,0:T(8,128)}, f32[16,128]{1,0:T(8,128)}, f32[16,128]{1,0:T(8,128)}, f32[96,128]{1,0:T(8,128)}, f32[128,8,128]{2,1,0:T(8,128)}) custom-call(f32[128,8,128]{2,1,0:T(8,128)S(1)} %all-to-all-done.refs_0_, f32[32,4096]{1,0:T(8,128)S(1)} %get-tuple-element.44.refs_1_, f32[1,32,32]{2,1,0:T(8,128)} %refs_2_.5, f32[32,128]{1,0:T(8,128)} %bitcast.5, ...), custom_call_target="tpu_custom_call" | custom-call | tf_op jit(solution)/shard_map/package_kernel/pallas_call | solution.py:628
  47.1 11.0 %all-to-all-start.2 = ((f32[128,8,128]{2,1,0:T(8,128)}), f32[128,8,128]{2,1,0:T(8,128)S(1)}, u32[]{:S(2)}, u32[]{:S(2)}) async-start(f32[128,8,128]{2,1,0:T(8,128)} %get-tuple-element.47), calls=%async_computation.2 | async-start | bytes 1048576 | tf_op jit(solution)/shard_map/all_to_all | solution.py:642
  58.2 8.9 %second_kernel.1 = (f32[16,128,256]{2,1,0:T(8,128)}, f32[16,128]{1,0:T(8,128)S(1)}, f32[48,128]{1,0:T(8,128)}, f32[136,384]{1,0:T(8,128)}, f32[128,256]{1,0:T(8,...) custom-call(f32[16,128,256]{2,1,0:T(8,128)} %refs_1_.7, f32[128,256]{1,0:T(8,128)} %refs_1_.6, ...), custom_call_target="tpu_custom_call" | custom-call | tf_op jit(solution)/shard_map/second_kernel/pallas_call | solution.py:628
  67.1 3.9 %all-to-all-done.2.refs_0_ = f32[128,8,128]{2,1,0:T(8,128)S(1)} async-done(((f32[128,8,128]{2,1,0:T(8,128)}), f32[128,8,128]{2,1,0:T(8,128)S(1)}, u32[]{:S(2)}, u32[]{:S(2)}) %all-to-all-start.2) | async-done | bytes 524320 | tf_op jit(solution)/shard_map/all_to_all | solution.py:642
  70.9 2.4 %package_kernel.3 = (f32[16,128]{1,0:T(8,128)}, f32[16,128]{1,0:T(8,128)}, f32[16,128]{1,0:T(8,128)}, f32[96,128]{1,0:T(8,128)}, f32[128,4,128]{2,1,0:T(4,128)}) custom-call(f32[128,8,128]{2,1,0:T(8,128)S(1)} %all-to-all-done.2.refs_0_, f32[32,4096]{1,0:T(8,128)S(1)} %get-tuple-element.44.refs_1_, f32[1,32,32]{2,1,0:T(8,128)} %refs_2_.5, f32[32,128]{1,0:T(8,128)} %bitcast.6, ...), custom_call_target="tpu_custom_call" | custom-call | tf_op jit(solution)/shard_map/package_kernel/pallas_call | solution.py:628
  73.4 5.9 %all-to-all-start.3 = ((f32[128,4,128]{2,1,0:T(4,128)}), f32[128,4,128]{2,1,0:T(4,128)S(1)}, u32[]{:S(2)}, u32[]{:S(2)}) async-start(f32[128,4,128]{2,1,0:T(4,128)} %get-tuple-element.54), calls=%async_computation.3 | async-start | bytes 524288 | tf_op jit(solution)/shard_map/all_to_all | solution.py:642
  79.3 6.4 %third_kernel.1 = (f32[16,128,256]{2,1,0:T(8,128)}, f32[128,128]{1,0:T(8,128)S(1)}) custom-call(f32[16,136,384]{2,1,0:T(8,128)} %get-tuple-element.57.refs_0_, f32[16,128,256]{2,1,0:T(8,128)} %get-tuple-element.58.refs_1_.refs_7_, f32[136,384]{1,0:T(8,128)} %get-tuple-element.59.refs_2_, f32[128,256]{1,0:T(8,128)} %get-tuple-element.60.refs_3_, ...), custom_call_target="tpu_custom_call" | custom-call | tf_op jit(solution)/shard_map/third_kernel/pallas_call | solution.py:628
  85.8 4.0 %all-to-all-done.3.refs_0_ = f32[128,4,128]{2,1,0:T(4,128)S(1)} async-done(((f32[128,4,128]{2,1,0:T(4,128)}), f32[128,4,128]{2,1,0:T(4,128)S(1)}, u32[]{:S(2)}, u32[]{:S(2)}) %all-to-all-start.3) | async-done | bytes 262176 | tf_op jit(solution)/shard_map/all_to_all | solution.py:642
  89.8 0.0 copy-start
  89.8 0.0 copy-start.1
  89.8 0.0 copy-start.2
  89.8 0.0 copy-start.3
  89.8 0.0 copy-start.4
  89.8 2.6 %fourth_kernel.1 = (f32[128,1,128]{2,1,0:T(1,128)S(1)}, f32[16,128,256]{2,1,0:T(8,128)S(1)}, f32[16,128,256]{2,1,0:T(8,128)S(1)}) custom-call(f32[128,4,128]{2,1,0:T(4,128)S(1)} %all-to-all-done.3.refs_0_, f32[32,4096]{1,0:T(8,128)S(1)} %get-tuple-element.44.refs_1_, f32[32,128]{1,0:T(8,128)} %bitcast.7, ...), custom_call_target="tpu_custom_call" | custom-call | tf_op jit(solution)/shard_map/fourth_kernel/pallas_call | solution.py:628
  92.4 15.0 %all_to_all.25.refs_0_ = f32[128,1,128]{2,1,0:T(1,128)S(1)} all-to-all(f32[128,1,128]{2,1,0:T(1,128)S(1)} %get-tuple-element.67), channel_id=1, replica_groups=mesh['row_0'=2,'row_1'=4,'row_2'=2,'col_0'=4,'col_1'=2] {'row_0','row_1'..., dimensions={0} | all-to-all | bytes 131072 | tf_op jit(solution)/shard_map/all_to_all | solution.py:642
  107.4 0.0 copy-done
  107.4 0.0 copy-done.1
  107.4 0.0 copy-done.2
  107.4 0.0 copy-done.3
  107.4 0.0 copy-done.4
  107.5 2.4 %last_kernel.1 = (f32[16,128,256]{2,1,0:T(8,128)}, f32[16,32]{1,0:T(8,128)}) custom-call(f32[128,1,128]{2,1,0:T(1,128)S(1)} %all_to_all.25.refs_0_, f32[16,128,256]{2,1,0:T(8,128)S(1)} %copy-done, f32[136,384]{1,0:T(8,128)S(1)} %copy-done.1, f32[16,128,256]{2,1,0:T(8,128)S(1)} %get-tuple-element.68.refs_3_, f32[16,128,256]{2,1,0:T(8,128)S(1)} %get-tuple-element.69.refs_4_, ...), custom_call_target="tpu_custom_call" | custom-call | tf_op jit(solution)/shard_map/last_kernel/pallas_call | solution.py:628
Async XLA Ops:
  3.5 20.4 %all-to-all-start.1 = ((f32[8,184,128]{2,1,0:T(8,128)}), f32[8,184,128]{2,1,0:T(8,128)S(1)}, u32[]{:S(2)}, u32[]{:S(2)}) async-start(f32[8,184,128]{2,1,0:T(8,128)} %get-tuple-element.37), calls=%async_computation.1 | async-start | bytes 1507328 | tf_op jit(solution)/shard_map/all_to_all | solution.py:642
  23.9 20.7 %all-to-all-start = ((f32[128,8,128]{2,1,0:T(8,128)}), f32[128,8,128]{2,1,0:T(8,128)S(1)}, u32[]{:S(2)}, u32[]{:S(2)}) async-start(f32[128,8,128]{2,1,0:T(8,128)} %get-tuple-element.36), calls=%async_computation | async-start | bytes 1048576 | tf_op jit(solution)/shard_map/all_to_all | solution.py:642
  32.8 8.2 %collective-permute-start = (f32[9,8,384]{2,1,0:T(8,128)S(1)}, f32[9,8,384]{2,1,0:T(8,128)S(1)}, u32[]{:S(2)}, u32[]{:S(2)}) collective-permute-start(f32[9,8,384]{2,1,0:T(8,128)S(1)} %get-tuple-element.40), channel_id=1, source_target_pairs={{8,0},{16,8},{24,16},{32,24},{40,32},{48,40},{56,48},{64,56},{72,6... | collective-permute-start | bytes 331784 | tf_op jit(solution)/shard_map/ppermute | solution.py:676
  35.8 5.7 %collective-permute-start.1 = (f32[9,8,384]{2,1,0:T(8,128)S(1)}, f32[9,8,384]{2,1,0:T(8,128)S(1)}, u32[]{:S(2)}, u32[]{:S(2)}) collective-permute-start(f32[9,8,384]{2,1,0:T(8,128)S(1)} %get-tuple-element.41), channel_id=1, source_target_pairs={{0,8},{8,16},{16,24},{24,32},{32,40},{40,48},{48,56},{56,64},{64,7... | collective-permute-start | bytes 331784 | tf_op jit(solution)/shard_map/ppermute | solution.py:677
  47.1 23.8 %all-to-all-start.2 = ((f32[128,8,128]{2,1,0:T(8,128)}), f32[128,8,128]{2,1,0:T(8,128)S(1)}, u32[]{:S(2)}, u32[]{:S(2)}) async-start(f32[128,8,128]{2,1,0:T(8,128)} %get-tuple-element.47), calls=%async_computation.2 | async-start | bytes 1048576 | tf_op jit(solution)/shard_map/all_to_all | solution.py:642
  73.4 16.4 %all-to-all-start.3 = ((f32[128,4,128]{2,1,0:T(4,128)}), f32[128,4,128]{2,1,0:T(4,128)S(1)}, u32[]{:S(2)}, u32[]{:S(2)}) async-start(f32[128,4,128]{2,1,0:T(4,128)} %get-tuple-element.54), calls=%async_computation.3 | async-start | bytes 524288 | tf_op jit(solution)/shard_map/all_to_all | solution.py:642
  89.8 17.7 %copy-start = (f32[16,128,256]{2,1,0:T(8,128)S(1)}, f32[16,128,256]{2,1,0:T(8,128)}, u32[]{:S(2)}) copy-start(f32[16,128,256]{2,1,0:T(8,128)} %refs_1_.7) | copy-start | bytes 6291460
  89.8 17.7 %copy-start.1 = (f32[136,384]{1,0:T(8,128)S(1)}, f32[136,384]{1,0:T(8,128)}, u32[]{:S(2)}) copy-start(f32[136,384]{1,0:T(8,128)} %get-tuple-element.59.refs_2_) | copy-start | bytes 626692
  89.8 17.7 %copy-start.2 = (f32[16,128]{1,0:T(8,128)S(1)}, f32[16,128]{1,0:T(8,128)}, u32[]{:S(2)}) copy-start(f32[16,128]{1,0:T(8,128)} %get-tuple-element.46.refs_6_.refs_7_.refs_5_) | copy-start | bytes 24580
  89.8 17.7 %copy-start.3 = (f32[16,128]{1,0:T(8,128)S(1)}, f32[16,128]{1,0:T(8,128)}, u32[]{:S(2)}) copy-start(f32[16,128]{1,0:T(8,128)} %get-tuple-element.51.refs_8_.refs_6_) | copy-start | bytes 24580
  89.8 17.7 %copy-start.4 = (f32[16,128]{1,0:T(8,128)S(1)}, f32[16,128]{1,0:T(8,128)}, u32[]{:S(2)}) copy-start(f32[16,128]{1,0:T(8,128)} %get-tuple-element.55.refs_6_.refs_4_.refs_7_) | copy-start | bytes 24580
